TPU v7x, 32 devices: a whole 2x2x4 slice. The times are simulated.
32 devices in a mesh: dp: 8 (over z, x), head: 4 (over y, core).
Axes of the slice: x: 2, y: 2, z: 4, core: 2. Of those that a mesh axis runs over, the one named last changes fastest.
Arguments:
- tokens: bfloat16 [11840, 768], P(('dp', 'head')), may hold values from -6 to 6
- caption_len: int32 [64], P('dp'), may hold values from 5 to 40, as said below
- first_gain: bfloat16 [768], P(('dp', 'head')), may hold values from 0.5 to 1.5
- first_shift: bfloat16 [768], P(('dp', 'head')), may hold values from -3 to 3
- qkv_weight: bfloat16 [768, 3, 768], P('dp', None, 'head'), may hold values from -0.21875 to 0.21875
- qkv_bias: bfloat16 [2, 768], P(None, ('head', 'dp')), may hold values from -3 to 3
- out_weight: bfloat16 [768, 768], P(('dp', 'head')), may hold values from -1.25 to 1.25
- out_bias: bfloat16 [768], P(('dp', 'head')), may hold values from -3 to 3
- second_gain: bfloat16 [768], P(('dp', 'head')), may hold values from 0.5 to 1.5
- second_shift: bfloat16 [768], P(('dp', 'head')), may hold values from -3 to 3
- up_weight: bfloat16 [768, 3072], P('dp', 'head'), may hold values from -0.21875 to 0.21875
- up_bias: bfloat16 [3072], P(('head', 'dp')), may hold values from -3 to 3
- down_weight: bfloat16 [3072, 768], P('head', 'dp'), may hold values from -0.109375 to 0.109375
- down_bias: bfloat16 [768], P(('dp', 'head')), may hold values from -3 to 3
- output_grad: bfloat16 [11840, 768], P(('dp', 'head')), may hold values from -6 to 6
Outputs:
- layer_out: bfloat16 [11840, 768], P(('dp', 'head'))
- tokens_grad: bfloat16 [11840, 768], P(('dp', 'head'))
- first_gain_grad: float32 [768], P(('dp', 'head'))
- first_shift_grad: float32 [768], P(('dp', 'head'))
- qkv_weight_grad: float32 [768, 3, 768], P('dp', None, 'head')
- qkv_bias_grad: float32 [2, 768], P(None, ('head', 'dp'))
- out_weight_grad: float32 [768, 768], P(('dp', 'head'))
- out_bias_grad: float32 [768], P(('dp', 'head'))
- second_gain_grad: float32 [768], P(('dp', 'head'))
- second_shift_grad: float32 [768], P(('dp', 'head'))
- up_weight_grad: float32 [768, 3072], P('dp', 'head')
- up_bias_grad: float32 [3072], P(('head', 'dp'))
- down_weight_grad: float32 [3072, 768], P('head', 'dp')
- down_bias_grad: float32 [768], P(('dp', 'head'))
Inputs may be any that keep to these rules, and one draw needn't show every extreme that they name: Each pair's caption fills its first caption_len slots; some pair's caption fills all 40 slots.
All inputs are finite; a program needn't handle non-finite values.
Results may differ from a plain program's by a relative error of at most 0.014.
Values may be sent and summed in bfloat16 or wider, within the bound.
No kernel may reach another device: no remote copies, remote signals or barrier semaphores. Data moves between devices by JAX's collectives and lax.ppermute only.
A program may use at most 128 MiB of HBM per device.

v0:
```python
from functools import partial

import jax
import jax.numpy as jnp
from jax import lax
from jax.sharding import PartitionSpec as P

HEAD_DIM = 64
TEXT = 40


def norm_rows(values, gain, shift):
    centre = jnp.mean(values, axis=-1, keepdims=True)
    spread = values - centre
    second = jnp.mean(spread * spread, axis=-1, keepdims=True)
    return spread * lax.rsqrt(second + 1e-06) * gain + shift


def contract_rows(former, latter):
    return lax.dot_general(
        former, latter, (((0,), (0,)), ((), ())), preferred_element_type=jnp.float32
    )


def times_transposed(former, latter):
    return lax.dot_general(
        former, latter, (((1,), (1,)), ((), ())), preferred_element_type=jnp.float32
    )


def column_sum(matrix):
    return jnp.sum(matrix.astype(jnp.float32), axis=0)


def local(
    tokens,
    caption_len,
    first_gain,
    first_shift,
    qkv_weight,
    qkv_bias,
    out_weight,
    out_bias,
    second_gain,
    second_shift,
    up_weight,
    up_bias,
    down_weight,
    down_bias,
    output_grad,
):
    width = tokens.shape[1]
    gain_one, shift_one, w_out, b_out, gain_two, shift_two, b_down = (
        lax.all_gather(first_gain, ("dp", "head"), axis=0, tiled=True),
        lax.all_gather(first_shift, ("dp", "head"), axis=0, tiled=True),
        lax.all_gather(out_weight, ("dp", "head"), axis=0, tiled=True),
        lax.all_gather(out_bias, ("dp", "head"), axis=0, tiled=True),
        lax.all_gather(second_gain, ("dp", "head"), axis=0, tiled=True),
        lax.all_gather(second_shift, ("dp", "head"), axis=0, tiled=True),
        lax.all_gather(down_bias, ("dp", "head"), axis=0, tiled=True),
    )
    w_qkv, b_qkv, w_up, b_up, w_down = (
        lax.all_gather(qkv_weight, "dp", axis=0, tiled=True),
        lax.all_gather(qkv_bias, "dp", axis=1, tiled=True),
        lax.all_gather(up_weight, "dp", axis=0, tiled=True),
        lax.all_gather(up_bias, "dp", axis=0, tiled=True),
        lax.all_gather(down_weight, "dp", axis=1, tiled=True),
    )
    local_width = w_qkv.shape[2]
    heads_local = local_width // HEAD_DIM
    flat_qkv = w_qkv.reshape(width, 3 * local_width)
    tok_rows = tokens.astype(jnp.float32)
    normed, first_pull = jax.vjp(
        norm_rows, tok_rows, gain_one.astype(jnp.float32), shift_one.astype(jnp.float32)
    )
    normed_low = normed.astype(jnp.bfloat16)
    whole = lax.all_gather(normed_low, "head", axis=0, tiled=True)
    group_rows = whole.shape[0]
    item_count = caption_len.shape[0]
    seq_length = group_rows // item_count
    projected = jnp.dot(whole, flat_qkv, preferred_element_type=jnp.float32).reshape(
        group_rows, 3, local_width
    )
    bias_rows = jnp.stack([b_qkv[0], jnp.zeros_like(b_qkv[0]), b_qkv[1]]).astype(jnp.float32)
    packed = (
        (projected + bias_rows)
        .astype(jnp.bfloat16)
        .reshape(item_count, seq_length, 3, heads_local, HEAD_DIM)
    )
    queries = packed[:, :, 0]
    key_rows = packed[:, :, 1]
    value_rows = packed[:, :, 2]
    score_scale = HEAD_DIM ** (-0.5)
    position = jnp.arange(seq_length, dtype=jnp.int32)
    visible = ((position[None, :] >= TEXT) | (position[None, :] < caption_len[:, None]))[
        :, None, None, :
    ]

    def masked_scores():
        product = (
            jnp.einsum("ishd,ithd->ihst", queries, key_rows, preferred_element_type=jnp.float32)
            * score_scale
        )
        return jnp.where(visible, product, -1000000000.0)

    scores = masked_scores()
    highest_score = jnp.max(scores, axis=-1, keepdims=True)
    unnormed = jnp.exp(scores - highest_score)
    row_totals = jnp.sum(unnormed, axis=-1, keepdims=True)
    attn_probs = unnormed / row_totals
    log_total = highest_score + jnp.log(row_totals)
    probs_low = attn_probs.astype(jnp.bfloat16)
    context = jnp.einsum(
        "ihst,ithd->ishd", probs_low, value_rows, preferred_element_type=jnp.float32
    )
    context_low = context.astype(jnp.bfloat16).reshape(group_rows, local_width)
    ctx_rows = lax.all_to_all(context_low, "head", split_axis=0, concat_axis=1, tiled=True)
    middle = tok_rows + (
        jnp.dot(ctx_rows, w_out, preferred_element_type=jnp.float32) + b_out.astype(jnp.float32)
    )
    hidden_in, second_pull = jax.vjp(
        norm_rows, middle, gain_two.astype(jnp.float32), shift_two.astype(jnp.float32)
    )
    hidden_low = hidden_in.astype(jnp.bfloat16)
    hidden_group = lax.all_gather(hidden_low, "head", axis=0, tiled=True)
    up_proj = jnp.dot(hidden_group, w_up, preferred_element_type=jnp.float32) + b_up.astype(
        jnp.float32
    )
    active, gelu_pull = jax.vjp(partial(jax.nn.gelu, approximate=False), up_proj)
    active_low = active.astype(jnp.bfloat16)
    branch_part = jnp.dot(active_low, w_down, preferred_element_type=jnp.float32)
    branch = lax.psum_scatter(
        branch_part.astype(jnp.bfloat16), "head", scatter_dimension=0, tiled=True
    ).astype(jnp.float32)
    layer_out = (middle + (branch + b_down.astype(jnp.float32))).astype(jnp.bfloat16)
    w_out = lax.all_gather(out_weight, ("dp", "head"), axis=0, tiled=True)
    w_qkv, w_up, w_down = (
        lax.all_gather(qkv_weight, "dp", axis=0, tiled=True),
        lax.all_gather(up_weight, "dp", axis=0, tiled=True),
        lax.all_gather(down_weight, "dp", axis=1, tiled=True),
    )
    flat_qkv = w_qkv.reshape(width, 3 * local_width)
    grad_top = output_grad.astype(jnp.float32)
    grad_low = grad_top.astype(jnp.bfloat16)
    down_bias_part = column_sum(grad_low)
    grad_group = lax.all_gather(grad_low, "head", axis=0, tiled=True)
    down_weight_part = contract_rows(active_low, grad_group)
    (grad_up,) = gelu_pull(times_transposed(grad_group, w_down))
    up_low = grad_up.astype(jnp.bfloat16)
    up_bias_part = column_sum(up_low)
    up_weight_part = contract_rows(hidden_group, up_low)
    grad_hidden = lax.psum_scatter(
        times_transposed(up_low, w_up).astype(jnp.bfloat16), "head", scatter_dimension=0, tiled=True
    ).astype(jnp.float32)
    grad_middle_part, gain_two_part, shift_two_part = second_pull(grad_hidden)
    grad_middle = grad_top + grad_middle_part
    middle_low = grad_middle.astype(jnp.bfloat16)
    out_bias_part = column_sum(middle_low)
    out_weight_part = contract_rows(ctx_rows, middle_low)
    grad_ctx = times_transposed(middle_low, w_out).astype(jnp.bfloat16)
    grad_context = lax.all_to_all(
        grad_ctx, "head", split_axis=1, concat_axis=0, tiled=True
    ).reshape(item_count, seq_length, heads_local, HEAD_DIM)
    scores = masked_scores()
    attn_probs = jnp.exp(scores - log_total)
    probs_low = attn_probs.astype(jnp.bfloat16)
    grad_probs = jnp.einsum(
        "ishd,ithd->ihst", grad_context, value_rows, preferred_element_type=jnp.float32
    )
    value_grad = jnp.einsum(
        "ihst,ishd->ithd", probs_low, grad_context, preferred_element_type=jnp.float32
    ).astype(jnp.bfloat16)
    grad_scores = attn_probs * (
        grad_probs - jnp.sum(attn_probs * grad_probs, axis=-1, keepdims=True)
    )
    scores_low = grad_scores.astype(jnp.bfloat16)
    query_grad = (
        jnp.einsum("ihst,ithd->ishd", scores_low, key_rows, preferred_element_type=jnp.float32)
        * score_scale
    ).astype(jnp.bfloat16)
    key_grad = (
        jnp.einsum("ihst,ishd->ithd", scores_low, queries, preferred_element_type=jnp.float32)
        * score_scale
    ).astype(jnp.bfloat16)
    grad_packed = jnp.stack([query_grad, key_grad, value_grad], axis=2).reshape(
        group_rows, 3 * local_width
    )
    qkv_weight_part = contract_rows(whole, grad_packed).reshape(width, 3, local_width)
    qkv_bias_part = jnp.stack(
        [column_sum(grad_packed[:, :local_width]), column_sum(grad_packed[:, 2 * local_width :])]
    )
    own_grads = lax.all_to_all(
        grad_packed.reshape(group_rows, 3, local_width),
        "head",
        split_axis=0,
        concat_axis=2,
        tiled=True,
    )
    all_columns = lax.all_gather(w_qkv, "head", axis=2, tiled=True)
    grad_normed = times_transposed(
        own_grads.reshape(own_grads.shape[0], 3 * width), all_columns.reshape(width, 3 * width)
    )
    grad_rows_part, gain_one_part, shift_one_part = first_pull(grad_normed)
    tokens_grad = (grad_middle + grad_rows_part).astype(jnp.bfloat16)
    layer_sums = (
        lax.psum_scatter(gain_one_part, ("dp", "head"), scatter_dimension=0, tiled=True),
        lax.psum_scatter(shift_one_part, ("dp", "head"), scatter_dimension=0, tiled=True),
        lax.psum_scatter(out_weight_part, ("dp", "head"), scatter_dimension=0, tiled=True),
        lax.psum_scatter(out_bias_part, ("dp", "head"), scatter_dimension=0, tiled=True),
        lax.psum_scatter(gain_two_part, ("dp", "head"), scatter_dimension=0, tiled=True),
        lax.psum_scatter(shift_two_part, ("dp", "head"), scatter_dimension=0, tiled=True),
        lax.psum_scatter(down_bias_part, ("dp", "head"), scatter_dimension=0, tiled=True),
    )
    head_sums = (
        lax.psum_scatter(qkv_weight_part, "dp", scatter_dimension=0, tiled=True),
        lax.psum_scatter(qkv_bias_part, "dp", scatter_dimension=1, tiled=True),
        lax.psum_scatter(up_weight_part, "dp", scatter_dimension=0, tiled=True),
        lax.psum_scatter(up_bias_part, "dp", scatter_dimension=0, tiled=True),
        lax.psum_scatter(down_weight_part, "dp", scatter_dimension=1, tiled=True),
    )
    return (
        layer_out,
        tokens_grad,
        layer_sums[0],
        layer_sums[1],
        head_sums[0],
        head_sums[1],
        layer_sums[2],
        layer_sums[3],
        layer_sums[4],
        layer_sums[5],
        head_sums[2],
        head_sums[3],
        head_sums[4],
        layer_sums[6],
    )


def solution(mesh):
    return jax.shard_map(
        local,
        mesh=mesh,
        in_specs=(
            P(("dp", "head"), None),
            P("dp"),
            P(("dp", "head")),
            P(("dp", "head")),
            P("dp", None, "head"),
            P(None, ("head", "dp")),
            P(("dp", "head"), None),
            P(("dp", "head")),
            P(("dp", "head")),
            P(("dp", "head")),
            P("dp", "head"),
            P(("head", "dp")),
            P("head", "dp"),
            P(("dp", "head")),
            P(("dp", "head"), None),
        ),
        out_specs=(
            P(("dp", "head"), None),
            P(("dp", "head"), None),
            P(("dp", "head")),
            P(("dp", "head")),
            P("dp", None, "head"),
            P(None, ("head", "dp")),
            P(("dp", "head"), None),
            P(("dp", "head")),
            P(("dp", "head")),
            P(("dp", "head")),
            P("dp", "head"),
            P(("head", "dp")),
            P("head", "dp"),
            P(("dp", "head")),
        ),
        check_vma=False,
    )
```

profile of v0, /device:TPU:0, one launch (start us, length us, event | category | flops | bytes accessed | tf_op | source)
XLA Modules:
  0.0 709.9 jit_solution(16283716665516034311)
XLA Ops:
  12.3 42.2 %all-reduce.21 = (bf16[768]{0:T(1024)(128)(2,1)S(1)}, bf16[768]{0:T(1024)(128)(2,1)S(1)}, bf16[768]{0:T(1024)(128)(2,1)S(1)}, bf16[768]{0:T(1024)(128)(2,1)S(1)}...) all-reduce(bf16[768]{0:T(1024)(128)(2,1)S(1)} %dynamic-update-slice, ...), channel_id=1, replica_groups=mesh['dp'=8,'head'=4] {'dp','head'}, use_global_device_ids=true, to_apply=%add.1 | all-reduce | flops 4608 | bytes 18432
  54.4 1.2 convert_reduce_fusion.2
  55.7 1.4 fusion.31
  57.0 2.2 fusion.40
  60.7 20.2 %all-gather.1 = bf16[8,24,2]{1,2,0:T(2,128)(2,1)S(1)} all-gather(bf16[1,24,2]{1,2,0:T(2,128)(2,1)S(1)} %bitcast.140), channel_id=1, replica_groups=mesh['dp'=8,'head'=4] {'dp'}, dimensions={0}, use_global_device_ids=true | all-gather | bytes 864 | tf_op jit(solution)/shard_map/all_gather | solution.py:64
  81.2 36.1 %all_gather.55 = bf16[768,3,192]{2,1,0:T(4,128)(2,1)S(1)} all-gather(bf16[96,3,192]{2,1,0:T(4,128)(2,1)S(1)} %copy.56), channel_id=1, replica_groups=mesh['dp'=8,'head'=4] {'dp'}, dimensions={0}, use_global_device_ids=true | all-gather | bytes 995328 | tf_op jit(solution)/shard_map/all_gather | solution.py:63
  118.4 2.3 reshape.228
  120.8 1.4 copy-done.21
  122.2 2.8 add_convert_fusion.1
  125.0 5.0 reshape.198
  130.2 1.7 fusion.53
  132.8 1.3 copy-done
  137.1 3.5 all-to-all-start
  141.2 8.8 %all-to-all-done = bf16[4,370,192]{1,2,0:T(8,128)(2,1)S(1)} async-done(((bf16[4,370,192]{1,2,0:T(8,128)(2,1)}), bf16[4,370,192]{1,2,0:T(8,128)(2,1)S(1)}, u32[]{:S(2)}, u32[]{:S(2)}) %all-to-all-start) | async-done | bytes 568352 | tf_op jit(solution)/shard_map/all_to_all | solution.py:117
  150.1 2.2 fusion.54
  157.2 20.8 %all-reduce.5 = bf16[768]{0:T(1024)(128)(2,1)S(1)} all-reduce(bf16[768]{0:T(1024)(128)(2,1)S(1)} %dynamic-update-slice.5), channel_id=1, replica_groups=mesh['dp'=8,'head'=4] {'dp'}, use_global_device_ids=true, to_apply=%add.5 | all-reduce | flops 768 | bytes 3072
  177.9 3.6 reshape.225
  181.6 9.8 %all-gather.22.cloned.1.call-done = bf16[4,370,768]{2,1,0:T(8,128)(2,1)} async-done(((bf16[1,370,768]{2,1,0:T(8,128)(2,1)}), bf16[4,370,768]{2,1,0:T(8,128)(2,1)}) %all-gather.22.cloned.1.call-update) | async-done | bytes 2273296 | tf_op jit(solution)/shard_map/all_gather | solution.py:125
  191.3 3.7 reshape.223
  195.0 39.5 %all-gather.14.cloned.1.call-done = bf16[768,768]{1,0:T(8,128)(2,1)} async-done(((bf16[96,768]{1,0:T(8,128)(2,1)}), bf16[768,768]{1,0:T(8,128)(2,1)}) %all-gather.14.cloned.1.call-update) | async-done | bytes 1179664 | tf_op jit(solution)/shard_map/all_gather | solution.py:65
  234.5 6.1 fusion.55
  240.6 35.8 %all-gather.16.cloned.1.call-done = bf16[768,768]{0,1:T(8,128)(2,1)} async-done(((bf16[768,96]{0,1:T(8,128)(2,1)}), bf16[768,768]{0,1:T(8,128)(2,1)}) %all-gather.16.cloned.1.call-update) | async-done | bytes 1179664 | tf_op jit(solution)/shard_map/all_gather | solution.py:67
  276.4 14.9 %convert_reduce_fusion = (f32[768]{0:T(1024)}, bf16[1480,768]{1,0:T(8,128)(2,1)S(1)}, f32[1480,768]{1,0:T(8,128)S(1)}) fusion(f32[1480,768]{1,0:T(8,128)} %fusion.55, f32[768]{0:T(1024)S(1)} %convert_element_type.133, bf16[1480,768]{1,0:T(8,128)(2,1)} %reshape.225, bf16[768,768]{0,1:T(8,128)(2,1)} %all-gather.16.cloned.1.call-done), kind=kOutput, calls=%fused_computation.8 | convolution fusion | flops 1831126272 | bytes 14825472 | tf_op jit(solution)/shard_map/dot_general | solution.py:26
  292.2 1.2 copy-done.35
  293.4 3.4 convolution_convert_fusion.1
  296.8 3.5 convolution_convert_fusion
  300.3 54.1 %fusion.46 = (bf16[376,768]{1,0:T(8,128)(2,1)S(1)}, bf16[376,768]{1,0:T(8,128)(2,1)S(1)}) fusion(bf16[1480,768]{1,0:T(8,128)(2,1)} %convolution_convert_fusion.1, bf16[1480,768]{1,0:T(8,128)(2,1)} %convolution_convert_fusion), kind=kCustom, calls=%all-reduce-scatter.2 | all-reduce-scatter fusion | flops 2310145 | bytes 5702144
  354.4 1.3 collective-permute-start
  355.7 3.2 collective-permute-start.1
  360.8 4.2 concatenate.5
  365.1 1.3 concatenate.6
  366.4 1.1 fusion.33
  368.3 3.0 fusion.49
  374.0 3.5 all-to-all-start.1
  377.6 3.5 fusion.57
  381.1 5.9 all-to-all-done.1
  387.0 1.3 copy.66
  388.3 2.5 reshape.199
  390.8 4.4 multiply_reduce_fusion
  395.2 1.1 multiply_convert_fusion
  400.7 2.9 copy.78
  403.6 4.9 reshape.202
  408.5 5.7 fusion.56
  414.5 5.9 fusion.58
  420.4 5.9 fusion.59
  427.5 1.3 copy.69
  428.8 2.7 stack.33
  431.5 2.5 copy.71
  434.0 2.6 stack.34
  436.7 1.4 copy.74
  438.0 2.0 stack.35
  440.0 2.7 pad_maximum_fusion.1
  442.7 5.5 copy.75
  448.2 4.8 all-to-all-start.2
  454.3 1.5 convert_reduce_fusion.5
  455.8 19.6 %all-reduce.20 = (f32[2,192]{1,0:T(2,128)S(1)}, f32[768]{0:T(1024)S(1)}) all-reduce(f32[2,192]{1,0:T(2,128)S(1)} %pad_maximum_fusion.2, f32[768]{0:T(1024)S(1)} %copy-done.28), channel_id=7, replica_groups=mesh['dp'=8,'head'=4] {'dp'}, use_global_device_ids=true, to_apply=%region_20.21.clone | all-reduce | flops 1152 | bytes 9216
  476.6 12.6 %all-to-all-done.2 = bf16[1480,3,192]{2,1,0:T(4,128)(2,1)} async-done(((bf16[1480,3,192]{2,1,0:T(4,128)(2,1)}), bf16[1480,3,192]{2,1,0:T(4,128)(2,1)}, u32[]{:S(2)}, u32[]{:S(2)}) %all-to-all-start.2) | async-done | bytes 1704992 | tf_op jit(solution)/shard_map/all_to_all | solution.py:192
  489.2 5.5 copy.76
  494.7 4.3 fusion.45
  499.7 1.4 convert_reduce_fusion.3
  501.1 39.7 %all-reduce.19 = (f32[768]{0:T(1024)S(1)}, f32[768]{0:T(1024)S(1)}, f32[768]{0:T(1024)S(1)}, f32[768]{0:T(1024)S(1)}, f32[768]{0:T(1024)S(1)}, /*index=5*/f32[768]{0:T(1024)S(1)}) all-reduce(f32[768]{0:T(1024)S(1)} %get-tuple-element.18, f32[768]{0:T(1024)S(1)} %get-tuple-element.20, ...), channel_id=4, replica_groups=mesh['dp'=8,'head'=4] {'dp','head'}, use_global_device_ids=true, to_apply=%region_14.15.clone | all-reduce | flops 4608 | bytes 36864
  544.3 12.9 %reduce-scatter.10.cloned.1.call-done = f32[96,3,192]{2,0,1:T(8,128)} async-done(((f32[768,3,192]{2,0,1:T(8,128)}), f32[96,3,192]{2,0,1:T(8,128)}) %reduce-scatter.10.cloned.1.call-update) | async-done | bytes 221200 | tf_op jit(solution)/shard_map/reduce_scatter | solution.py:215
  557.2 72.8 %reduce-scatter.14.cloned.1.call-done = f32[96,768]{1,0:T(8,128)} async-done(((f32[768,768]{1,0:T(8,128)}), f32[96,768]{1,0:T(8,128)}) %reduce-scatter.14.cloned.1.call-update) | async-done | bytes 294928 | tf_op jit(solution)/shard_map/reduce_scatter | solution.py:217
  630.0 73.0 %reduce-scatter.16.cloned.1.call-done = f32[768,96]{0,1:T(8,128)} async-done(((f32[768,768]{0,1:T(8,128)}), f32[768,96]{0,1:T(8,128)}) %reduce-scatter.16.cloned.1.call-update) | async-done | bytes 294928 | tf_op jit(solution)/shard_map/reduce_scatter | solution.py:219
  (174 shorter events, 33.6 us)
Async XLA Ops:
  7.2 53.5 %copy-start.30 = (bf16[2,24]{1,0:T(2,128)(2,1)S(1)}, bf16[2,24]{1,0:T(2,128)(2,1)}, u32[]{:S(2)}) copy-start(bf16[2,24]{1,0:T(2,128)(2,1)} %param.20) | copy-start | bytes 292
  7.2 73.8 %copy-start.22 = (bf16[96,3,192]{2,0,1:T(8,128)(2,1)S(1)}, bf16[96,3,192]{2,0,1:T(8,128)(2,1)}, u32[]{:S(2)}) copy-start(bf16[96,3,192]{2,0,1:T(8,128)(2,1)} %param.19) | copy-start | bytes 331780
  7.2 111.2 %all-gather.20.cloned.1.call-start = ((), (), s32[]{:S(2)}) async-start(), calls=%async_computation.15 | async-start | bytes 2887680 | tf_op jit(solution)/shard_map/all_gather | solution.py:77
  57.0 61.1 %copy-start.23 = (f32[370]{0:T(512)}, f32[370]{0:T(512)S(1)}, u32[]{:S(2)}) copy-start(f32[370]{0:T(512)S(1)} %fusion.31) | copy-start | bytes 4444
  59.2 82.0 %all-gather.12.cloned.1.call-start = ((), (), s32[]{:S(2)}) async-start(), calls=%async_computation.7 | async-start | bytes 1216512 | tf_op jit(solution)/shard_map/all_gather | solution.py:56
  60.0 118.0 %all-gather.24.cloned.1.call-start = ((), (), s32[]{:S(2)}) async-start(), calls=%async_computation.17 | async-start | bytes 2887680 | tf_op jit(solution)/shard_map/all_gather | solution.py:146
  81.0 37.3 %copy-start.32 = (s32[8]{0:T(128)S(1)}, s32[8]{0:T(128)}, u32[]{:S(2)}) copy-start(s32[8]{0:T(128)} %param.16) | copy-start | bytes 100
  118.2 2.6 copy-start.11
  120.8 1.4 copy-start.21
  130.2 1.7 copy-start.12
  130.2 1.7 copy-start.14
  130.2 2.5 copy-start.16
  131.9 2.1 copy-start
  135.5 14.6 %copy-start.1 = (bf16[370,768]{1,0:T(8,128)(2,1)S(1)}, bf16[370,768]{1,0:T(8,128)(2,1)}, u32[]{:S(2)}) copy-start(bf16[370,768]{1,0:T(8,128)(2,1)} %param.15) | copy-start | bytes 1704964
  137.1 13.0 %all-to-all-start = ((bf16[4,370,192]{1,2,0:T(8,128)(2,1)}), bf16[4,370,192]{1,2,0:T(8,128)(2,1)S(1)}, u32[]{:S(2)}, u32[]{:S(2)}) async-start(bf16[4,370,192]{1,2,0:T(8,128)(2,1)} %copy.64), calls=%async_computation | async-start | bytes 1179648 | tf_op jit(solution)/shard_map/all_to_all | solution.py:117
  140.6 50.7 %all-gather.22.cloned.1.call-start = ((), (), s32[]{:S(2)}) async-start(), calls=%async_computation.16 | async-start | bytes 2887680 | tf_op jit(solution)/shard_map/all_gather | solution.py:125
  150.1 2.5 copy-start.17
  152.3 3.3 copy-start.29
  152.3 4.6 copy-start.36
  152.6 28.9 %copy-start.25 = (f32[370]{0:T(512)}, f32[370]{0:T(512)S(1)}, u32[]{:S(2)}) copy-start(f32[370]{0:T(512)S(1)} %multiply_reduce_fusion.1) | copy-start | bytes 4444
  153.7 80.8 %all-gather.14.cloned.1.call-start = ((), (), s32[]{:S(2)}) async-start(), calls=%async_computation.8 | async-start | bytes 1327104 | tf_op jit(solution)/shard_map/all_gather | solution.py:65
  154.3 122.1 %all-gather.16.cloned.1.call-start = ((), (), s32[]{:S(2)}) async-start(), calls=%async_computation.9 | async-start | bytes 1327104 | tf_op jit(solution)/shard_map/all_gather | solution.py:67
  154.9 339.8 %all-gather.18.cloned.1.call-start = ((), (), s32[]{:S(2)}) async-start(), calls=%async_computation.10 | async-start | bytes 4423680 | tf_op jit(solution)/shard_map/all_gather | solution.py:199
  276.4 14.9 %copy-start.10 = (f32[1480,768]{1,0:T(8,128)S(1)}, f32[1480,768]{1,0:T(8,128)}, u32[]{:S(2)}) copy-start(f32[1480,768]{1,0:T(8,128)} %fusion.55) | copy-start | bytes 13639684
  291.3 5.5 copy-start.20
  291.3 2.1 copy-start.35
  293.4 3.4 copy-start.19
  293.4 3.4 copy-start.34
  300.3 58.7 %copy-start.31 = (u32[32]{0:T(128)S(1)}, u32[32]{0:T(128)}, u32[]{:S(2)}) copy-start(u32[32]{0:T(128)} %constant.130) | copy-start | bytes 388
  354.4 6.4 collective-permute-start
  355.7 9.3 %collective-permute-start.1 = (bf16[18,768]{1,0:T(8,128)(2,1)S(1)}, bf16[18,768]{1,0:T(8,128)(2,1)S(1)}, u32[]{:S(2)}, u32[]{:S(2)}) collective-permute-start(bf16[18,768]{1,0:T(8,128)(2,1)S(1)} %slice.36), channel_id=1, source_target_pairs={{0,1},{1,2},{2,3},{4,5},{5,6},{6,7},{8,9},{9,10},{10,11},{12,13},{... | collective-permute-start | bytes 82952
  366.4 1.1 copy-start.9
  367.5 3.7 copy-start.8
  368.3 4.0 copy-start.33
  371.5 0.8 copy-start.18
  374.0 13.0 %all-to-all-start.1 = ((bf16[370,4,192]{0,2,1:T(8,128)(2,1)}), bf16[370,4,192]{0,2,1:T(8,128)(2,1)S(1)}, u32[]{:S(2)}, u32[]{:S(2)}) async-start(bf16[370,4,192]{0,2,1:T(8,128)(2,1)} %bitcast.133), calls=%async_computation.1 | async-start | bytes 1179648 | tf_op jit(solution)/shard_map/all_to_all | solution.py:161
  377.5 166.8 %reduce-scatter.12.cloned.1.call-start = ((), (), s32[]{:S(2)}) async-start(), calls=%async_computation.12 | async-start | bytes 2433024 | tf_op jit(solution)/shard_map/reduce_scatter | solution.py:208
  381.0 176.2 %reduce-scatter.10.cloned.1.call-start = ((), (), s32[]{:S(2)}) async-start(), calls=%async_computation.11 | async-start | bytes 2654208 | tf_op jit(solution)/shard_map/reduce_scatter | solution.py:215
  388.3 6.9 slice-start
  390.8 4.4 slice-start.1
  395.2 1.2 copy-start.15
  396.4 1.1 copy-start.13
  397.6 2.3 copy-start.5
  397.6 1.4 copy-start.7
  399.0 0.9 copy-start.4
  399.9 0.9 copy-start.2
  414.2 215.8 %reduce-scatter.14.cloned.1.call-start = ((), (), s32[]{:S(2)}) async-start(), calls=%async_computation.13 | async-start | bytes 2654208 | tf_op jit(solution)/shard_map/reduce_scatter | solution.py:217
  420.4 282.6 %reduce-scatter.16.cloned.1.call-start = ((), (), s32[]{:S(2)}) async-start(), calls=%async_computation.14 | async-start | bytes 2654208 | tf_op jit(solution)/shard_map/reduce_scatter | solution.py:219
  426.4 1.1 copy-start.6
  428.8 7.8 %copy-start.3 = (bf16[8,3,64,185]{3,2,1,0:T(8,128)(2,1)S(1)}, bf16[8,3,64,185]{3,2,1,0:T(8,128)(2,1)}, u32[]{:S(2)}) copy-start(bf16[8,3,64,185]{3,2,1,0:T(8,128)(2,1)} %copy-done.2) | copy-start | bytes 1704964
  448.2 7.6 %copy-start.28 = (f32[768]{0:T(1024)S(1)}, f32[768]{0:T(1024)}, u32[]{:S(2)}) copy-start(f32[768]{0:T(1024)} %get-tuple-element.41) | copy-start | bytes 9220
  448.2 41.0 %all-to-all-start.2 = ((bf16[1480,3,192]{2,1,0:T(4,128)(2,1)}), bf16[1480,3,192]{2,1,0:T(4,128)(2,1)}, u32[]{:S(2)}, u32[]{:S(2)}) async-start(bf16[1480,3,192]{2,1,0:T(4,128)(2,1)} %copy.75), calls=%async_computation.2 | async-start | bytes 6062080 | tf_op jit(solution)/shard_map/all_to_all | solution.py:192
  494.7 4.3 copy-start.24
  499.6 1.4 copy-start.26
  499.6 1.4 copy-start.27
Sparse Core Ops, SparseCore 0:
  59.3 23.5 all-gather.19
  85.9 55.2 all-gather.11
  142.8 22.6 all-gather.23
  167.5 23.7 all-gather.21
  193.3 41.1 all-gather.13
  236.5 39.8 all-gather.15
  277.9 29.4 all-gather.17
  384.2 100.1 reduce-scatter.11
  488.5 68.6 reduce-scatter.9
  561.1 68.8 reduce-scatter.13
  634.1 68.8 reduce-scatter.15
where the time goes:
time: 720 us; the launch traced here: 710 us
  waiting for transfers between devices  275 us (38%)
  blocking collectives  233 us (32%)
  local copies, waits for them, and re-layouts  78.2 us (11%)
  matrix products  68.1 us (9%)
  other arithmetic  21.6 us (3%)
  between operations  17.6 us (2%)
  starting transfers between devices  17.2 us (2%)
    unnamed x5, blocking collectives  176 us
    reduce_scatter x1, waiting for transfers between devices, local(): lax.psum_scatter(down_weight_part, 'dp', scatter_dimension=1, tiled=True)  73 us
    reduce_scatter x1, waiting for transfers between devices, local(): lax.psum_scatter(up_weight_part, 'dp', scatter_dimension=0, tiled=True)  72.8 us
    all_gather x1, waiting for transfers between devices, local(): lax.all_gather(up_weight, 'dp', axis=0, tiled=True)  39.5 us
    all_gather x1, blocking collectives, local(): lax.all_gather(qkv_weight, 'dp', axis=0, tiled=True)  36.1 us
    all_gather x1, waiting for transfers between devices, local(): lax.all_gather(down_weight, 'dp', axis=1, tiled=True)  35.8 us
    unnamed x111, local copies, waits for them, and re-layouts  34 us
    dot_general x4, matrix products, times_transposed(): lax.dot_general(former, latter, (((1,), (1,)), ((), ())), preferred_eleme...  23.3 us
  transfers between devices with their start and end apart: 16, of which 10 were waited for; matrix products, arithmetic and copies ran while one was open for 29% of the time, Pallas kernels for 0%

commit v1 on v0

v1 whole, which is shorter than its diff:
```python
import jax
import jax.numpy as jnp
from jax import lax
from jax.sharding import PartitionSpec as P

HEAD_DIM = 64
TEXT = 40
ALL = ("dp", "head")
F32 = jnp.float32
BF16 = jnp.bfloat16


def mm(a, b):
    return jnp.dot(a, b, preferred_element_type=F32)


def mm_t(a, b):
    return lax.dot_general(a, b, (((1,), (1,)), ((), ())), preferred_element_type=F32)


def t_mm(a, b):
    return lax.dot_general(a, b, (((0,), (0,)), ((), ())), preferred_element_type=F32)


def norm_parts(values):
    spread = values - jnp.mean(values, axis=-1, keepdims=True)
    root = lax.rsqrt(jnp.mean(spread * spread, axis=-1, keepdims=True) + 1e-06)
    return spread * root, root


def norm_back(grad, gain, hat, root):
    scaled = grad * gain
    first = jnp.mean(scaled, axis=-1, keepdims=True)
    second = jnp.mean(scaled * hat, axis=-1, keepdims=True)
    return root * (scaled - first - hat * second)


def local(
    n_dp,
    n_head,
    tokens,
    caption_len,
    first_gain,
    first_shift,
    qkv_weight,
    qkv_bias,
    out_weight,
    out_bias,
    second_gain,
    second_shift,
    up_weight,
    up_bias,
    down_weight,
    down_bias,
    output_grad,
):
    rows, width = tokens.shape
    hidden = up_weight.shape[1] * n_head
    devices = n_dp * n_head
    item_count = caption_len.shape[0] // n_head
    seq = rows // item_count
    heads = width // HEAD_DIM

    def gather(piece):
        return lax.all_gather(piece, ALL, axis=0)

    per = first_gain.shape[0]
    smalls = gather(
        jnp.concatenate(
            [
                first_gain,
                first_shift,
                out_bias,
                second_gain,
                second_shift,
                down_bias,
                qkv_bias.reshape(-1),
                up_bias,
            ]
        )
    ).astype(F32)

    def plain(index):
        return smalls[:, index * per : (index + 1) * per].reshape(width)

    def by_head(piece):
        return piece.reshape(n_dp, n_head, -1).transpose(1, 0, 2).reshape(-1)

    gain_one, shift_one, b_out, gain_two, shift_two, b_down = (plain(i) for i in range(6))
    b_query = by_head(smalls[:, 6 * per : 7 * per])
    b_value = by_head(smalls[:, 7 * per : 8 * per])
    b_up = by_head(smalls[:, 8 * per :])

    w_qkv = gather(qkv_weight)
    w_out = gather(out_weight).reshape(width, width)
    w_up = gather(up_weight)
    w_down_t = gather(down_weight.T)
    w_qkv = (
        w_qkv.reshape(n_dp, n_head, width // n_dp, 3, width // n_head)
        .transpose(0, 2, 3, 1, 4)
        .reshape(width, 3 * width)
    )

    def square(tiles):
        return (
            tiles.reshape(n_dp, n_head, width // n_dp, hidden // n_head)
            .transpose(0, 2, 1, 3)
            .reshape(width, hidden)
        )

    w_up = square(w_up)
    w_down_t = square(w_down_t)

    x = tokens.astype(F32)
    hat_one, root_one = norm_parts(x)
    normed = (hat_one * gain_one + shift_one).astype(BF16)
    bias = jnp.concatenate([b_query, jnp.zeros_like(b_query), b_value])
    packed = (mm(normed, w_qkv) + bias).astype(BF16).reshape(item_count, seq, 3, heads, HEAD_DIM)
    query, key, value = packed[:, :, 0], packed[:, :, 1], packed[:, :, 2]
    mine = lax.axis_index("head") * item_count
    lengths = lax.dynamic_slice_in_dim(caption_len, mine, item_count)
    position = jnp.arange(seq, dtype=jnp.int32)
    visible = (position[None, :] >= TEXT) | (position[None, :] < lengths[:, None])
    scale = HEAD_DIM**-0.5
    scores = jnp.einsum("ishd,ithd->ihst", query, key, preferred_element_type=F32) * scale
    scores = jnp.where(visible[:, None, None, :], scores, -1000000000.0)
    probs = jax.nn.softmax(scores, axis=-1)
    probs_low = probs.astype(BF16)
    context = (
        jnp.einsum("ihst,ithd->ishd", probs_low, value, preferred_element_type=F32)
        .astype(BF16)
        .reshape(rows, width)
    )
    middle = x + (mm(context, w_out) + b_out)
    hat_two, root_two = norm_parts(middle)
    hidden_in = (hat_two * gain_two + shift_two).astype(BF16)
    up = mm(hidden_in, w_up) + b_up
    phi = 0.5 * (1.0 + lax.erf(up * (0.5**0.5)))
    active = (up * phi).astype(BF16)
    slope = phi + up * jnp.exp(-0.5 * up * up) * ((2.0 * jnp.pi) ** -0.5)
    layer_out = (middle + (mm_t(active, w_down_t) + b_down)).astype(BF16)

    grad_low = output_grad
    grad_top = output_grad.astype(F32)

    def tiles_of(matrix):
        return (
            matrix.reshape(n_dp, width // n_dp, n_head, -1)
            .transpose(0, 2, 1, 3)
            .reshape(devices, width // n_dp, -1)
        )

    def scatter(tiles):
        return lax.psum_scatter(tiles.astype(BF16), ALL, scatter_dimension=0, tiled=True)[0].astype(
            F32
        )

    g_down_t = scatter(tiles_of(t_mm(grad_low, active)))
    grad_up = (mm(grad_low, w_down_t) * slope).astype(BF16)
    g_up = scatter(tiles_of(t_mm(hidden_in, grad_up)))
    grad_hidden = mm_t(grad_up, w_up)
    grad_middle = grad_top + norm_back(grad_hidden, gain_two, hat_two, root_two)
    grad_attn = grad_middle.astype(BF16)
    g_out = scatter(t_mm(context, grad_attn).reshape(devices, width // devices, width))
    grad_context = mm_t(grad_attn, w_out).astype(BF16).reshape(item_count, seq, heads, HEAD_DIM)
    grad_probs = jnp.einsum("ishd,ithd->ihst", grad_context, value, preferred_element_type=F32)
    value_grad = jnp.einsum(
        "ihst,ishd->ithd", probs_low, grad_context, preferred_element_type=F32
    ).astype(BF16)
    grad_scores = (
        probs * (grad_probs - jnp.sum(probs * grad_probs, axis=-1, keepdims=True))
    ).astype(BF16)
    query_grad = (
        jnp.einsum("ihst,ithd->ishd", grad_scores, key, preferred_element_type=F32) * scale
    ).astype(BF16)
    key_grad = (
        jnp.einsum("ihst,ishd->ithd", grad_scores, query, preferred_element_type=F32) * scale
    ).astype(BF16)
    grad_packed = jnp.stack([query_grad, key_grad, value_grad], axis=2).reshape(rows, 3 * width)
    g_qkv = t_mm(normed, grad_packed)
    g_qkv = (
        g_qkv.reshape(n_dp, width // n_dp, 3, n_head, width // n_head)
        .transpose(0, 3, 1, 2, 4)
        .reshape(devices, width // n_dp, 3 * (width // n_head))
    )
    g_qkv = scatter(g_qkv).reshape(width // n_dp, 3, width // n_head)
    grad_normed = mm_t(grad_packed, w_qkv)
    tokens_grad = (grad_middle + norm_back(grad_normed, gain_one, hat_one, root_one)).astype(BF16)

    def total(matrix):
        return jnp.sum(matrix.astype(F32), axis=0)

    def from_head(vector):
        return vector.reshape(n_head, n_dp, -1).transpose(1, 0, 2).reshape(devices, -1)

    packed_total = total(grad_packed)
    sums = jnp.concatenate(
        [
            v.reshape(devices, per)
            for v in (
                total(grad_normed * hat_one),
                total(grad_normed),
                total(grad_attn),
                total(grad_hidden * hat_two),
                total(grad_hidden),
                total(grad_low),
            )
        ]
        + [
            from_head(packed_total[:width]),
            from_head(packed_total[2 * width :]),
            from_head(total(grad_up)),
        ],
        axis=1,
    )
    sums = lax.psum_scatter(sums, ALL, scatter_dimension=0, tiled=True)[0]

    def part(index):
        return sums[index * per : (index + 1) * per]

    return (
        layer_out,
        tokens_grad,
        part(0),
        part(1),
        g_qkv,
        sums[6 * per : 8 * per].reshape(2, per),
        g_out,
        part(2),
        part(3),
        part(4),
        g_up,
        sums[8 * per :],
        g_down_t.T,
        part(5),
    )


def solution(mesh):
    n_dp, n_head = mesh.shape["dp"], mesh.shape["head"]

    def run(*args):
        return local(n_dp, n_head, *args)

    return jax.shard_map(
        run,
        mesh=mesh,
        in_specs=(
            P(ALL, None),
            P("dp"),
            P(ALL),
            P(ALL),
            P("dp", None, "head"),
            P(None, ("head", "dp")),
            P(ALL, None),
            P(ALL),
            P(ALL),
            P(ALL),
            P("dp", "head"),
            P(("head", "dp")),
            P("head", "dp"),
            P(ALL),
            P(ALL, None),
        ),
        out_specs=(
            P(ALL, None),
            P(ALL, None),
            P(ALL),
            P(ALL),
            P("dp", None, "head"),
            P(None, ("head", "dp")),
            P(ALL, None),
            P(ALL),
            P(ALL),
            P(ALL),
            P("dp", "head"),
            P(("head", "dp")),
            P("head", "dp"),
            P(ALL),
        ),
        check_vma=False,
    )
```

time: 720 us -> 751 us (1.043)
  waiting for transfers between devices: 275 us -> 439 us
  blocking collectives: 233 us -> 82.1 us
  local copies, waits for them, and re-layouts: 78.2 us -> 123 us
  starting transfers between devices: 17.2 us -> 0.78 us
  matrix products: 68.1 us -> 60.1 us
    reduce_scatter x4, waiting for transfers between devices: 159 us -> 292 us  [scatter(): lax.psum_scatter(tiles.astype(BF16), ALL, scatter_dimension=0, tiled=True)]
    unnamed x5 -> x2, blocking collectives: 176 us -> 82.1 us
    all_gather x7 -> x4, waiting for transfers between devices: 85.6 us -> 144 us  [gather(): return lax.all_gather(piece, ALL, axis=0)]
    all_gather x2 -> x0, blocking collectives: 56.3 us -> none  [the longest x1 36.1 us: local(): lax.all_gather(qkv_weight, 'dp', axis=0, tiled=True)]
    convert_element_type x5 -> x8, local copies, waits for them, and re-layouts: 6.69 us -> 44.7 us  [the longest x6 43.8 us: scatter(): tiles.astype(BF16)]
    reshape x2 -> x22, local copies, waits for them, and re-layouts: 7.54 us -> 40.5 us  [the longest x2 12.1 us: square(): tiles.reshape(n_dp, n_head, width // n_dp, hidden // n_head)]
    all_to_all x3 -> x0, waiting for transfers between devices: 27.3 us -> none  [the longest x1 12.6 us: local(): lax.all_to_all(grad_packed.reshape(group_rows, 3, local_width), 'head', s...]
    unnamed x111 -> x92, local copies, waits for them, and re-layouts: 34 us -> 19.1 us
  transfers between devices with their start and end apart: 16 -> 8, of which waited for: 10 -> 7; matrix products, arithmetic and copies ran while one was open for 29% -> 21% of each run, Pallas kernels for 0% -> 0%
where the time goes in v1:
time: 751 us; the launch traced here: 740 us
  waiting for transfers between devices  439 us (58%)
  local copies, waits for them, and re-layouts  123 us (16%)
  blocking collectives  82.1 us (11%)
  matrix products  60.1 us (8%)
  other arithmetic  20.1 us (3%)
  between operations  15.2 us (2%)
    reduce_scatter x4, waiting for transfers between devices, scatter(): lax.psum_scatter(tiles.astype(BF16), ALL, scatter_dimension=0, tiled=True)  292 us
    all_gather x4, waiting for transfers between devices, gather(): return lax.all_gather(piece, ALL, axis=0)  144 us
    unnamed x2, blocking collectives  82.1 us
    convert_element_type x6, local copies, waits for them, and re-layouts, scatter(): tiles.astype(BF16)  43.8 us
    dot_general x4, matrix products, t_mm(): lax.dot_general(a, b, (((0,), (0,)), ((), ())), preferred_element_type=F32)  20.7 us
    unnamed x92, local copies, waits for them, and re-layouts  19.1 us
  transfers between devices with their start and end apart: 8, of which 7 were waited for; matrix products, arithmetic and copies ran while one was open for 21% of the time, Pallas kernels for 0%

profile of v1, /device:TPU:0, one launch (start us, length us, event | category | flops | bytes accessed | tf_op | source)
XLA Modules:
  0.0 740.1 jit_solution(4650993745215177978)
XLA Ops:
  10.8 4.8 concatenate.9
  15.8 42.6 %all-reduce = bf16[9216]{0:T(1024)(128)(2,1)S(1)} all-reduce(bf16[9216]{0:T(1024)(128)(2,1)S(1)} %dynamic-update-slice), channel_id=2, replica_groups=mesh['dp'=8,'head'=4] {'dp','head'}, use_global_device_ids=true, to_apply=%add | all-reduce | flops 9216 | bytes 36864
  60.8 1.2 convert_reduce_fusion.2
  62.0 1.4 fusion.35
  63.5 13.8 %all-gather.10.cloned.1.call-done = bf16[3072,3,192]{2,0,1:T(8,128)(2,1)} async-done(((bf16[96,3,192]{2,0,1:T(8,128)(2,1)}), bf16[3072,3,192]{2,0,1:T(8,128)(2,1)}) %all-gather.10.cloned.1.call-update) | async-done | bytes 3538960 | tf_op jit(solution)/shard_map/all_gather | solution.py:65
  77.3 7.0 copy.93
  84.3 8.3 %reshape.244 = bf16[768,2304]{0,1:T(8,128)(2,1)} reshape(bf16[8,96,3,4,192]{1,0,4,3,2:T(8,128)(2,1)} %bitcast.154) | data formatting | bytes 7077888 | tf_op jit(solution)/shard_map/reshape | solution.py:101
  92.7 3.7 fusion.8
  96.4 4.7 reshape.289
  101.1 4.8 fusion.51
  105.8 2.1 copy.131
  108.0 1.9 copy.130
  109.9 2.1 copy.132
  112.0 0.8 fusion.37
  112.9 2.5 fusion.54
  116.0 1.5 copy-done.3
  117.5 0.8 copy.101
  118.4 1.3 reshape.250
  119.7 12.9 %all-gather.12.cloned.1.call-done = bf16[768,768]{1,0:T(8,128)(2,1)} async-done(((bf16[24,768]{1,0:T(8,128)(2,1)}), bf16[768,768]{1,0:T(8,128)(2,1)}) %all-gather.12.cloned.1.call-update) | async-done | bytes 1179664 | tf_op jit(solution)/shard_map/all_gather | solution.py:65
  132.5 2.2 fusion.55
  134.8 1.0 copy-done.4
  136.1 61.9 %all-gather.14.cloned.1.call-done = bf16[3072,768]{1,0:T(8,128)(2,1)} async-done(((bf16[96,768]{1,0:T(8,128)(2,1)}), bf16[3072,768]{1,0:T(8,128)(2,1)}) %all-gather.14.cloned.1.call-update) | async-done | bytes 4718608 | tf_op jit(solution)/shard_map/all_gather | solution.py:65
  197.9 6.0 copy.102
  203.9 3.1 copy.133
  207.1 55.5 %all-gather.16.cloned.1.call-done = bf16[3072,768]{1,0:T(8,128)(2,1)} async-done(((bf16[96,768]{1,0:T(8,128)(2,1)}), bf16[3072,768]{1,0:T(8,128)(2,1)}) %all-gather.16.cloned.1.call-update) | async-done | bytes 4718608 | tf_op jit(solution)/shard_map/all_gather | solution.py:65
  262.6 6.1 copy.104
  268.8 1.2 copy.134
  270.2 4.0 multiply_convert_fusion.1
  274.1 4.0 convert_reduce_fusion.1
  278.2 2.9 multiply_reduce_fusion.1
  281.1 1.1 convert_reduce_fusion.4
  283.0 2.0 reshape.290
  285.0 2.9 copy.106
  287.9 3.6 fusion.22
  291.5 6.1 multiply_reduce_fusion
  297.6 1.8 convolution_convert_fusion.2
  299.7 4.9 multiply_convert_fusion
  304.5 0.9 fusion.24
  306.6 2.5 copy.111
  309.1 2.5 reshape.258
  311.6 4.2 fusion.56
  315.8 1.1 copy-done.7
  317.0 0.8 fusion.34
  318.0 6.2 convert_bitcast_fusion
  324.2 6.8 copy.116
  331.4 0.9 copy-done.6
  332.3 6.2 convolution_convert_fusion.1
  338.5 9.8 %convert_element_type.173 = bf16[8,96,4,768]{3,2,1,0:T(4,128)(2,1)} reshape(bf16[768,3072]{1,0:T(8,128)(2,1)} %convolution_convert_fusion.1) | data formatting | bytes 9437184 | tf_op jit(solution)/shard_map/convert_element_type | solution.py:154
  348.3 5.5 copy.117
  353.9 1.0 copy-done.14
  354.8 6.5 fusion.7
  361.4 6.6 copy.118
  368.0 9.8 %convert_element_type.180 = bf16[8,96,4,768]{3,2,1,0:T(4,128)(2,1)} reshape(bf16[768,3072]{1,0:T(8,128)(2,1)} %copy.118) | data formatting | bytes 9437184 | tf_op jit(solution)/shard_map/convert_element_type | solution.py:154
  377.8 5.3 copy.119
  384.7 39.5 %all-reduce.1 = f32[32,288]{1,0:T(8,128)S(1)} all-reduce(f32[32,288]{1,0:T(8,128)S(1)} %concatenate.11), channel_id=7, replica_groups=mesh['dp'=8,'head'=4] {'dp','head'}, use_global_device_ids=true, to_apply=%region_19.20.clone | all-reduce | flops 9216 | bytes 73728
  426.1 2.5 fusion.33
  428.7 5.3 fusion.20
  434.0 1.4 bitcast_convert_fusion.1
  435.4 71.4 %reduce-scatter.5.cloned.1.call-done = bf16[1,96,576]{1,2,0:T(8,128)(2,1)} async-done(((bf16[32,96,576]{1,2,0:T(8,128)(2,1)}), bf16[1,96,576]{1,2,0:T(8,128)(2,1)}) %reduce-scatter.5.cloned.1.call-update) | async-done | bytes 110608 | tf_op jit(solution)/shard_map/reduce_scatter | solution.py:154
  506.8 1.8 copy.120
  508.6 110.5 %reduce-scatter.9.cloned.1.call-done = bf16[1,96,768]{2,1,0:T(8,128)(2,1)} async-done(((bf16[32,96,768]{2,1,0:T(8,128)(2,1)}), bf16[1,96,768]{2,1,0:T(8,128)(2,1)}) %reduce-scatter.9.cloned.1.call-update) | async-done | bytes 147472 | tf_op jit(solution)/shard_map/reduce_scatter | solution.py:154
  619.1 1.6 bitcast_convert_fusion
  620.8 110.4 %reduce-scatter.11.cloned.1.call-done = bf16[1,96,768]{2,1,0:T(8,128)(2,1)} async-done(((bf16[32,96,768]{2,1,0:T(8,128)(2,1)}), bf16[1,96,768]{2,1,0:T(8,128)(2,1)}) %reduce-scatter.11.cloned.1.call-update) | async-done | bytes 147472 | tf_op jit(solution)/shard_map/reduce_scatter | solution.py:154
  731.2 1.6 convert_bitcast_fusion.1
  (151 shorter events, 13.6 us)
Async XLA Ops:
  7.2 70.1 %all-gather.10.cloned.1.call-start = ((), (), s32[]{:S(2)}) async-start(), calls=%async_computation.8 | async-start | bytes 4866048 | tf_op jit(solution)/shard_map/all_gather | solution.py:65
  7.9 124.6 %all-gather.12.cloned.1.call-start = ((), (), s32[]{:S(2)}) async-start(), calls=%async_computation.9 | async-start | bytes 1216512 | tf_op jit(solution)/shard_map/all_gather | solution.py:65
  8.7 189.3 %all-gather.14.cloned.1.call-start = ((), (), s32[]{:S(2)}) async-start(), calls=%async_computation.10 | async-start | bytes 4866048 | tf_op jit(solution)/shard_map/all_gather | solution.py:65
  9.4 253.2 %all-gather.16.cloned.1.call-start = ((), (), s32[]{:S(2)}) async-start(), calls=%async_computation.11 | async-start | bytes 4866048 | tf_op jit(solution)/shard_map/all_gather | solution.py:65
  10.0 424.0 %reduce-scatter.7.cloned.1.call-start = ((), (), s32[]{:S(2)}) async-start(), calls=%async_computation.5 | async-start | bytes 1216512 | tf_op jit(solution)/shard_map/reduce_scatter | solution.py:154
  58.9 222.2 %copy-start.27 = (f32[768]{0:T(1024)}, f32[768]{0:T(1024)S(1)}, u32[]{:S(2)}) copy-start(f32[768]{0:T(1024)S(1)} %mul.165) | copy-start | bytes 9220
  59.0 33.7 %copy-start.15 = (f32[768]{0:T(1024)}, f32[768]{0:T(1024)S(1)}, u32[]{:S(2)}) copy-start(f32[768]{0:T(1024)S(1)} %mul.156) | copy-start | bytes 9220
  59.7 32.9 %copy-start.25 = (f32[768]{0:T(1024)}, f32[768]{0:T(1024)S(1)}, u32[]{:S(2)}) copy-start(f32[768]{0:T(1024)S(1)} %add.109) | copy-start | bytes 9220
  62.0 30.6 %copy-start.19 = (f32[370]{0:T(512)}, f32[370]{0:T(512)S(1)}, u32[]{:S(2)}) copy-start(f32[370]{0:T(512)S(1)} %broadcast_multiply_fusion.5) | copy-start | bytes 4444
  63.5 29.2 %copy-start.23 = (f32[370]{0:T(512)}, f32[370]{0:T(512)S(1)}, u32[]{:S(2)}) copy-start(f32[370]{0:T(512)S(1)} %add_rsqrt_fusion.1) | copy-start | bytes 4444
  84.3 8.3 %copy-start = (bf16[370,768]{1,0:T(8,128)(2,1)S(1)}, bf16[370,768]{1,0:T(8,128)(2,1)}, u32[]{:S(2)}) copy-start(bf16[370,768]{1,0:T(8,128)(2,1)} %param.15) | copy-start | bytes 1704964
  112.9 2.5 copy-start.10
  115.4 2.1 copy-start.3
  115.4 2.2 copy-start.17
  134.7 1.1 copy-start.4
  134.8 146.3 %copy-start.21 = (f32[370]{0:T(512)}, f32[370]{0:T(512)S(1)}, u32[]{:S(2)}) copy-start(f32[370]{0:T(512)S(1)} %broadcast_multiply_fusion.4) | copy-start | bytes 4444
  136.1 145.0 %copy-start.32 = (f32[370]{0:T(512)}, f32[370]{0:T(512)S(1)}, u32[]{:S(2)}) copy-start(f32[370]{0:T(512)S(1)} %add_rsqrt_fusion) | copy-start | bytes 4444
  262.6 7.4 slice-start
  268.7 1.3 slice-start.1
  268.7 1.4 copy-start.5
  268.7 1.4 copy-start.34
  270.0 4.1 copy-start.2
  270.2 4.0 copy-start.13
  278.2 2.9 copy-start.38
  281.0 1.3 copy-start.9
  287.9 3.6 copy-start.11
  287.9 3.6 copy-start.12
  287.9 3.6 copy-start.18
  291.5 6.1 copy-start.8
  299.4 207.5 %reduce-scatter.5.cloned.1.call-start = ((), (), s32[]{:S(2)}) async-start(), calls=%async_computation.4 | async-start | bytes 4866048 | tf_op jit(solution)/shard_map/reduce_scatter | solution.py:154
  311.6 5.3 copy-start.1
  311.6 5.3 copy-start.16
  311.6 5.3 copy-start.20
  311.6 5.3 copy-start.24
  311.6 5.3 copy-start.26
  315.8 1.1 copy-start.7
  331.1 1.3 copy-start.6
  331.1 1.3 copy-start.22
  331.1 1.3 copy-start.28
  331.1 1.3 copy-start.33
  331.1 1.3 copy-start.35
  331.1 288.0 %reduce-scatter.9.cloned.1.call-start = ((), (), s32[]{:S(2)}) async-start(), calls=%async_computation.6 | async-start | bytes 4866048 | tf_op jit(solution)/shard_map/reduce_scatter | solution.py:154
  353.8 1.1 copy-start.14
  353.8 377.4 %reduce-scatter.11.cloned.1.call-start = ((), (), s32[]{:S(2)}) async-start(), calls=%async_computation.7 | async-start | bytes 4866048 | tf_op jit(solution)/shard_map/reduce_scatter | solution.py:154
  383.1 0.7 copy-start.31
  383.1 0.8 copy-start.30
  383.1 0.9 copy-start.37
  383.1 1.0 copy-start.29
  383.1 1.1 copy-start.36
  424.9 3.7 copy-start.39
Sparse Core Ops, SparseCore 0:
  10.9 66.3 all-gather.9
  80.2 52.2 all-gather.11
  135.4 62.4 all-gather.13
  200.7 61.8 all-gather.15
  299.5 95.4 reduce-scatter.6
  400.3 106.4 reduce-scatter.4
  512.3 106.7 reduce-scatter.8
  624.6 106.5 reduce-scatter.10

commit v2 on v1

v2 whole, which is shorter than its diff:
```python
import functools

import jax
import jax.numpy as jnp
from jax import lax
from jax.experimental.layout import Layout, with_layout_constraint
from jax.experimental import pallas as pl
from jax.experimental.pallas import tpu as pltpu
from jax.sharding import PartitionSpec as P

HEAD_DIM = 64
TEXT = 40
ALL = ("dp", "head")
F32 = jnp.float32
BF16 = jnp.bfloat16


def mm(a, b):
    return jnp.dot(a, b, preferred_element_type=F32)


def mm_t(a, b):
    return lax.dot_general(a, b, (((1,), (1,)), ((), ())), preferred_element_type=F32)


def t_mm(a, b):
    return lax.dot_general(a, b, (((0,), (0,)), ((), ())), preferred_element_type=F32)


def norm_parts(values):
    spread = values - jnp.mean(values, axis=-1, keepdims=True)
    root = lax.rsqrt(jnp.mean(spread * spread, axis=-1, keepdims=True) + 1e-06)
    return spread * root, root


def norm_back(grad, gain, hat, root):
    scaled = grad * gain
    first = jnp.mean(scaled, axis=-1, keepdims=True)
    second = jnp.mean(scaled * hat, axis=-1, keepdims=True)
    return root * (scaled - first - hat * second)


VMEM = pltpu.VMEM


def spec(shape, index):
    return pl.BlockSpec(shape, index, memory_space=VMEM)


def whole(shape):
    return spec(shape, lambda *_: (0,) * len(shape))


def chunk(shape):
    return spec((1,) + shape, lambda j, *_: (j,) + (0,) * len(shape))


def nearer(t, near, far):
    return jnp.where(t < pl.num_programs(0) // 2, near[0], far[0])


def store(t, near, far, value):
    half = pl.num_programs(0) // 2

    @pl.when(t < half)
    def _():
        near[0] = value

    @pl.when(t >= half)
    def _():
        far[0] = value


def column_sum(matrix):
    return jnp.sum(matrix.astype(F32), axis=0, keepdims=True)


def attention_forward(
    items,
    seq,
    lengths,
    order,
    x,
    vectors,
    qk_near,
    qk_far,
    vo_near,
    vo_far,
    b_qv,
    out_q,
    out_k,
    out_v,
    out_p,
    out_c,
    normed,
):
    t = pl.program_id(0)
    rows = x.shape[0] // items
    cols = out_q.shape[2]
    scale = HEAD_DIM**-0.5

    @pl.when(t == 0)
    def _():
        hat, _ = norm_parts(x[...].astype(F32))
        normed[...] = (hat * vectors[0:1, :] + vectors[1:2, :]).astype(BF16)

    bias = b_qv[order[t]]
    both = mm(normed[...], nearer(t, qk_near, qk_far))
    query = (both[:, :cols] + bias[0:1, :]).astype(BF16)
    key = both[:, cols:].astype(BF16)
    value = (mm(normed[...], nearer(t, vo_near, vo_far)[:, :cols]) + bias[1:2, :]).astype(BF16)
    out_q[0] = query
    out_k[0] = key
    out_v[0] = value
    heads = cols // HEAD_DIM
    at = lax.broadcasted_iota(jnp.int32, (rows, rows), 1)
    for item in range(items):
        mine = slice(item * rows, (item + 1) * rows)
        visible = ((at >= TEXT) & (at < seq)) | (at < lengths[item])
        parts = []
        for head in range(heads):
            lanes = slice(head * HEAD_DIM, (head + 1) * HEAD_DIM)
            scores = mm_t(query[mine, lanes], key[mine, lanes]) * scale
            scores = jnp.where(visible, scores, -1000000000.0)
            raised = jnp.exp(scores - jnp.max(scores, axis=-1, keepdims=True))
            probs = raised / jnp.sum(raised, axis=-1, keepdims=True)
            out_p[0, item * heads + head] = probs
            parts.append(mm(probs.astype(BF16), value[mine, lanes]))
        out_c[0, mine, :] = jnp.concatenate(parts, axis=1).astype(BF16)


def feed_forward(
    order,
    x,
    ctx,
    w_out,
    vectors,
    top,
    turn,
    up_near,
    up_far,
    down_near,
    down_far,
    b_up,
    out_y,
    out_gm,
    out_gc,
    out_go,
    gup_near,
    gup_far,
    gdown_near,
    gdown_far,
    out_bu,
    out_sums,
    middle,
    hat,
    root,
    hidden,
    hidden_t,
    top_t,
    sum_y,
    sum_h,
):
    t, n = pl.program_id(0), pl.program_id(1)
    chunks, _, cols = ctx.shape
    gain = vectors[3:4, :]

    def span(c):
        return pl.ds(pl.multiple_of(order[c] * cols, cols), cols)

    @pl.when((t == 0) & (n == 0))
    def _():
        total = x[...].astype(F32) + vectors[2:3, :]
        for c in range(chunks):
            total += mm(ctx[c], w_out[span(c), :])
        middle[...] = total
        hat_two, root_two = norm_parts(total)
        hat[...] = hat_two
        root[...] = root_two
        low = hat_two * gain + vectors[4:5, :]
        hidden[...] = low.astype(BF16)
        hidden_t[...] = low.T.astype(BF16)
        top_t[...] = top[...].astype(F32).T.astype(BF16)
        sum_y[...] = jnp.zeros_like(sum_y)
        sum_h[...] = jnp.zeros_like(sum_h)

    def work(up_ref, down_ref, gup, gdown):
        w_up, w_down_t = up_ref[0], down_ref[0]
        up = mm(hidden[...], w_up) + b_up[0]
        phi = 0.5 * (1.0 + lax.erf(up * (0.5**0.5)))
        active = (up * phi).astype(BF16)
        slope = phi + up * jnp.exp(-0.5 * up * up) * ((2.0 * jnp.pi) ** -0.5)
        grad_up = (mm(top[...], w_down_t) * slope).astype(BF16)
        sum_y[...] += mm_t(active, w_down_t)
        sum_h[...] += mm_t(grad_up, w_up)
        gdown[0] = mm(top_t[...], active).astype(BF16)
        gup[0] = mm(hidden_t[...], grad_up).astype(BF16)
        out_bu[0] = column_sum(grad_up)

    @pl.when(t < pl.num_programs(0) // 2)
    def _():
        work(up_near, down_near, gup_near, gdown_near)

    @pl.when(t >= pl.num_programs(0) // 2)
    def _():
        work(up_far, down_far, gup_far, gdown_far)

    @pl.when((t == pl.num_programs(0) - 1) & (n == pl.num_programs(1) - 1))
    def _():
        out_y[...] = (middle[...] + (sum_y[...] + vectors[5:6, :])).astype(BF16)
        grad_hidden = sum_h[...]
        grad_top = top[...].astype(F32)
        grad_middle = grad_top + norm_back(grad_hidden, gain, hat[...], root[...])
        out_gm[...] = grad_middle
        grad_attn = grad_middle.astype(BF16)
        out_sums[0:1, :] = column_sum(grad_attn)
        out_sums[1:2, :] = column_sum(grad_hidden * hat[...])
        out_sums[2:3, :] = column_sum(grad_hidden)
        out_sums[3:4, :] = column_sum(grad_top)
        for c in range(chunks):
            out_gc[c] = mm_t(grad_attn, w_out[span(c), :]).astype(BF16)
            grad_out = t_mm(ctx[c], grad_attn).astype(BF16)
            out_go[span(c), :] = mm_t(grad_out, turn[...]).astype(BF16)


def attention_backward(
    items,
    x,
    vectors,
    qk_near,
    qk_far,
    vo_near,
    vo_far,
    grad_out,
    query,
    key,
    value,
    probs,
    grad_ctx,
    grad_middle,
    out_x,
    gqk_near,
    gqk_far,
    gvo_near,
    gvo_far,
    out_b,
    out_sums,
    hat,
    root,
    normed_t,
    sum_n,
):
    rows = x.shape[0] // items
    cols = query.shape[2]
    heads = cols // HEAD_DIM
    scale = HEAD_DIM**-0.5
    t = pl.program_id(0)
    gain = vectors[0:1, :]

    @pl.when(t == 0)
    def _():
        hat_one, root_one = norm_parts(x[...].astype(F32))
        hat[...] = hat_one
        root[...] = root_one
        normed_t[...] = (hat_one * gain + vectors[1:2, :]).T.astype(BF16)
        sum_n[...] = jnp.zeros_like(sum_n)

    whole_q, whole_k, whole_v = [], [], []
    for item in range(items):
        mine = slice(item * rows, (item + 1) * rows)
        parts_q, parts_k, parts_v = [], [], []
        for head in range(heads):
            lanes = slice(head * HEAD_DIM, (head + 1) * HEAD_DIM)
            p = probs[0, item * heads + head]
            g = grad_ctx[0, mine, lanes]
            grad_p = mm_t(g, value[0, mine, lanes])
            parts_v.append(t_mm(p.astype(BF16), g))
            row = jnp.sum(p * grad_p, axis=-1, keepdims=True)
            grad_s = (p * (grad_p - row)).astype(BF16)
            parts_q.append(mm(grad_s, key[0, mine, lanes]) * scale)
            parts_k.append(t_mm(grad_s, query[0, mine, lanes]) * scale)
        whole_q.append(jnp.concatenate(parts_q, axis=1))
        whole_k.append(jnp.concatenate(parts_k, axis=1))
        whole_v.append(jnp.concatenate(parts_v, axis=1))
    grad_all = jnp.concatenate(
        [jnp.concatenate(parts, axis=0) for parts in (whole_q, whole_k, whole_v)], axis=1
    ).astype(BF16)
    out_b[0] = column_sum(grad_all)
    grad_qk, grad_v = grad_all[:, : 2 * cols], grad_all[:, 2 * cols :]
    store(t, gqk_near, gqk_far, mm(normed_t[...], grad_qk).astype(BF16))
    grad_weight = mm(normed_t[...], grad_v).astype(BF16)
    store(t, gvo_near, gvo_far, jnp.concatenate([grad_weight, grad_out[0]], axis=1))
    sum_n[...] += mm_t(grad_qk, nearer(t, qk_near, qk_far))
    sum_n[...] += mm_t(grad_v, nearer(t, vo_near, vo_far)[:, :cols])

    @pl.when(t == pl.num_programs(0) - 1)
    def _():
        grad_normed = sum_n[...]
        back = norm_back(grad_normed, gain, hat[...], root[...])
        out_x[...] = (grad_middle[...] + back).astype(BF16)
        out_sums[0:1, :] = column_sum(grad_normed * hat[...])
        out_sums[1:2, :] = column_sum(grad_normed)


def call(body, grid, in_specs, outs, scratch, flops, moved, *args):
    return pl.pallas_call(
        body,
        grid=grid,
        in_specs=in_specs,
        out_specs=[o[1] for o in outs],
        out_shape=[jax.ShapeDtypeStruct(*o[0]) for o in outs],
        scratch_shapes=scratch,
        compiler_params=pltpu.CompilerParams(
            dimension_semantics=("arbitrary",) * len(grid), vmem_limit_bytes=60 * 1024 * 1024
        ),
        cost_estimate=pl.CostEstimate(flops=flops, bytes_accessed=moved, transcendentals=0),
    )(*args)


def local(
    n_dp,
    n_head,
    tokens,
    caption_len,
    first_gain,
    first_shift,
    qkv_weight,
    qkv_bias,
    out_weight,
    out_bias,
    second_gain,
    second_shift,
    up_weight,
    up_bias,
    down_weight,
    down_bias,
    output_grad,
):
    rows, width = tokens.shape
    hidden = up_weight.shape[1] * n_head
    devices = n_dp * n_head
    item_count = caption_len.shape[0] // n_head
    seq = rows // item_count
    dp_bits = [("dp", 1 << i) for i in reversed(range(n_dp.bit_length() - 1))]
    head_bits = [("head", 1 << i) for i in reversed(range(n_head.bit_length() - 1))]
    held = (dp_bits + head_bits)[::-1]
    along_z, along_x, along_y = dp_bits[:-1], dp_bits[-1:], head_bits[:-1]
    core = head_bits[-1]

    def flip(piece, step):
        axis, bit = step
        count = n_dp if axis == "dp" else n_head
        rows_first = Layout(tuple(range(piece.ndim)))
        piece = with_layout_constraint(piece, rows_first)
        piece = lax.ppermute(piece, axis, [(i, i ^ bit) for i in range(count)])
        return with_layout_constraint(piece, rows_first)

    def together(*values):
        return lax.optimization_barrier(values)

    def place_of(step, have):
        return sum(held.index(h) < held.index(step) for h in have)

    def grow(piece, step, have):
        other = flip(piece, step)
        piece = jnp.stack([piece, other], axis=place_of(step, have))
        have.append(step)
        return piece

    def add(terms, which, place):
        terms = [lax.index_in_dim(term, which, place, False) for term in terms]
        return (terms[0].astype(F32) + terms[1].astype(F32)).astype(BF16)

    def shrink(terms, step, have):
        place = have.index(step)
        have.remove(step)
        near, far = add(terms, 0, place), add(terms, 1, place)
        return near, far

    def reverse_bits(value, count):
        return sum(
            ((value >> i) & 1) << (count.bit_length() - 2 - i) for i in range(count.bit_length() - 1)
        )

    my_dp, my_head = lax.axis_index("dp"), lax.axis_index("head")
    order_chunks = my_head ^ reverse_bits(jnp.arange(n_head, dtype=jnp.int32), n_head)
    order_blocks = my_dp ^ reverse_bits(jnp.arange(n_dp, dtype=jnp.int32), n_dp)

    def exchange(blocks):
        return lax.all_to_all(blocks, ALL, 0, 0, tiled=True)

    per = first_gain.shape[0]
    pieces = [first_gain, first_shift, out_bias, second_gain, second_shift, down_bias]
    pieces += [qkv_bias[0], qkv_bias[1], up_bias]
    small_size = sum(piece.shape[0] for piece in pieces)
    smalls, start = 0, 0
    for piece in pieces:
        stop = start + piece.shape[0]
        smalls += jnp.pad(piece, (start, small_size - stop))
        start = stop
    part_rows = width // n_dp
    part_cols = width // n_head
    part_hidden = up_weight.shape[1]
    part_hidden = up_weight.shape[1]
    features = jnp.arange(width, dtype=jnp.int32)
    place = jnp.repeat(order_blocks, part_rows) * part_rows + features % part_rows
    turn = (features[:, None] == place[None, :]).astype(BF16)

    def turned(piece):
        return mm(piece, turn).astype(BF16)

    def turned_back(piece):
        return mm_t(piece, turn).astype(BF16)

    ranks = order_blocks[None, :] * n_head + order_chunks[:, None]
    ranks = ranks.reshape(-1)
    chunk_of = reverse_bits(my_head ^ jnp.arange(n_head, dtype=jnp.int32), n_head)
    block_of = reverse_bits(my_dp ^ jnp.arange(n_dp, dtype=jnp.int32), n_dp)
    ranks_back = (chunk_of[None, :] * n_dp + block_of[:, None]).reshape(-1)
    padded = -(-seq // 16) * 16
    total_rows = item_count * padded

    def pad(piece):
        piece = piece.reshape(item_count, seq, width)
        return jnp.pad(piece, ((0, 0), (0, padded - seq), (0, 0))).reshape(total_rows, width)

    def unpad(piece):
        return piece.reshape(item_count, padded, width)[:, :seq].reshape(rows, width)

    def out_pack(piece):
        return piece.reshape(-1, n_head, part_cols).transpose(1, 0, 2).reshape(part_rows, part_cols)

    have, have_rest = [], []
    first = [qkv_weight.reshape(part_rows, 3 * part_cols), out_pack(out_weight)]
    first = jnp.concatenate(first, axis=1)
    rest = jnp.concatenate([up_weight, down_weight.T])
    for step in along_z[:-1]:
        first = grow(first, step, have)
    first, smalls, turn = together(first, smalls, turn)
    x, top = turned(pad(tokens)), turned(pad(output_grad))
    smalls = exchange(jnp.broadcast_to(smalls[None], (devices,) + smalls.shape))

    smalls = smalls.reshape(n_dp, n_head, -1)
    vectors = smalls[..., : 6 * per].reshape(n_dp, n_head, 6, per).transpose(2, 0, 1, 3)
    vectors = vectors.reshape(6, width)
    b_qv = smalls[..., 6 * per : 8 * per].reshape(n_dp, n_head, 2, per).transpose(1, 2, 0, 3)
    b_qv = b_qv.reshape(n_head, 2, n_dp * per).astype(F32)
    b_up = smalls[..., 8 * per :].transpose(1, 0, 2).reshape(n_head, 1, -1).astype(F32)

    first = grow(first, along_z[-1], have)
    first, rest, x, top, vectors, b_qv, b_up = together(
        first, rest, x, top, vectors, b_qv, b_up
    )
    vectors = turned(vectors).astype(F32)
    w_qk, w_vo = first[..., : 2 * part_cols], first[..., 2 * part_cols :]
    have_qk, have_vo = list(have), list(have)
    w_qk, w_vo = grow(w_qk, along_x[0], have_qk), grow(w_vo, along_y[0], have_vo)
    rest = grow(rest, along_z[0], have_rest)
    w_qk, w_vo, rest = together(w_qk, w_vo, rest)
    for step in along_z[1:-1]:
        rest = grow(rest, step, have_rest)
    for step in along_y[:-1]:
        w_qk = grow(w_qk, step, have_qk)
    for step in along_y[1:]:
        w_vo = grow(w_vo, step, have_vo)
    w_qk, w_vo = grow(w_qk, along_y[-1], have_qk), grow(w_vo, along_x[0], have_vo)
    rest = grow(rest, along_z[-1], have_rest)
    w_up, w_down = rest[..., :part_rows, :], rest[..., part_rows:, :]
    pair_shape = (-1, width, 2 * part_cols)
    near_qk, near_vo, w_up, w_down = together(
        w_qk.reshape(pair_shape), w_vo.reshape(pair_shape), w_up, w_down
    )
    far_qk, far_vo = flip(near_qk, core), flip(near_vo, core)
    have_up, have_down = list(have_rest), have_rest
    w_up_sent = flip(w_up, along_x[0])
    w_down_sent = flip(w_down, along_y[0])


    lengths = lax.dynamic_slice_in_dim(caption_len, my_head * item_count, item_count)
    pairs = item_count * (part_cols // HEAD_DIM)

    full = (total_rows, width)
    slab = (total_rows, part_cols)
    slab_out = (((n_head,) + slab, BF16), chunk(slab))
    probs_out = (((n_head, pairs, padded, padded), F32), chunk((pairs, padded, padded)))
    smem = pl.BlockSpec(memory_space=pltpu.SMEM)
    weights = width * width

    half = n_head // 2

    def near(shape):
        return spec((1,) + shape, lambda t: (jnp.minimum(t, half - 1), 0, 0))

    def far(shape):
        return spec((1,) + shape, lambda t: (jnp.maximum(t - half, 0), 0, 0))

    two_cols = (width, 2 * part_cols)
    first_specs = [near(two_cols), far(two_cols)] * 2
    query, key, value, probs, context = call(
        functools.partial(attention_forward, item_count, seq),
        (n_head,),
        [smem, smem, whole(full), whole(vectors.shape)]
        + first_specs
        + [whole(b_qv.shape)],
        [slab_out, slab_out, slab_out, probs_out, slab_out],
        [pltpu.VMEM(full, BF16)],
        8 * total_rows * weights,
        12 * weights,
        lengths,
        order_chunks,
        x,
        vectors,
        near_qk,
        far_qk,
        near_vo,
        far_vo,
        b_qv,
    )

    w_up, w_down, w_up_sent, w_down_sent, context = together(
        w_up, w_down, w_up_sent, w_down_sent, context
    )
    w_up = jnp.stack([w_up, w_up_sent], axis=place_of(along_x[0], have_up))
    w_down = jnp.stack([w_down, w_down_sent], axis=place_of(along_y[0], have_down))
    have_up.append(along_x[0])
    have_down.append(along_y[0])
    for step in along_y[:-1]:
        w_up = grow(w_up, step, have_up)
    for step in along_y[1:]:
        w_down = grow(w_down, step, have_down)
    w_up, w_down = together(w_up, w_down)
    w_up, w_down = grow(w_up, along_y[-1], have_up), grow(w_down, along_x[-1], have_down)
    w_out = jnp.concatenate([near_vo[..., part_cols:], far_vo[..., part_cols:]])
    w_out = w_out.reshape(devices, n_head, -1, part_cols).transpose(0, 2, 1, 3)
    w_out = w_out.reshape(devices, -1, width)
    w_out = turned(w_out[ranks_back].reshape(width, width))
    near_up, near_down, w_out = together(
        w_up.reshape(-1, width, part_hidden), w_down.reshape(-1, width, part_hidden), w_out
    )
    far_up, far_down = flip(near_up, core), flip(near_down, core)

    block = 256 if part_hidden % 256 == 0 else part_hidden
    steps = part_hidden // block

    def strip(index):
        return spec((1, width, block), index)

    near_strip = strip(lambda t, n: (jnp.minimum(t, half - 1), 0, jnp.where(t < half, n, steps - 1)))
    far_strip = strip(lambda t, n: (jnp.maximum(t - half, 0), 0, jnp.where(t < half, 0, n)))
    bias_out = spec((1, 1, block), lambda t, n: (t, 0, n))
    half_hidden = (half, width, part_hidden)
    (
        layer_out,
        grad_middle,
        grad_context,
        g_out,
        gup_near,
        gup_far,
        gdown_near,
        gdown_far,
        g_bu,
        sums_two,
    ) = call(
        feed_forward,
        (n_head, steps),
        [smem, whole(full), whole((n_head,) + slab), whole((width, width))]
        + [whole(vectors.shape), whole(full), whole((width, width))]
        + [near_strip, far_strip, near_strip, far_strip, bias_out],
        [
            ((full, BF16), whole(full)),
            ((full, F32), whole(full)),
            (((n_head,) + slab, BF16), whole((n_head,) + slab)),
            (((width, width), BF16), whole((width, width))),
            ((half_hidden, BF16), near_strip),
            ((half_hidden, BF16), far_strip),
            ((half_hidden, BF16), near_strip),
            ((half_hidden, BF16), far_strip),
            (((n_head, 1, part_hidden), F32), bias_out),
            (((4, width), F32), whole((4, width))),
        ],
        [
            pltpu.VMEM(full, F32),
            pltpu.VMEM(full, F32),
            pltpu.VMEM((total_rows, 1), F32),
            pltpu.VMEM(full, BF16),
            pltpu.VMEM(full[::-1], BF16),
            pltpu.VMEM(full[::-1], BF16),
            pltpu.VMEM(full, F32),
            pltpu.VMEM(full, F32),
        ],
        12 * total_rows * width * hidden,
        16 * weights,
        order_chunks,
        x,
        context,
        w_out,
        vectors,
        top,
        turn,
        near_up,
        far_up,
        near_down,
        far_down,
        b_up[order_chunks],
    )
    rest_bits = held[1:]
    shape = (2,) * len(rest_bits)
    tile = (part_rows, part_hidden)
    def pair(near, far, tile):
        return near.reshape(shape + tile), flip(far.reshape(shape + tile), core)

    down_terms = pair(gdown_near, gdown_far, tile)
    up_terms = pair(gup_near, gup_far, tile)

    have_down, have_up = list(rest_bits), list(rest_bits)
    first_x, first_y = have_down.index(along_x[0]), have_up.index(along_y[0])
    down_away = add(down_terms, 1, first_x)
    up_away = add(up_terms, 1, first_y)
    have_down.remove(along_x[0])
    have_up.remove(along_y[0])
    down_sent, up_sent = flip(down_away, along_x[0]), flip(up_away, along_y[0])
    grad_context, down_away, up_away = together(grad_context, down_away, up_away)
    g_out = g_out.reshape(devices, -1, width)[ranks]
    g_out = g_out.reshape(devices, -1, n_head, part_cols).transpose(0, 2, 1, 3)
    g_out = g_out.reshape(n_head, width, part_cols)

    tokens_grad, gqk_near, gqk_far, gvo_near, gvo_far, g_b, sums_one = call(
        functools.partial(attention_backward, item_count),
        (n_head,),
        [whole(full), whole(vectors.shape)]
        + first_specs
        + [chunk((width, part_cols))]
        + [chunk(slab)] * 3
        + [chunk((pairs, padded, padded)), chunk(slab), whole(full)],
        [
            ((full, BF16), whole(full)),
            (((half,) + two_cols, BF16), near(two_cols)),
            (((half,) + two_cols, BF16), far(two_cols)),
            (((half,) + two_cols, BF16), near(two_cols)),
            (((half,) + two_cols, BF16), far(two_cols)),
            (((n_head, 1, 3 * part_cols), F32), chunk((1, 3 * part_cols))),
            (((2, width), F32), whole((2, width))),
        ],
        [
            pltpu.VMEM(full, F32),
            pltpu.VMEM((total_rows, 1), F32),
            pltpu.VMEM(full[::-1], BF16),
            pltpu.VMEM(full, F32),
        ],
        16 * total_rows * weights,
        12 * weights,
        x,
        vectors,
        near_qk,
        far_qk,
        near_vo,
        far_vo,
        g_out,
        query,
        key,
        value,
        probs,
        grad_context,
        grad_middle,
    )
    two = (part_rows, 2 * part_cols)
    down_sent, up_sent, gqk_near, gqk_far, gvo_near, gvo_far = together(
        down_sent, up_sent, gqk_near, gqk_far, gvo_near, gvo_far
    )
    qk_terms, vo_terms = pair(gqk_near, gqk_far, two), pair(gvo_near, gvo_far, two)
    have_qk, have_vo = list(rest_bits), list(rest_bits)
    down_terms = (add(down_terms, 0, first_x), down_sent)
    up_terms = (add(up_terms, 0, first_y), up_sent)

    def descend(terms, steps, have):
        for step in steps:
            near, away = shrink(terms, step, have)
            terms = (near, flip(away, step))
        return terms

    def lockstep(*pairs):
        flat = together(*(term for terms in pairs for term in terms))
        return [tuple(flat[i : i + 2]) for i in range(0, len(flat), 2)]

    def descend_joined(one, other, axis, step, have):
        place = have.index(step)
        have.remove(step)
        near, away = (
            jnp.concatenate([add(one, which, place), add(other, which, place)], axis=axis)
            for which in (0, 1)
        )
        return near, flip(away, step)

    up_terms = descend(up_terms, along_y[1:] + along_x, have_up)
    down_terms = descend(down_terms, along_x[1:] + along_y, have_down)
    up_terms, down_terms, qk_terms, vo_terms = lockstep(up_terms, down_terms, qk_terms, vo_terms)
    qk_terms = descend(qk_terms, along_y[:1], have_qk)
    vo_terms = descend(vo_terms, along_x, have_vo)
    back_z = along_z[::-1]
    rest_terms = descend_joined(up_terms, down_terms, -2, back_z[0], have_up)
    rest_terms, qk_terms, vo_terms = lockstep(rest_terms, qk_terms, vo_terms)
    qk_terms = descend(qk_terms, along_y[1:] + along_x, have_qk)
    vo_terms = descend(vo_terms, along_y, have_vo)
    rest_terms = descend(rest_terms, back_z[1:], have_up)
    rest_terms, qk_terms, vo_terms = lockstep(rest_terms, qk_terms, vo_terms)
    first_terms = descend_joined(qk_terms, vo_terms, -1, back_z[0], have_qk)
    first_terms = descend(first_terms, back_z[1:], have_qk)
    rest = rest_terms[0].astype(F32) + rest_terms[1].astype(F32)
    g_up, g_down_t = rest[:part_rows], rest[part_rows:]
    first = first_terms[0].astype(F32) + first_terms[1].astype(F32)
    g_qkv = first[:, : 3 * part_cols].reshape(part_rows, 3, part_cols)
    g_out = first[:, 3 * part_cols :].reshape(n_head, -1, part_cols).transpose(1, 0, 2)
    g_out = g_out.reshape(out_weight.shape)
    layer_out = unpad(turned_back(layer_out))
    tokens_grad = unpad(turned_back(tokens_grad))

    sums = lax.dot_general(
        jnp.concatenate([sums_one, sums_two]),
        turn.astype(F32),
        (((1,), (1,)), ((), ())),
        precision=lax.Precision.HIGHEST,
        preferred_element_type=F32,
    )
    g_b = g_b[chunk_of].reshape(n_head, 3, n_dp, per).transpose(2, 0, 1, 3)
    g_bu = g_bu[chunk_of].reshape(n_head, n_dp, -1).transpose(1, 0, 2)
    sums = jnp.concatenate(
        [
            sums.reshape(6, devices, per).transpose(1, 0, 2).reshape(devices, 6 * per),
            g_b[:, :, ::2].reshape(devices, 2 * per),
            g_bu.reshape(devices, -1),
        ],
        axis=1,
    )
    sums = jnp.sum(exchange(sums), axis=0)

    def part(index):
        return sums[index * per : (index + 1) * per]

    return (
        layer_out,
        tokens_grad,
        part(0),
        part(1),
        g_qkv,
        sums[6 * per : 8 * per].reshape(2, per),
        g_out,
        part(2),
        part(3),
        part(4),
        g_up,
        sums[8 * per :],
        g_down_t.T,
        part(5),
    )


def solution(mesh):
    n_dp, n_head = mesh.shape["dp"], mesh.shape["head"]

    def run(*args):
        return local(n_dp, n_head, *args)

    return jax.shard_map(
        run,
        mesh=mesh,
        in_specs=(
            P(ALL, None),
            P("dp"),
            P(ALL),
            P(ALL),
            P("dp", None, "head"),
            P(None, ("head", "dp")),
            P(ALL, None),
            P(ALL),
            P(ALL),
            P(ALL),
            P("dp", "head"),
            P(("head", "dp")),
            P("head", "dp"),
            P(ALL),
            P(ALL, None),
        ),
        out_specs=(
            P(ALL, None),
            P(ALL, None),
            P(ALL),
            P(ALL),
            P("dp", None, "head"),
            P(None, ("head", "dp")),
            P(ALL, None),
            P(ALL),
            P(ALL),
            P(ALL),
            P("dp", "head"),
            P(("head", "dp")),
            P("head", "dp"),
            P(ALL),
        ),
        check_vma=False,
    )
```

time: 751 us -> 288 us (0.38); the launches traced: 740 us -> 287 us
  waiting for transfers between devices: 439 us -> 105 us
  local copies, waits for them, and re-layouts: 123 us -> 35 us
  blocking collectives: 82.1 us -> 0 us
  Pallas kernels: 0 us -> 62.8 us
  matrix products: 60.1 us -> 10 us
  starting transfers between devices: 0.78 us -> 35.5 us
  other arithmetic: 20.1 us -> 36.7 us
  between operations: 15.2 us -> 1.46 us
    reduce_scatter x4 -> x0, waiting for transfers between devices: 292 us -> none  [scatter(): lax.psum_scatter(tiles.astype(BF16), ALL, scatter_dimension=0, tiled=True)]
    all_gather x4 -> x0, waiting for transfers between devices: 144 us -> none  [gather(): return lax.all_gather(piece, ALL, axis=0)]
    ppermute x0 -> x32, waiting for transfers between devices: none -> 93.3 us  [flip(): piece = lax.ppermute(piece, axis, [(i, i ^ bit) for i in range(count)])]
    unnamed x2 -> x0, blocking collectives: 82.1 us -> none
    pallas_call x0 -> x3, Pallas kernels: none -> 62.8 us  [call(): pl.pallas_call(body, grid=grid, in_specs=in_specs, out_specs=[o[1] for o...]
    convert_element_type x8 -> x5, local copies, waits for them, and re-layouts: 44.7 us -> 0.86 us  [the longest x3 0.77 us: local(): b_qv = b_qv.reshape(n_head, 2, n_dp * per).astype(F32)]
    dot_general x10 -> x1, matrix products: 33.2 us -> 1.02 us  [local(): lax.dot_general(jnp.concatenate([sums_one, sums_two]), turn.astype(F32),...]
    reshape x22 -> x21, local copies, waits for them, and re-layouts: 42.3 us -> 13 us  [the longest x1 3.47 us: local(): g_out = g_out.reshape(devices, -1, n_head, part_cols).transpose(0, 2, 1, 3)]
  transfers between devices with their start and end apart: 8 -> 34, of which waited for: 7 -> 20; matrix products, arithmetic and copies ran while one was open for 21% -> 22% of each run, Pallas kernels for 0% -> 12%
where the time goes in v2:
time: 288 us; the launch traced here: 287 us
  waiting for transfers between devices  105 us (36%)
  Pallas kernels  62.8 us (22%)
  other arithmetic  36.7 us (13%)
  starting transfers between devices  35.5 us (12%)
  local copies, waits for them, and re-layouts  35 us (12%)
  matrix products  10 us (3%)
    ppermute x32, waiting for transfers between devices, flip(): piece = lax.ppermute(piece, axis, [(i, i ^ bit) for i in range(count)])  93.3 us
    pallas_call x3, Pallas kernels, call(): pl.pallas_call(body, grid=grid, in_specs=in_specs, out_specs=[o[1] for o...  62.8 us
    ppermute x32, starting transfers between devices, flip(): piece = lax.ppermute(piece, axis, [(i, i ^ bit) for i in range(count)])  25.5 us
    convert_element_type x14, other arithmetic, add(): return (terms[0].astype(F32) + terms[1].astype(F32)).astype(BF16)  20.1 us
    all_to_all x2, waiting for transfers between devices, exchange(): return lax.all_to_all(blocks, ALL, 0, 0, tiled=True)  11.9 us
    all_to_all x2, starting transfers between devices, exchange(): return lax.all_to_all(blocks, ALL, 0, 0, tiled=True)  9.98 us
    another operation x11, other arithmetic, grow(): piece = jnp.stack([piece, other], axis=place_of(step, have))  7.71 us
    dot_general x4, matrix products, mm(): return jnp.dot(a, b, preferred_element_type=F32)  6.61 us
  transfers between devices with their start and end apart: 34, of which 20 were waited for; matrix products, arithmetic and copies ran while one was open for 22% of the time, Pallas kernels for 12%

profile of v2, /device:TPU:0, one launch (start us, length us, event | category | flops | bytes accessed | tf_op | source)
XLA Modules:
  0.0 286.6 jit_solution(6436290028891274522)
XLA Ops:
  0.6 1.1 copy.84
  3.0 4.1 %collective-permute-start = (bf16[96,768]{1,0:T(8,128)(2,1)S(1)}, bf16[96,768]{1,0:T(8,128)(2,1)S(1)}, u32[]{:S(2)}, u32[]{:S(2)}) collective-permute-start(bf16[96,768]{1,0:T(8,128)(2,1)S(1)} %pad_maximum_fusion.18), channel_id=1, source_target_pairs={{0,16},{4,20},{8,24},{12,28},{16,0},{20,4},{24,8},{28,12},{1,17},{... | collective-permute-start | bytes 442376 | tf_op jit(solution)/shard_map/ppermute | solution.py:355
  9.6 4.5 %collective-permute-done = bf16[96,768]{1,0:T(8,128)(2,1)S(1)} collective-permute-done((bf16[96,768]{1,0:T(8,128)(2,1)S(1)}, bf16[96,768]{1,0:T(8,128)(2,1)S(1)}, u32[]{:S(2)}, u32[]{:S(2)}) %collective-permute-start) | collective-permute-done | bytes 147488 | tf_op jit(solution)/shard_map/ppermute | solution.py:355
  17.0 5.6 %all-to-all-start = ((bf16[32,2,144]{2,1,0:T(2,128)(2,1)}), bf16[32,2,144]{2,1,0:T(2,128)(2,1)S(1)}, u32[]{:S(2)}, u32[]{:S(2)}) async-start(bf16[32,2,144]{2,1,0:T(2,128)(2,1)} %reshape.620), calls=%async_computation | async-start | bytes 65536 | tf_op jit(solution)/shard_map/all_to_all | solution.py:390
  22.6 1.4 convolution_convert_fusion.3.top
  24.1 1.5 convolution_convert_fusion.4.x
  25.5 4.3 %all-to-all-done = bf16[32,2,144]{2,1,0:T(2,128)(2,1)S(1)} async-done(((bf16[32,2,144]{2,1,0:T(2,128)(2,1)}), bf16[32,2,144]{2,1,0:T(2,128)(2,1)S(1)}, u32[]{:S(2)}, u32[]{:S(2)}) %all-to-all-start) | async-done | bytes 18464 | tf_op jit(solution)/shard_map/all_to_all | solution.py:390
  34.1 7.3 %collective-permute-done.3 = bf16[2,2,96,384]{3,2,1,0:T(8,128)(2,1)S(1)} collective-permute-done((bf16[2,2,96,384]{3,2,1,0:T(8,128)(2,1)S(1)}, bf16[2,2,96,384]{3,2,1,0:T(8,128)(2,1)S(1)}, u32[]{:S(2)}, u32[]{:S(2)}) %collective-permute-start.3) | collective-permute-done | bytes 294944 | tf_op jit(solution)/shard_map/ppermute | solution.py:355
  41.7 7.5 %collective-permute-done.4 = bf16[192,768]{1,0:T(8,128)(2,1)S(1)} collective-permute-done((bf16[192,768]{1,0:T(8,128)(2,1)S(1)}, bf16[192,768]{1,0:T(8,128)(2,1)S(1)}, u32[]{:S(2)}, u32[]{:S(2)}) %collective-permute-start.4) | collective-permute-done | bytes 294944 | tf_op jit(solution)/shard_map/ppermute | solution.py:355
  49.2 1.5 collective-permute-start.6
  50.7 1.1 collective-permute-start.5
  51.8 12.7 %collective-permute-done.6 = bf16[2,2,2,96,384]{4,3,2,1,0:T(8,128)(2,1)S(1)} collective-permute-done((bf16[2,2,2,96,384]{4,3,2,1,0:T(8,128)(2,1)S(1)}, bf16[2,2,2,96,384]{4,3,2,1,0:T(8,128)(2,1)S(1)}, u32[]{:S(2)}, u32[]{:S(2)}) %collective-permute-start.6) | collective-permute-done | bytes 589856 | tf_op jit(solution)/shard_map/ppermute | solution.py:355
  65.6 1.1 pad_maximum_fusion.7
  68.2 1.4 collective-permute-start.9
  70.7 1.6 fusion.6.vectors
  72.3 11.6 %shard_map.254 = (bf16[4,384,192]{2,1,0:T(8,128)(2,1)}, bf16[4,384,192]{2,1,0:T(8,128)(2,1)}, bf16[4,384,192]{2,1,0:T(8,128)(2,1)}, f32[4,6,192,192]{3,2,1,0:T(8,128)}, bf16[4,384,192]{2,1,0:T(8,128)(2,1)}) custom-call(s32[2]{0:T(128)} %dynamic_slice.3.lengths, s32[4]{0:T(128)} %fusion.44.order, bf16[384,768]{1,0:T(8,128)(2,1)} %convolution_convert_fusion.4.x, ...), custom_call_target="tpu_custom_call" | custom-call | flops 1811939328 | bytes 7077888 | tf_op jit(solution)/shard_map/pallas_call | solution.py:306
  83.9 3.3 %pad_maximum_fusion.5 = (bf16[2,2,2,96,768]{4,3,2,1,0:T(8,128)(2,1)}, bf16[2,2,2,96,768]{4,3,2,1,0:T(8,128)(2,1)}) fusion(bf16[1,2,2,96,768]{4,3,2,1,0:T(8,128)(2,1)} %bitcast.29, bf16[1,2,2,96,768]{4,3,2,1,0:T(8,128)(2,1)} %bitcast.28, bf16[1,2,2,96,768]{4,3,2,1,0:T(8,128)(2,1)} %bitcast.31, bf16[1,2,2,96,768]{4,3,2,1,0:T(8,128)(2,1)} %bitcast.30), kind=kLoop, calls=%fused_computation.29 | loop fusion | flops 1179648 | bytes 4718592 | tf_op jit(solution)/shard_map/stack | solution.py:523
  87.2 1.1 collective-permute-start.13
  88.3 1.1 collective-permute-start.12
  89.9 1.5 slice.355
  92.4 2.3 reshape.535
  94.7 1.9 gather_fusion
  96.6 2.1 convolution_convert_fusion.w_out
  98.7 16.2 %collective-permute-done.13 = bf16[2,2,2,96,768]{4,3,2,1,0:T(8,128)(2,1)} collective-permute-done((bf16[2,2,2,96,768]{4,3,2,1,0:T(8,128)(2,1)}, bf16[2,2,2,96,768]{4,3,2,1,0:T(8,128)(2,1)}, u32[]{:S(2)}, u32[]{:S(2)}) %collective-permute-start.13) | collective-permute-done | bytes 1179680 | tf_op jit(solution)/shard_map/ppermute | solution.py:355
  114.9 1.8 pad_maximum_fusion.1
  116.9 4.1 %pad_maximum_fusion.up_near = bf16[2,768,768]{2,1,0:T(8,128)(2,1)} fusion(bf16[1,768,768]{2,1,0:T(8,128)(2,1)} %bitcast.33, bf16[1,768,768]{2,1,0:T(8,128)(2,1)} %bitcast.32), kind=kLoop, calls=%fused_computation.5 | loop fusion | flops 1179648 | bytes 4718592 | tf_op jit(solution)/shard_map/stack | solution.py:366
  122.8 3.2 %collective-permute-done.14.up_far = bf16[2,768,768]{2,1,0:T(8,128)(2,1)} collective-permute-done((bf16[2,768,768]{2,1,0:T(8,128)(2,1)}, bf16[2,768,768]{2,1,0:T(8,128)(2,1)}, u32[]{:S(2)}, u32[]{:S(2)}) %collective-permute-start.14) | collective-permute-done | bytes 2359328 | tf_op jit(solution)/shard_map/ppermute | solution.py:355
  126.0 3.4 %collective-permute-done.15.down_far = bf16[2,768,768]{2,1,0:T(8,128)(2,1)} collective-permute-done((bf16[2,768,768]{2,1,0:T(8,128)(2,1)S(1)}, bf16[2,768,768]{2,1,0:T(8,128)(2,1)}, u32[]{:S(2)}, u32[]{:S(2)}) %collective-permute-start.15) | collective-permute-done | bytes 2359328 | tf_op jit(solution)/shard_map/ppermute | solution.py:355
  129.3 28.9 %shard_map.255 = (bf16[384,768]{1,0:T(8,128)(2,1)}, f32[384,768]{1,0:T(8,128)}, bf16[4,384,192]{2,1,0:T(8,128)(2,1)}, bf16[768,768]{1,0:T(8,128)(2,1)}, bf16[2,7...) custom-call(s32[4]{0:T(128)} %fusion.44.order, ...), custom_call_target="tpu_custom_call" | custom-call | flops 10871635968 | bytes 9437184 | tf_op jit(solution)/shard_map/pallas_call | solution.py:306
  158.8 1.8 fusion.67
  160.6 2.5 collective-permute-done.17
  163.1 1.8 fusion
  164.8 1.1 collective-permute-start.19
  166.4 2.1 add_convert_fusion
  168.6 1.1 collective-permute-start.18
  169.8 1.7 gather_fusion.2
  171.5 3.5 %reshape.540 = bf16[32,24,4,192]{3,2,1,0:T(4,128)(2,1)S(1)} reshape(bf16[32,24,768]{2,1,0:T(8,128)(2,1)} %gather_fusion.2) | data formatting | bytes 2359296 | tf_op jit(solution)/shard_map/reshape | solution.py:624
  175.0 1.5 copy.95
  176.5 22.4 %shard_map.256 = (bf16[384,768]{1,0:T(8,128)(2,1)}, bf16[2,768,384]{2,1,0:T(8,128)(2,1)}, bf16[2,768,384]{2,1,0:T(8,128)(2,1)}, bf16[2,768,384]{2,1,0:T(8,128)(2...) custom-call(bf16[384,768]{1,0:T(8,128)(2,1)} %convolution_convert_fusion.4.x, ...), custom_call_target="tpu_custom_call" | custom-call | flops 3623878656 | bytes 7077888 | tf_op jit(solution)/shard_map/pallas_call | solution.py:306
  199.4 2.3 fusion.14
  201.8 1.0 collective-permute-start.21
  202.8 2.3 fusion.8
  205.1 1.1 collective-permute-start.20
  207.5 9.8 %collective-permute-done.21 = bf16[2,2,96,768]{3,2,1,0:T(8,128)(2,1)S(1)} collective-permute-done((bf16[2,2,96,768]{3,2,1,0:T(8,128)(2,1)}, bf16[2,2,96,768]{3,2,1,0:T(8,128)(2,1)S(1)}, u32[]{:S(2)}, u32[]{:S(2)}) %collective-permute-start.21) | collective-permute-done | bytes 589856 | tf_op jit(solution)/shard_map/ppermute | solution.py:355
  217.3 3.0 %collective-permute-done.20 = bf16[2,2,96,768]{3,2,1,0:T(8,128)(2,1)S(1)} collective-permute-done((bf16[2,2,96,768]{3,2,1,0:T(8,128)(2,1)}, bf16[2,2,96,768]{3,2,1,0:T(8,128)(2,1)S(1)}, u32[]{:S(2)}, u32[]{:S(2)}) %collective-permute-start.20) | collective-permute-done | bytes 589856 | tf_op jit(solution)/shard_map/ppermute | solution.py:355
  220.4 3.0 %fusion.12 = (bf16[2,2,2,96,384]{4,3,2,1,0:T(8,128)(2,1)}, bf16[2,2,2,96,384]{4,3,2,1,0:T(8,128)(2,1)S(1)}) fusion(bf16[2,2,2,2,96,384]{5,4,3,2,1,0:T(8,128)(2,1)} %bitcast.205, bf16[2,2,2,2,96,384]{5,4,3,2,1,0:T(8,128)(2,1)} %collective-permute-done.23), kind=kLoop, calls=%fused_computation.48 | loop fusion | flops 2359296 | bytes 3538944 | tf_op jit(solution)/shard_map/convert_element_type | solution.py:372
  223.3 1.1 collective-permute-start.26
  224.4 2.3 fusion.10
  230.9 0.9 reshape.538
  231.8 1.0 fusion.33
  234.8 3.0 %collective-permute-done.26 = bf16[2,2,2,96,384]{4,3,2,1,0:T(8,128)(2,1)} collective-permute-done((bf16[2,2,2,96,384]{4,3,2,1,0:T(8,128)(2,1)}, bf16[2,2,2,96,384]{4,3,2,1,0:T(8,128)(2,1)}, u32[]{:S(2)}, u32[]{:S(2)}) %collective-permute-start.26) | collective-permute-done | bytes 589856 | tf_op jit(solution)/shard_map/ppermute | solution.py:355
  237.8 3.2 %collective-permute-done.25 = bf16[2,2,2,96,384]{4,3,2,1,0:T(8,128)(2,1)} collective-permute-done((bf16[2,2,2,96,384]{4,3,2,1,0:T(8,128)(2,1)}, bf16[2,2,2,96,384]{4,3,2,1,0:T(8,128)(2,1)}, u32[]{:S(2)}, u32[]{:S(2)}) %collective-permute-start.25) | collective-permute-done | bytes 589856 | tf_op jit(solution)/shard_map/ppermute | solution.py:355
  241.0 2.5 collective-permute-done.24
  243.5 1.2 fusion.25
  244.7 1.2 collective-permute-start.29
  245.9 1.9 fusion.23
  247.8 0.9 collective-permute-start.28
  248.7 1.9 fusion.21
  251.4 4.4 %all-to-all-start.1 = ((f32[32,1,288]{2,1,0:T(1,128)}), f32[32,1,288]{2,1,0:T(1,128)}, u32[]{:S(2)}, u32[]{:S(2)}) async-start(f32[32,1,288]{2,1,0:T(1,128)} %all_to_all.11), calls=%async_computation.1 | async-start | bytes 98304 | tf_op jit(solution)/shard_map/all_to_all | solution.py:390
  255.7 1.7 convolution_convert_fusion.1
  258.4 7.5 %all-to-all-done.1 = f32[32,1,288]{2,1,0:T(1,128)} async-done(((f32[32,1,288]{2,1,0:T(1,128)}), f32[32,1,288]{2,1,0:T(1,128)}, u32[]{:S(2)}, u32[]{:S(2)}) %all-to-all-start.1) | async-done | bytes 36896 | tf_op jit(solution)/shard_map/all_to_all | solution.py:390
  269.6 1.0 convert_add_fusion.4
  270.6 5.2 %collective-permute-done.30 = bf16[2,96,768]{2,1,0:T(8,128)(2,1)S(1)} collective-permute-done((bf16[2,96,768]{2,1,0:T(8,128)(2,1)S(1)}, bf16[2,96,768]{2,1,0:T(8,128)(2,1)S(1)}, u32[]{:S(2)}, u32[]{:S(2)}) %collective-permute-start.30) | collective-permute-done | bytes 294944 | tf_op jit(solution)/shard_map/ppermute | solution.py:355
  276.7 7.9 %collective-permute-done.31 = bf16[96,768]{1,0:T(8,128)(2,1)S(1)} collective-permute-done((bf16[96,768]{1,0:T(8,128)(2,1)S(1)}, bf16[96,768]{1,0:T(8,128)(2,1)S(1)}, u32[]{:S(2)}, u32[]{:S(2)}) %collective-permute-start.31) | collective-permute-done | bytes 147488 | tf_op jit(solution)/shard_map/ppermute | solution.py:355
  (214 shorter events, 35.3 us)
Async XLA Ops:
  1.7 6.1 %copy-start.25 = (bf16[2,24]{1,0:T(2,128)(2,1)S(1)}, bf16[2,24]{1,0:T(2,128)(2,1)}, u32[]{:S(2)}) copy-start(bf16[2,24]{1,0:T(2,128)(2,1)} %param.20) | copy-start | bytes 292
  1.7 6.1 %copy-start.27 = (bf16[96]{0:T(256)(128)(2,1)S(1)}, bf16[96]{0:T(256)(128)(2,1)}, u32[]{:S(2)}) copy-start(bf16[96]{0:T(256)(128)(2,1)} %param.26) | copy-start | bytes 580
  1.7 6.1 %copy-start.28 = (bf16[24]{0:T(256)(128)(2,1)S(1)}, bf16[24]{0:T(256)(128)(2,1)}, u32[]{:S(2)}) copy-start(bf16[24]{0:T(256)(128)(2,1)} %param.28) | copy-start | bytes 148
  1.7 6.1 %copy-start.29 = (bf16[24]{0:T(256)(128)(2,1)S(1)}, bf16[24]{0:T(256)(128)(2,1)}, u32[]{:S(2)}) copy-start(bf16[24]{0:T(256)(128)(2,1)} %param.24) | copy-start | bytes 148
  1.8 6.1 %copy-start.30 = (bf16[24]{0:T(256)(128)(2,1)S(1)}, bf16[24]{0:T(256)(128)(2,1)}, u32[]{:S(2)}) copy-start(bf16[24]{0:T(256)(128)(2,1)} %param.23) | copy-start | bytes 148
  1.8 6.1 %copy-start.31 = (bf16[24]{0:T(256)(128)(2,1)S(1)}, bf16[24]{0:T(256)(128)(2,1)}, u32[]{:S(2)}) copy-start(bf16[24]{0:T(256)(128)(2,1)} %param.22) | copy-start | bytes 148
  1.8 6.1 %copy-start.32 = (bf16[24]{0:T(256)(128)(2,1)S(1)}, bf16[24]{0:T(256)(128)(2,1)}, u32[]{:S(2)}) copy-start(bf16[24]{0:T(256)(128)(2,1)} %param.18) | copy-start | bytes 148
  1.8 6.1 %copy-start.33 = (bf16[24]{0:T(256)(128)(2,1)S(1)}, bf16[24]{0:T(256)(128)(2,1)}, u32[]{:S(2)}) copy-start(bf16[24]{0:T(256)(128)(2,1)} %param.17) | copy-start | bytes 148
  1.8 6.2 %copy-start.15 = (bf16[370,768]{1,0:T(8,128)(2,1)S(1)}, bf16[370,768]{1,0:T(8,128)(2,1)}, u32[]{:S(2)}) copy-start(bf16[370,768]{1,0:T(8,128)(2,1)} %param.29) | copy-start | bytes 1704964
  3.0 11.1 %collective-permute-start = (bf16[96,768]{1,0:T(8,128)(2,1)S(1)}, bf16[96,768]{1,0:T(8,128)(2,1)S(1)}, u32[]{:S(2)}, u32[]{:S(2)}) collective-permute-start(bf16[96,768]{1,0:T(8,128)(2,1)S(1)} %pad_maximum_fusion.18), channel_id=1, source_target_pairs={{0,16},{4,20},{8,24},{12,28},{16,0},{20,4},{24,8},{28,12},{1,17},{... | collective-permute-start | bytes 442376 | tf_op jit(solution)/shard_map/ppermute | solution.py:355
  7.8 88.7 %copy-start = (bf16[768,768]{1,0:T(8,128)(2,1)}, bf16[768,768]{1,0:T(8,128)(2,1)S(1)}, u32[]{:S(2)}) copy-start(bf16[768,768]{1,0:T(8,128)(2,1)S(1)} %fusion.2.turn) | copy-start | bytes 3538948
  14.2 17.9 %collective-permute-start.1 = (bf16[2,96,768]{2,1,0:T(8,128)(2,1)S(1)}, bf16[2,96,768]{2,1,0:T(8,128)(2,1)S(1)}, u32[]{:S(2)}, u32[]{:S(2)}) collective-permute-start(bf16[2,96,768]{2,1,0:T(8,128)(2,1)S(1)} %pad_maximum_fusion.14), channel_id=1, source_target_pairs={{0,8},{4,12},{8,0},{12,4},{16,24},{20,28},{24,16},{28,20},{1,9},{5... | collective-permute-start | bytes 884744 | tf_op jit(solution)/shard_map/ppermute | solution.py:355
  17.0 12.9 %all-to-all-start = ((bf16[32,2,144]{2,1,0:T(2,128)(2,1)}), bf16[32,2,144]{2,1,0:T(2,128)(2,1)S(1)}, u32[]{:S(2)}, u32[]{:S(2)}) async-start(bf16[32,2,144]{2,1,0:T(2,128)(2,1)} %reshape.620), calls=%async_computation | async-start | bytes 65536 | tf_op jit(solution)/shard_map/all_to_all | solution.py:390
  32.3 9.1 %collective-permute-start.3 = (bf16[2,2,96,384]{3,2,1,0:T(8,128)(2,1)S(1)}, bf16[2,2,96,384]{3,2,1,0:T(8,128)(2,1)S(1)}, u32[]{:S(2)}, u32[]{:S(2)}) collective-permute-start(bf16[2,2,96,384]{3,2,1,0:T(8,128)(2,1)S(1)} %get-tuple-element.256), channel_id=1, source_target_pairs={{0,2},{1,3},{2,0},{3,1},{4,6},{5,7},{6,4},{7,5},{8,10},{9,11},{10,... | collective-permute-start | bytes 884744 | tf_op jit(solution)/shard_map/ppermute | solution.py:355
  32.9 8.7 %collective-permute-start.2 = (bf16[2,2,96,384]{3,2,1,0:T(8,128)(2,1)S(1)}, bf16[2,2,96,384]{3,2,1,0:T(8,128)(2,1)S(1)}, u32[]{:S(2)}, u32[]{:S(2)}) collective-permute-start(bf16[2,2,96,384]{3,2,1,0:T(8,128)(2,1)S(1)} %get-tuple-element.257), channel_id=1, source_target_pairs={{0,4},{4,0},{8,12},{12,8},{16,20},{20,16},{24,28},{28,24},{1,5},{5... | collective-permute-start | bytes 884744 | tf_op jit(solution)/shard_map/ppermute | solution.py:355
  33.6 15.6 %collective-permute-start.4 = (bf16[192,768]{1,0:T(8,128)(2,1)S(1)}, bf16[192,768]{1,0:T(8,128)(2,1)S(1)}, u32[]{:S(2)}, u32[]{:S(2)}) collective-permute-start(bf16[192,768]{1,0:T(8,128)(2,1)S(1)} %pad_maximum_fusion.15), channel_id=1, source_target_pairs={{0,16},{4,20},{8,24},{12,28},{16,0},{20,4},{24,8},{28,12},{1,17},{... | collective-permute-start | bytes 884744 | tf_op jit(solution)/shard_map/ppermute | solution.py:355
  49.2 15.3 %collective-permute-start.6 = (bf16[2,2,2,96,384]{4,3,2,1,0:T(8,128)(2,1)S(1)}, bf16[2,2,2,96,384]{4,3,2,1,0:T(8,128)(2,1)S(1)}, u32[]{:S(2)}, u32[]{:S(2)}) collective-permute-start(bf16[2,2,2,96,384]{4,3,2,1,0:T(8,128)(2,1)S(1)} %pad_maximum_fusion.10), channel_id=1, source_target_pairs={{0,4},{4,0},{8,12},{12,8},{16,20},{20,16},{24,28},{28,24},{1,5},{5... | collective-permute-start | bytes 1769480 | tf_op jit(solution)/shard_map/ppermute | solution.py:355
  50.7 14.9 %collective-permute-start.7 = (bf16[2,192,768]{2,1,0:T(8,128)(2,1)S(1)}, bf16[2,192,768]{2,1,0:T(8,128)(2,1)S(1)}, u32[]{:S(2)}, u32[]{:S(2)}) collective-permute-start(bf16[2,192,768]{2,1,0:T(8,128)(2,1)S(1)} %pad_maximum_fusion.11), channel_id=1, source_target_pairs={{0,8},{4,12},{8,0},{12,4},{16,24},{20,28},{24,16},{28,20},{1,9},{5... | collective-permute-start | bytes 1769480 | tf_op jit(solution)/shard_map/ppermute | solution.py:355
  50.7 16.0 %collective-permute-start.5 = (bf16[2,2,2,96,384]{4,3,2,1,0:T(8,128)(2,1)S(1)}, bf16[2,2,2,96,384]{4,3,2,1,0:T(8,128)(2,1)S(1)}, u32[]{:S(2)}, u32[]{:S(2)}) collective-permute-start(bf16[2,2,2,96,384]{4,3,2,1,0:T(8,128)(2,1)S(1)} %pad_maximum_fusion.9), channel_id=1, source_target_pairs={{0,2},{1,3},{2,0},{3,1},{4,6},{5,7},{6,4},{7,5},{8,10},{9,11},{10,... | collective-permute-start | bytes 1769480 | tf_op jit(solution)/shard_map/ppermute | solution.py:355
  64.8 2.1 copy-start.2
  66.7 2.8 copy-start.34
  66.9 5.4 %copy-start.4 = (bf16[2,768,384]{2,1,0:T(8,128)(2,1)}, bf16[2,768,384]{2,1,0:T(8,128)(2,1)S(1)}, u32[]{:S(2)}) copy-start(bf16[2,768,384]{2,1,0:T(8,128)(2,1)S(1)} %pad_maximum_fusion.3.qk_near) | copy-start | bytes 3538948
  66.9 5.3 %collective-permute-start.11 = (bf16[2,768,384]{2,1,0:T(8,128)(2,1)S(1)}, bf16[2,768,384]{2,1,0:T(8,128)(2,1)}, u32[]{:S(2)}, u32[]{:S(2)}) collective-permute-start(bf16[2,768,384]{2,1,0:T(8,128)(2,1)S(1)} %bitcast.188), channel_id=1, source_target_pairs={{0,1},{1,0},{2,3},{3,2},{4,5},{5,4},{6,7},{7,6},{8,9},{9,8},{10,11... | collective-permute-start | bytes 3538952 | tf_op jit(solution)/shard_map/ppermute | solution.py:355
  67.0 5.3 %collective-permute-start.10 = (bf16[2,768,384]{2,1,0:T(8,128)(2,1)S(1)}, bf16[2,768,384]{2,1,0:T(8,128)(2,1)}, u32[]{:S(2)}, u32[]{:S(2)}) collective-permute-start(bf16[2,768,384]{2,1,0:T(8,128)(2,1)S(1)} %pad_maximum_fusion.3.qk_near), channel_id=1, source_target_pairs={{0,1},{1,0},{2,3},{3,2},{4,5},{5,4},{6,7},{7,6},{8,9},{9,8},{10,11... | collective-permute-start | bytes 3538952 | tf_op jit(solution)/shard_map/ppermute | solution.py:355
  67.5 16.4 %collective-permute-start.8 = (bf16[2,2,96,768]{3,2,1,0:T(8,128)(2,1)}, bf16[2,2,96,768]{3,2,1,0:T(8,128)(2,1)}, u32[]{:S(2)}, u32[]{:S(2)}) collective-permute-start(bf16[2,2,96,768]{3,2,1,0:T(8,128)(2,1)} %get-tuple-element.107), channel_id=1, source_target_pairs={{0,4},{4,0},{8,12},{12,8},{16,20},{20,16},{24,28},{28,24},{1,5},{5... | collective-permute-start | bytes 1769480 | tf_op jit(solution)/shard_map/ppermute | solution.py:355
  68.2 15.7 %collective-permute-start.9 = (bf16[2,2,96,768]{3,2,1,0:T(8,128)(2,1)}, bf16[2,2,96,768]{3,2,1,0:T(8,128)(2,1)}, u32[]{:S(2)}, u32[]{:S(2)}) collective-permute-start(bf16[2,2,96,768]{3,2,1,0:T(8,128)(2,1)} %get-tuple-element.109), channel_id=1, source_target_pairs={{0,2},{1,3},{2,0},{3,1},{4,6},{5,7},{6,4},{7,5},{8,10},{9,11},{10,... | collective-permute-start | bytes 1769480 | tf_op jit(solution)/shard_map/ppermute | solution.py:355
  83.9 5.7 %copy-start.3 = (bf16[2,2,2,2,96,384]{5,4,3,2,1,0:T(8,128)(2,1)S(1)}, bf16[2,2,2,2,96,384]{5,4,3,2,1,0:T(8,128)(2,1)}, u32[]{:S(2)}) copy-start(bf16[2,2,2,2,96,384]{5,4,3,2,1,0:T(8,128)(2,1)} %copy-done.2) | copy-start | bytes 3538948
  87.2 27.7 %collective-permute-start.13 = (bf16[2,2,2,96,768]{4,3,2,1,0:T(8,128)(2,1)}, bf16[2,2,2,96,768]{4,3,2,1,0:T(8,128)(2,1)}, u32[]{:S(2)}, u32[]{:S(2)}) collective-permute-start(bf16[2,2,2,96,768]{4,3,2,1,0:T(8,128)(2,1)} %get-tuple-element.112), channel_id=1, source_target_pairs={{0,4},{4,0},{8,12},{12,8},{16,20},{20,16},{24,28},{28,24},{1,5},{5... | collective-permute-start | bytes 3538952 | tf_op jit(solution)/shard_map/ppermute | solution.py:355
  88.3 28.7 %collective-permute-start.12 = (bf16[2,2,2,96,768]{4,3,2,1,0:T(8,128)(2,1)}, bf16[2,2,2,96,768]{4,3,2,1,0:T(8,128)(2,1)}, u32[]{:S(2)}, u32[]{:S(2)}) collective-permute-start(bf16[2,2,2,96,768]{4,3,2,1,0:T(8,128)(2,1)} %get-tuple-element.111), channel_id=1, source_target_pairs={{0,2},{1,3},{2,0},{3,1},{4,6},{5,7},{6,4},{7,5},{8,10},{9,11},{10,... | collective-permute-start | bytes 3538952 | tf_op jit(solution)/shard_map/ppermute | solution.py:355
  116.9 4.2 %copy-start.7 = (bf16[2,2,2,2,96,768]{5,4,3,2,1,0:T(8,128)(2,1)}, bf16[2,2,2,2,96,768]{5,4,3,2,1,0:T(8,128)(2,1)S(1)}, u32[]{:S(2)}) copy-start(bf16[2,2,2,2,96,768]{5,4,3,2,1,0:T(8,128)(2,1)S(1)} %copy.93) | copy-start | bytes 7077892
  121.1 4.9 %collective-permute-start.14 = (bf16[2,768,768]{2,1,0:T(8,128)(2,1)}, bf16[2,768,768]{2,1,0:T(8,128)(2,1)}, u32[]{:S(2)}, u32[]{:S(2)}) collective-permute-start(bf16[2,768,768]{2,1,0:T(8,128)(2,1)} %pad_maximum_fusion.up_near), channel_id=1, source_target_pairs={{0,1},{1,0},{2,3},{3,2},{4,5},{5,4},{6,7},{7,6},{8,9},{9,8},{10,11... | collective-permute-start | bytes 7077896 | tf_op jit(solution)/shard_map/ppermute | solution.py:355
  121.1 8.2 %collective-permute-start.15 = (bf16[2,768,768]{2,1,0:T(8,128)(2,1)S(1)}, bf16[2,768,768]{2,1,0:T(8,128)(2,1)}, u32[]{:S(2)}, u32[]{:S(2)}) collective-permute-start(bf16[2,768,768]{2,1,0:T(8,128)(2,1)S(1)} %bitcast.199), channel_id=1, source_target_pairs={{0,1},{1,0},{2,3},{3,2},{4,5},{5,4},{6,7},{7,6},{8,9},{9,8},{10,11... | collective-permute-start | bytes 7077896 | tf_op jit(solution)/shard_map/ppermute | solution.py:355
  158.2 4.8 %collective-permute-start.17 = (bf16[2,2,2,2,96,768]{5,4,3,2,1,0:T(8,128)(2,1)}, bf16[2,2,2,2,96,768]{5,4,3,2,1,0:T(8,128)(2,1)S(1)}, u32[]{:S(2)}, u32[]{:S(2)}) collective-permute-start(bf16[2,2,2,2,96,768]{5,4,3,2,1,0:T(8,128)(2,1)} %bitcast.238), channel_id=1, source_target_pairs={{0,1},{1,0},{2,3},{3,2},{4,5},{5,4},{6,7},{7,6},{8,9},{9,8},{10,11... | collective-permute-start | bytes 7077896 | tf_op jit(solution)/shard_map/ppermute | solution.py:355
  158.4 8.0 %collective-permute-start.16 = (bf16[2,2,2,2,96,768]{5,4,3,2,1,0:T(8,128)(2,1)}, bf16[2,2,2,2,96,768]{5,4,3,2,1,0:T(8,128)(2,1)S(1)}, u32[]{:S(2)}, u32[]{:S(2)}) collective-permute-start(bf16[2,2,2,2,96,768]{5,4,3,2,1,0:T(8,128)(2,1)} %bitcast.237), channel_id=1, source_target_pairs={{0,1},{1,0},{2,3},{3,2},{4,5},{5,4},{6,7},{7,6},{8,9},{9,8},{10,11... | collective-permute-start | bytes 7077896 | tf_op jit(solution)/shard_map/ppermute | solution.py:355
  163.1 3.4 %copy-start.6 = (bf16[2,768,768]{2,1,0:T(8,128)(2,1)S(1)}, bf16[2,768,768]{2,1,0:T(8,128)(2,1)}, u32[]{:S(2)}) copy-start(bf16[2,768,768]{2,1,0:T(8,128)(2,1)} %get-tuple-element.125) | copy-start | bytes 7077892
  164.8 34.0 %collective-permute-start.19 = (bf16[2,2,2,96,768]{4,3,2,1,0:T(8,128)(2,1)}, bf16[2,2,2,96,768]{4,3,2,1,0:T(8,128)(2,1)}, u32[]{:S(2)}, u32[]{:S(2)}) collective-permute-start(bf16[2,2,2,96,768]{4,3,2,1,0:T(8,128)(2,1)} %get-tuple-element.233), channel_id=1, source_target_pairs={{0,2},{1,3},{2,0},{3,1},{4,6},{5,7},{6,4},{7,5},{8,10},{9,11},{10,... | collective-permute-start | bytes 3538952 | tf_op jit(solution)/shard_map/ppermute | solution.py:355
  166.4 3.2 %copy-start.26 = (s32[4]{0:T(128)S(1)}, s32[4]{0:T(128)}, u32[]{:S(2)}) copy-start(s32[4]{0:T(128)} %fusion.44.order) | copy-start | bytes 52
  166.4 3.4 %copy-start.9 = (bf16[768,768]{1,0:T(8,128)(2,1)S(1)}, bf16[768,768]{1,0:T(8,128)(2,1)}, u32[]{:S(2)}) copy-start(bf16[768,768]{1,0:T(8,128)(2,1)} %get-tuple-element.119) | copy-start | bytes 3538948
  168.6 30.3 %collective-permute-start.18 = (bf16[2,2,2,96,768]{4,3,2,1,0:T(8,128)(2,1)}, bf16[2,2,2,96,768]{4,3,2,1,0:T(8,128)(2,1)}, u32[]{:S(2)}, u32[]{:S(2)}) collective-permute-start(bf16[2,2,2,96,768]{4,3,2,1,0:T(8,128)(2,1)} %get-tuple-element.223), channel_id=1, source_target_pairs={{0,4},{4,0},{8,12},{12,8},{16,20},{20,16},{24,28},{28,24},{1,5},{5... | collective-permute-start | bytes 3538952 | tf_op jit(solution)/shard_map/ppermute | solution.py:355
  176.5 23.0 %copy-start.5 = (bf16[2,1,2,2,96,768]{5,4,3,2,1,0:T(8,128)(2,1)S(1)}, bf16[2,1,2,2,96,768]{5,4,3,2,1,0:T(8,128)(2,1)}, u32[]{:S(2)}) copy-start(bf16[2,1,2,2,96,768]{5,4,3,2,1,0:T(8,128)(2,1)} %get-tuple-element.222) | copy-start | bytes 3538948
  198.9 21.5 %collective-permute-start.22 = (bf16[2,2,2,2,96,384]{5,4,3,2,1,0:T(8,128)(2,1)}, bf16[2,2,2,2,96,384]{5,4,3,2,1,0:T(8,128)(2,1)}, u32[]{:S(2)}, u32[]{:S(2)}) collective-permute-start(bf16[2,2,2,2,96,384]{5,4,3,2,1,0:T(8,128)(2,1)} %bitcast.240), channel_id=1, source_target_pairs={{0,1},{1,0},{2,3},{3,2},{4,5},{5,4},{6,7},{7,6},{8,9},{9,8},{10,11... | collective-permute-start | bytes 3538952 | tf_op jit(solution)/shard_map/ppermute | solution.py:355
  198.9 21.4 %collective-permute-start.23 = (bf16[2,2,2,2,96,384]{5,4,3,2,1,0:T(8,128)(2,1)}, bf16[2,2,2,2,96,384]{5,4,3,2,1,0:T(8,128)(2,1)}, u32[]{:S(2)}, u32[]{:S(2)}) collective-permute-start(bf16[2,2,2,2,96,384]{5,4,3,2,1,0:T(8,128)(2,1)} %bitcast.239), channel_id=1, source_target_pairs={{0,1},{1,0},{2,3},{3,2},{4,5},{5,4},{6,7},{7,6},{8,9},{9,8},{10,11... | collective-permute-start | bytes 3538952 | tf_op jit(solution)/shard_map/ppermute | solution.py:355
  201.8 15.5 %collective-permute-start.21 = (bf16[2,2,96,768]{3,2,1,0:T(8,128)(2,1)}, bf16[2,2,96,768]{3,2,1,0:T(8,128)(2,1)S(1)}, u32[]{:S(2)}, u32[]{:S(2)}) collective-permute-start(bf16[2,2,96,768]{3,2,1,0:T(8,128)(2,1)} %get-tuple-element.228), channel_id=1, source_target_pairs={{0,2},{1,3},{2,0},{3,1},{4,6},{5,7},{6,4},{7,5},{8,10},{9,11},{10,... | collective-permute-start | bytes 1769480 | tf_op jit(solution)/shard_map/ppermute | solution.py:355
  202.8 3.4 %copy-start.22 = (f32[4,1,768]{2,1,0:T(1,128)S(1)}, f32[4,1,768]{2,1,0:T(1,128)}, u32[]{:S(2)}) copy-start(f32[4,1,768]{2,1,0:T(1,128)} %get-tuple-element.135) | copy-start | bytes 36868
  205.1 15.2 %collective-permute-start.20 = (bf16[2,2,96,768]{3,2,1,0:T(8,128)(2,1)}, bf16[2,2,96,768]{3,2,1,0:T(8,128)(2,1)S(1)}, u32[]{:S(2)}, u32[]{:S(2)}) collective-permute-start(bf16[2,2,96,768]{3,2,1,0:T(8,128)(2,1)} %get-tuple-element.230), channel_id=1, source_target_pairs={{0,4},{4,0},{8,12},{12,8},{16,20},{20,16},{24,28},{28,24},{1,5},{5... | collective-permute-start | bytes 1769480 | tf_op jit(solution)/shard_map/ppermute | solution.py:355
  217.3 3.0 %copy-start.11 = (bf16[2,2,96,768]{3,2,1,0:T(8,128)(2,1)}, bf16[2,2,96,768]{3,2,1,0:T(8,128)(2,1)S(1)}, u32[]{:S(2)}) copy-start(bf16[2,2,96,768]{3,2,1,0:T(8,128)(2,1)S(1)} %collective-permute-done.21) | copy-start | bytes 1769476
  220.3 3.0 %copy-start.13 = (bf16[2,2,96,768]{3,2,1,0:T(8,128)(2,1)}, bf16[2,2,96,768]{3,2,1,0:T(8,128)(2,1)S(1)}, u32[]{:S(2)}) copy-start(bf16[2,2,96,768]{3,2,1,0:T(8,128)(2,1)S(1)} %collective-permute-done.20) | copy-start | bytes 1769476
  220.4 4.1 %copy-start.8 = (bf16[2,768,384]{2,1,0:T(8,128)(2,1)S(1)}, bf16[2,768,384]{2,1,0:T(8,128)(2,1)}, u32[]{:S(2)}) copy-start(bf16[2,768,384]{2,1,0:T(8,128)(2,1)} %get-tuple-element.142) | copy-start | bytes 3538948
  223.3 4.4 %copy-start.14 = (bf16[2,2,96,768]{3,2,1,0:T(8,128)(2,1)S(1)}, bf16[2,2,96,768]{3,2,1,0:T(8,128)(2,1)}, u32[]{:S(2)}) copy-start(bf16[2,2,96,768]{3,2,1,0:T(8,128)(2,1)} %copy-done.13) | copy-start | bytes 1769476
  223.3 14.5 %collective-permute-start.26 = (bf16[2,2,2,96,384]{4,3,2,1,0:T(8,128)(2,1)}, bf16[2,2,2,96,384]{4,3,2,1,0:T(8,128)(2,1)}, u32[]{:S(2)}, u32[]{:S(2)}) collective-permute-start(bf16[2,2,2,96,384]{4,3,2,1,0:T(8,128)(2,1)} %get-tuple-element.224), channel_id=1, source_target_pairs={{0,4},{4,0},{8,12},{12,8},{16,20},{20,16},{24,28},{28,24},{1,5},{5... | collective-permute-start | bytes 1769480 | tf_op jit(solution)/shard_map/ppermute | solution.py:355
  226.8 1.8 copy-start.12
  226.8 14.2 %collective-permute-start.25 = (bf16[2,2,2,96,384]{4,3,2,1,0:T(8,128)(2,1)}, bf16[2,2,2,96,384]{4,3,2,1,0:T(8,128)(2,1)}, u32[]{:S(2)}, u32[]{:S(2)}) collective-permute-start(bf16[2,2,2,96,384]{4,3,2,1,0:T(8,128)(2,1)} %get-tuple-element.226), channel_id=1, source_target_pairs={{0,2},{1,3},{2,0},{3,1},{4,6},{5,7},{6,4},{7,5},{8,10},{9,11},{10,... | collective-permute-start | bytes 1769480 | tf_op jit(solution)/shard_map/ppermute | solution.py:355
  228.6 1.6 copy-start.35
  229.6 13.9 %collective-permute-start.24 = (bf16[2,192,768]{2,1,0:T(8,128)(2,1)}, bf16[2,192,768]{2,1,0:T(8,128)(2,1)}, u32[]{:S(2)}, u32[]{:S(2)}) collective-permute-start(bf16[2,192,768]{2,1,0:T(8,128)(2,1)} %pad_maximum_fusion.13), channel_id=1, source_target_pairs={{0,8},{4,12},{8,0},{12,4},{16,24},{20,28},{24,16},{28,20},{1,9},{5... | collective-permute-start | bytes 1769480 | tf_op jit(solution)/shard_map/ppermute | solution.py:355
  230.9 2.9 %copy-start.23 = (f32[4,1,576]{2,1,0:T(1,128)S(1)}, f32[4,1,576]{2,1,0:T(1,128)}, u32[]{:S(2)}) copy-start(f32[4,1,576]{2,1,0:T(1,128)} %get-tuple-element.134) | copy-start | bytes 27652
  231.8 3.0 %copy-start.10 = (bf16[2,96,768]{2,1,0:T(8,128)(2,1)S(1)}, bf16[2,96,768]{2,1,0:T(8,128)(2,1)}, u32[]{:S(2)}) copy-start(bf16[2,96,768]{2,1,0:T(8,128)(2,1)} %get-tuple-element.243) | copy-start | bytes 884740
  244.7 22.1 %collective-permute-start.29 = (bf16[2,2,96,384]{3,2,1,0:T(8,128)(2,1)S(1)}, bf16[2,2,96,384]{3,2,1,0:T(8,128)(2,1)S(1)}, u32[]{:S(2)}, u32[]{:S(2)}) collective-permute-start(bf16[2,2,96,384]{3,2,1,0:T(8,128)(2,1)S(1)} %get-tuple-element.236), channel_id=1, source_target_pairs={{0,2},{1,3},{2,0},{3,1},{4,6},{5,7},{6,4},{7,5},{8,10},{9,11},{10,... | collective-permute-start | bytes 884744 | tf_op jit(solution)/shard_map/ppermute | solution.py:355
  247.8 2.9 copy-start.19
  247.8 2.9 copy-start.20
  247.8 19.0 %collective-permute-start.28 = (bf16[2,2,96,384]{3,2,1,0:T(8,128)(2,1)}, bf16[2,2,96,384]{3,2,1,0:T(8,128)(2,1)S(1)}, u32[]{:S(2)}, u32[]{:S(2)}) collective-permute-start(bf16[2,2,96,384]{3,2,1,0:T(8,128)(2,1)} %get-tuple-element.238), channel_id=1, source_target_pairs={{0,4},{4,0},{8,12},{12,8},{16,20},{20,16},{24,28},{28,24},{1,5},{5... | collective-permute-start | bytes 884744 | tf_op jit(solution)/shard_map/ppermute | solution.py:355
  250.6 16.2 %collective-permute-start.27 = (bf16[192,768]{1,0:T(8,128)(2,1)}, bf16[192,768]{1,0:T(8,128)(2,1)}, u32[]{:S(2)}, u32[]{:S(2)}) collective-permute-start(bf16[192,768]{1,0:T(8,128)(2,1)} %get-tuple-element.240), channel_id=1, source_target_pairs={{0,16},{4,20},{8,24},{12,28},{16,0},{20,4},{24,8},{28,12},{1,17},{... | collective-permute-start | bytes 884744 | tf_op jit(solution)/shard_map/ppermute | solution.py:355
  251.4 14.5 %all-to-all-start.1 = ((f32[32,1,288]{2,1,0:T(1,128)}), f32[32,1,288]{2,1,0:T(1,128)}, u32[]{:S(2)}, u32[]{:S(2)}) async-start(f32[32,1,288]{2,1,0:T(1,128)} %all_to_all.11), calls=%async_computation.1 | async-start | bytes 98304 | tf_op jit(solution)/shard_map/all_to_all | solution.py:390
  267.0 8.8 %collective-permute-start.30 = (bf16[2,96,768]{2,1,0:T(8,128)(2,1)S(1)}, bf16[2,96,768]{2,1,0:T(8,128)(2,1)S(1)}, u32[]{:S(2)}, u32[]{:S(2)}) collective-permute-start(bf16[2,96,768]{2,1,0:T(8,128)(2,1)S(1)} %pad_maximum_fusion.16), channel_id=1, source_target_pairs={{0,8},{4,12},{8,0},{12,4},{16,24},{20,28},{24,16},{28,20},{1,9},{5... | collective-permute-start | bytes 884744 | tf_op jit(solution)/shard_map/ppermute | solution.py:355
  275.8 8.8 %collective-permute-start.31 = (bf16[96,768]{1,0:T(8,128)(2,1)S(1)}, bf16[96,768]{1,0:T(8,128)(2,1)S(1)}, u32[]{:S(2)}, u32[]{:S(2)}) collective-permute-start(bf16[96,768]{1,0:T(8,128)(2,1)S(1)} %fusion.31), channel_id=1, source_target_pairs={{0,16},{4,20},{8,24},{12,28},{16,0},{20,4},{24,8},{28,12},{1,17},{... | collective-permute-start | bytes 442376 | tf_op jit(solution)/shard_map/ppermute | solution.py:355
  (6 other events, 7.2 us)

commit v3 on v2

--- a/solution.py
+++ b/solution.py
@@ -73,6 +73,87 @@
 
 def column_sum(matrix):
     return jnp.sum(matrix.astype(F32), axis=0, keepdims=True)
+
+
+def counting(shape, axis):
+    return lax.broadcasted_iota(jnp.int32, shape, axis)
+
+
+def repeats(part, size):
+    return (counting((part, size), 1) % part == counting((part, size), 0)).astype(F32)
+
+
+def owners(devices, part, size):
+    return counting((devices, size), 1) // part, counting((devices, size), 0)
+
+
+def spread_vectors(per, order, smalls, turn, vectors, b_qv, b_up):
+    devices, width = smalls.shape[0], turn.shape[0]
+    chunks, _, part = b_up.shape
+    values = smalls[...].astype(F32)
+    plain = vectors.shape[0]
+    pattern = repeats(per, width).astype(BF16)
+    block, device = owners(devices, per, width)
+    rows = []
+    for v in range(plain):
+        row = mm(values[:, v * per : (v + 1) * per].astype(BF16), pattern)
+        rows.append(jnp.sum(jnp.where(block == device, row, 0.0), axis=0, keepdims=True))
+    vectors[...] = mm(jnp.concatenate(rows, axis=0).astype(BF16), turn[...])
+
+    def by_chunk(first, size, length, out):
+        tall = mm(
+            values[:, first : first + size].astype(BF16), repeats(size, length).astype(BF16)
+        )
+        block, device = owners(devices, size, length)
+        for t in range(chunks):
+            mine = device == block * chunks + order[t]
+            out(t, jnp.sum(jnp.where(mine, tall, 0.0), axis=0, keepdims=True))
+
+    def set_query(t, row):
+        b_qv[t, 0:1, :] = row
+
+    def set_value(t, row):
+        b_qv[t, 1:2, :] = row
+
+    def set_up(t, row):
+        b_up[t] = row
+
+    cols = b_qv.shape[2]
+    by_chunk(plain * per, per, cols, set_query)
+    by_chunk((plain + 1) * per, per, cols, set_value)
+    by_chunk((plain + 2) * per, values.shape[1] - (plain + 2) * per, part, set_up)
+
+
+def collect_vectors(per, order, sums_one, sums_two, g_b, g_bu, turn, out):
+    devices, width = out.shape[0], turn.shape[0]
+    chunks, _, part = g_bu.shape
+
+    def exact(a, b):
+        dims = (((1,), (1,)), ((), ()))
+        return lax.dot_general(
+            a, b, dims, precision=lax.Precision.HIGHEST, preferred_element_type=F32
+        )
+
+    plain = sums_one.shape[0] + sums_two.shape[0]
+    rows = jnp.concatenate([sums_one[...], sums_two[...]], axis=0)
+    rows = exact(rows, turn[...].astype(F32))
+    block, device = owners(devices, per, width)
+    tall = [jnp.where(block == device, rows[v : v + 1, :], 0.0) for v in range(plain)]
+    tall = exact(jnp.concatenate(tall, axis=0), repeats(per, width))
+    columns = [tall[v * devices : (v + 1) * devices, :] for v in range(plain)]
+
+    def by_chunk(row_of, size, length):
+        block, device = owners(devices, size, length)
+        tall = jnp.zeros((devices, length), F32)
+        for t in range(chunks):
+            tall = jnp.where(device == block * chunks + order[t], row_of(t), tall)
+        columns.append(exact(tall, repeats(size, length)))
+
+    cols = g_b.shape[2] // 3
+    by_chunk(lambda t: g_b[t][:, :cols], per, cols)
+    by_chunk(lambda t: g_b[t][:, 2 * cols :], per, cols)
+    by_chunk(lambda t: g_bu[t], out.shape[1] - (plain + 2) * per, part)
+    out[...] = jnp.concatenate(columns, axis=1)
 
 
 def attention_forward(
@@ -104,7 +185,7 @@
         hat, _ = norm_parts(x[...].astype(F32))
         normed[...] = (hat * vectors[0:1, :] + vectors[1:2, :]).astype(BF16)
 
-    bias = b_qv[order[t]]
+    bias = b_qv[t]
     both = mm(normed[...], nearer(t, qk_near, qk_far))
     query = (both[:, :cols] + bias[0:1, :]).astype(BF16)
     key = both[:, cols:].astype(BF16)
@@ -129,63 +210,54 @@
         out_c[0, mine, :] = jnp.concatenate(parts, axis=1).astype(BF16)
 
 
+def chunk_rows(order, c, cols):
+    return pl.ds(pl.multiple_of(order[c] * cols, cols), cols)
+
+
+def between(order, x, ctx, w_out, vectors, top, middle, hidden, hidden_t, top_t):
+    chunks, _, cols = ctx.shape
+    total = x[...].astype(F32) + vectors[2:3, :]
+    for c in range(chunks):
+        total += mm(ctx[c], w_out[chunk_rows(order, c, cols), :])
+    middle[...] = total
+    hat, _ = norm_parts(total)
+    low = hat * vectors[3:4, :] + vectors[4:5, :]
+    hidden[...] = low.astype(BF16)
+    hidden_t[...] = low.T.astype(BF16)
+    top_t[...] = top[...].astype(F32).T.astype(BF16)
+
+
 def feed_forward(
-    order,
-    x,
-    ctx,
-    w_out,
-    vectors,
-    top,
-    turn,
-    up_near,
-    up_far,
-    down_near,
-    down_far,
-    b_up,
-    out_y,
-    out_gm,
-    out_gc,
-    out_go,
-    gup_near,
-    gup_far,
-    gdown_near,
-    gdown_far,
-    out_bu,
-    out_sums,
-    middle,
-    hat,
-    root,
+    last,
     hidden,
     hidden_t,
+    top,
     top_t,
-    sum_y,
-    sum_h,
+    *rest,
 ):
+    ups, downs, b_up, rest = rest[:4], rest[4:8], rest[8], rest[9:]
+    if last:
+        in_y, in_h, order, middle, w_out, vectors = rest[:6]
+        rest = rest[6:]
+    gup_near, gup_far, gdown_near, gdown_far, out_bu = rest[:5]
+    if last:
+        out_y, out_gm, out_ga, out_gc, out_sums, sum_y, sum_h = rest[5:]
+    else:
+        sum_y, sum_h = rest[5:]
     t, n = pl.program_id(0), pl.program_id(1)
-    chunks, _, cols = ctx.shape
-    gain = vectors[3:4, :]
-
-    def span(c):
-        return pl.ds(pl.multiple_of(order[c] * cols, cols), cols)
 
     @pl.when((t == 0) & (n == 0))
     def _():
-        total = x[...].astype(F32) + vectors[2:3, :]
-        for c in range(chunks):
-            total += mm(ctx[c], w_out[span(c), :])
-        middle[...] = total
-        hat_two, root_two = norm_parts(total)
-        hat[...] = hat_two
-        root[...] = root_two
-        low = hat_two * gain + vectors[4:5, :]
-        hidden[...] = low.astype(BF16)
-        hidden_t[...] = low.T.astype(BF16)
-        top_t[...] = top[...].astype(F32).T.astype(BF16)
-        sum_y[...] = jnp.zeros_like(sum_y)
-        sum_h[...] = jnp.zeros_like(sum_h)
-
-    def work(up_ref, down_ref, gup, gdown):
-        w_up, w_down_t = up_ref[0], down_ref[0]
+        if last:
+            sum_y[...] = in_y[...]
+            sum_h[...] = in_h[...]
+        else:
+            sum_y[...] = jnp.zeros_like(sum_y)
+            sum_h[...] = jnp.zeros_like(sum_h)
+
+    def work(up_refs, down_refs, gup, gdown):
+        w_up = jnp.concatenate([ref[...] for ref in up_refs], axis=0)
+        w_down_t = jnp.concatenate([ref[...] for ref in down_refs], axis=0)
         up = mm(hidden[...], w_up) + b_up[0]
         phi = 0.5 * (1.0 + lax.erf(up * (0.5**0.5)))
         active = (up * phi).astype(BF16)
@@ -193,34 +265,46 @@
         grad_up = (mm(top[...], w_down_t) * slope).astype(BF16)
         sum_y[...] += mm_t(active, w_down_t)
         sum_h[...] += mm_t(grad_up, w_up)
-        gdown[0] = mm(top_t[...], active).astype(BF16)
-        gup[0] = mm(hidden_t[...], grad_up).astype(BF16)
+        gdown[...] = mm(top_t[...], active).astype(BF16)
+        gup[...] = mm(hidden_t[...], grad_up).astype(BF16)
         out_bu[0] = column_sum(grad_up)
 
-    @pl.when(t < pl.num_programs(0) // 2)
+    @pl.when(t == 0)
     def _():
-        work(up_near, down_near, gup_near, gdown_near)
-
-    @pl.when(t >= pl.num_programs(0) // 2)
+        work(ups[:2], downs[:2], gup_near, gdown_near)
+
+    @pl.when(t == 1)
     def _():
-        work(up_far, down_far, gup_far, gdown_far)
-
-    @pl.when((t == pl.num_programs(0) - 1) & (n == pl.num_programs(1) - 1))
+        work(ups[2:], downs[2:], gup_far, gdown_far)
+
+    if not last:
+        return
+
+    @pl.when((t == 1) & (n == pl.num_programs(1) - 1))
     def _():
+        chunks, _, cols = out_gc.shape
+        gain = vectors[3:4, :]
+        hat, root = norm_parts(middle[...])
         out_y[...] = (middle[...] + (sum_y[...] + vectors[5:6, :])).astype(BF16)
         grad_hidden = sum_h[...]
         grad_top = top[...].astype(F32)
-        grad_middle = grad_top + norm_back(grad_hidden, gain, hat[...], root[...])
+        grad_middle = grad_top + norm_back(grad_hidden, gain, hat, root)
         out_gm[...] = grad_middle
         grad_attn = grad_middle.astype(BF16)
+        out_ga[...] = grad_attn
         out_sums[0:1, :] = column_sum(grad_attn)
-        out_sums[1:2, :] = column_sum(grad_hidden * hat[...])
+        out_sums[1:2, :] = column_sum(grad_hidden * hat)
         out_sums[2:3, :] = column_sum(grad_hidden)
         out_sums[3:4, :] = column_sum(grad_top)
         for c in range(chunks):
-            out_gc[c] = mm_t(grad_attn, w_out[span(c), :]).astype(BF16)
-            grad_out = t_mm(ctx[c], grad_attn).astype(BF16)
-            out_go[span(c), :] = mm_t(grad_out, turn[...]).astype(BF16)
+            out_gc[c] = mm_t(grad_attn, w_out[chunk_rows(order, c, cols), :]).astype(BF16)
+
+
+def out_gradient(order, ctx, grad_attn, turn, out_go):
+    chunks, _, cols = ctx.shape
+    for c in range(chunks):
+        grad_out = t_mm(ctx[c], grad_attn[...]).astype(BF16)
+        out_go[chunk_rows(order, c, cols), :] = mm_t(grad_out, turn[...]).astype(BF16)
 
 
 def attention_backward(
@@ -231,7 +315,6 @@
     qk_far,
     vo_near,
     vo_far,
-    grad_out,
     query,
     key,
     value,
@@ -289,7 +372,7 @@
     grad_qk, grad_v = grad_all[:, : 2 * cols], grad_all[:, 2 * cols :]
     store(t, gqk_near, gqk_far, mm(normed_t[...], grad_qk).astype(BF16))
     grad_weight = mm(normed_t[...], grad_v).astype(BF16)
-    store(t, gvo_near, gvo_far, jnp.concatenate([grad_weight, grad_out[0]], axis=1))
+    store(t, gvo_near, gvo_far, grad_weight)
     sum_n[...] += mm_t(grad_qk, nearer(t, qk_near, qk_far))
     sum_n[...] += mm_t(grad_v, nearer(t, vo_near, vo_far)[:, :cols])
 
@@ -313,7 +396,7 @@
         compiler_params=pltpu.CompilerParams(
             dimension_semantics=("arbitrary",) * len(grid), vmem_limit_bytes=60 * 1024 * 1024
         ),
-        cost_estimate=pl.CostEstimate(flops=flops, bytes_accessed=moved, transcendentals=0),
+        cost_estimate=pl.CostEstimate(flops=flops // 8, bytes_accessed=moved // 8, transcendentals=0),
     )(*args)
 
 
@@ -367,15 +450,17 @@
         have.append(step)
         return piece
 
-    def add(terms, which, place):
-        terms = [lax.index_in_dim(term, which, place, False) for term in terms]
-        return (terms[0].astype(F32) + terms[1].astype(F32)).astype(BF16)
+    def side(terms, which, place):
+        return [lax.index_in_dim(term, which, place, False) for term in terms]
+
+    def total(terms):
+        return sum(term.astype(F32) for term in terms)
 
     def shrink(terms, step, have):
         place = have.index(step)
         have.remove(step)
-        near, far = add(terms, 0, place), add(terms, 1, place)
-        return near, far
+        away = total(side(terms, 1, place)).astype(BF16)
+        return side(terms, 0, place) + [flip(away, step)]
 
     def reverse_bits(value, count):
         return sum(
@@ -390,6 +475,7 @@
         return lax.all_to_all(blocks, ALL, 0, 0, tiled=True)
 
     per = first_gain.shape[0]
+    smem = pl.BlockSpec(memory_space=pltpu.SMEM)
     pieces = [first_gain, first_shift, out_bias, second_gain, second_shift, down_bias]
     pieces += [qkv_bias[0], qkv_bias[1], up_bias]
     small_size = sum(piece.shape[0] for piece in pieces)
@@ -440,23 +526,30 @@
     x, top = turned(pad(tokens)), turned(pad(output_grad))
     smalls = exchange(jnp.broadcast_to(smalls[None], (devices,) + smalls.shape))
 
-    smalls = smalls.reshape(n_dp, n_head, -1)
-    vectors = smalls[..., : 6 * per].reshape(n_dp, n_head, 6, per).transpose(2, 0, 1, 3)
-    vectors = vectors.reshape(6, width)
-    b_qv = smalls[..., 6 * per : 8 * per].reshape(n_dp, n_head, 2, per).transpose(1, 2, 0, 3)
-    b_qv = b_qv.reshape(n_head, 2, n_dp * per).astype(F32)
-    b_up = smalls[..., 8 * per :].transpose(1, 0, 2).reshape(n_head, 1, -1).astype(F32)
-
+    part_cols = width // n_head
+    vectors, b_qv, b_up = call(
+        functools.partial(spread_vectors, per),
+        (1,),
+        [smem, whole(smalls.shape), whole((width, width))],
+        [
+            (((6, width), F32), whole((6, width))),
+            (((n_head, 2, part_cols), F32), whole((n_head, 2, part_cols))),
+            (((n_head, 1, hidden // n_head), F32), whole((n_head, 1, hidden // n_head))),
+        ],
+        [],
+        0,
+        4 * width * width,
+        order_chunks,
+        smalls,
+        turn,
+    )
     first = grow(first, along_z[-1], have)
-    first, rest, x, top, vectors, b_qv, b_up = together(
-        first, rest, x, top, vectors, b_qv, b_up
-    )
-    vectors = turned(vectors).astype(F32)
+    first, rest, x, top = together(first, rest, x, top)
     w_qk, w_vo = first[..., : 2 * part_cols], first[..., 2 * part_cols :]
     have_qk, have_vo = list(have), list(have)
     w_qk, w_vo = grow(w_qk, along_x[0], have_qk), grow(w_vo, along_y[0], have_vo)
     rest = grow(rest, along_z[0], have_rest)
-    w_qk, w_vo, rest = together(w_qk, w_vo, rest)
+    w_qk, w_vo, rest, vectors, b_qv, b_up = together(w_qk, w_vo, rest, vectors, b_qv, b_up)
     for step in along_z[1:-1]:
         rest = grow(rest, step, have_rest)
     for step in along_y[:-1]:
@@ -471,9 +564,9 @@
         w_qk.reshape(pair_shape), w_vo.reshape(pair_shape), w_up, w_down
     )
     far_qk, far_vo = flip(near_qk, core), flip(near_vo, core)
-    have_up, have_down = list(have_rest), have_rest
-    w_up_sent = flip(w_up, along_x[0])
-    w_down_sent = flip(w_down, along_y[0])
+    step_x, step_y = along_x[0], along_y[0]
+    up_x, down_x = flip(w_up, step_x), flip(w_down, step_x)
+    up_y, down_y = flip(w_up, step_y), flip(w_down, step_y)
 
 
     lengths = lax.dynamic_slice_in_dim(caption_len, my_head * item_count, item_count)
@@ -483,7 +576,6 @@
     slab = (total_rows, part_cols)
     slab_out = (((n_head,) + slab, BF16), chunk(slab))
     probs_out = (((n_head, pairs, padded, padded), F32), chunk((pairs, padded, padded)))
-    smem = pl.BlockSpec(memory_space=pltpu.SMEM)
     weights = width * width
 
     half = n_head // 2
@@ -494,7 +586,7 @@
     def far(shape):
         return spec((1,) + shape, lambda t: (jnp.maximum(t - half, 0), 0, 0))
 
-    two_cols = (width, 2 * part_cols)
+    two_cols, one_col = (width, 2 * part_cols), (width, part_cols)
     first_specs = [near(two_cols), far(two_cols)] * 2
     query, key, value, probs, context = call(
         functools.partial(attention_forward, item_count, seq),
@@ -517,127 +609,137 @@
         b_qv,
     )
 
-    w_up, w_down, w_up_sent, w_down_sent, context = together(
-        w_up, w_down, w_up_sent, w_down_sent, context
-    )
-    w_up = jnp.stack([w_up, w_up_sent], axis=place_of(along_x[0], have_up))
-    w_down = jnp.stack([w_down, w_down_sent], axis=place_of(along_y[0], have_down))
-    have_up.append(along_x[0])
-    have_down.append(along_y[0])
-    for step in along_y[:-1]:
-        w_up = grow(w_up, step, have_up)
-    for step in along_y[1:]:
-        w_down = grow(w_down, step, have_down)
-    w_up, w_down = together(w_up, w_down)
-    w_up, w_down = grow(w_up, along_y[-1], have_up), grow(w_down, along_x[-1], have_down)
     w_out = jnp.concatenate([near_vo[..., part_cols:], far_vo[..., part_cols:]])
     w_out = w_out.reshape(devices, n_head, -1, part_cols).transpose(0, 2, 1, 3)
     w_out = w_out.reshape(devices, -1, width)
     w_out = turned(w_out[ranks_back].reshape(width, width))
-    near_up, near_down, w_out = together(
-        w_up.reshape(-1, width, part_hidden), w_down.reshape(-1, width, part_hidden), w_out
-    )
-    far_up, far_down = flip(near_up, core), flip(near_down, core)
-
-    block = 256 if part_hidden % 256 == 0 else part_hidden
-    steps = part_hidden // block
-
-    def strip(index):
-        return spec((1, width, block), index)
-
-    near_strip = strip(lambda t, n: (jnp.minimum(t, half - 1), 0, jnp.where(t < half, n, steps - 1)))
-    far_strip = strip(lambda t, n: (jnp.maximum(t - half, 0), 0, jnp.where(t < half, 0, n)))
-    bias_out = spec((1, 1, block), lambda t, n: (t, 0, n))
-    half_hidden = (half, width, part_hidden)
-    (
-        layer_out,
-        grad_middle,
-        grad_context,
-        g_out,
-        gup_near,
-        gup_far,
-        gdown_near,
-        gdown_far,
-        g_bu,
-        sums_two,
-    ) = call(
-        feed_forward,
-        (n_head, steps),
+    middle, low, low_t, top_t = call(
+        between,
+        (1,),
         [smem, whole(full), whole((n_head,) + slab), whole((width, width))]
-        + [whole(vectors.shape), whole(full), whole((width, width))]
-        + [near_strip, far_strip, near_strip, far_strip, bias_out],
+        + [whole(vectors.shape), whole(full)],
         [
+            ((full, F32), whole(full)),
             ((full, BF16), whole(full)),
-            ((full, F32), whole(full)),
-            (((n_head,) + slab, BF16), whole((n_head,) + slab)),
-            (((width, width), BF16), whole((width, width))),
-            ((half_hidden, BF16), near_strip),
-            ((half_hidden, BF16), far_strip),
-            ((half_hidden, BF16), near_strip),
-            ((half_hidden, BF16), far_strip),
-            (((n_head, 1, part_hidden), F32), bias_out),
-            (((4, width), F32), whole((4, width))),
+            ((full[::-1], BF16), whole(full[::-1])),
+            ((full[::-1], BF16), whole(full[::-1])),
         ],
-        [
-            pltpu.VMEM(full, F32),
-            pltpu.VMEM(full, F32),
-            pltpu.VMEM((total_rows, 1), F32),
-            pltpu.VMEM(full, BF16),
-            pltpu.VMEM(full[::-1], BF16),
-            pltpu.VMEM(full[::-1], BF16),
-            pltpu.VMEM(full, F32),
-            pltpu.VMEM(full, F32),
-        ],
-        12 * total_rows * width * hidden,
-        16 * weights,
+        [],
+        2 * total_rows * weights,
+        8 * weights,
         order_chunks,
         x,
         context,
         w_out,
         vectors,
         top,
-        turn,
-        near_up,
-        far_up,
-        near_down,
-        far_down,
-        b_up[order_chunks],
-    )
+    )
+
+    up_x, down_x, up_y, down_y, low = together(up_x, down_x, up_y, down_y, low)
+    up_d, down_d = flip(up_x, step_y), flip(down_y, step_x)
+    own = [w_up, up_x, w_down, down_x]
+    own_far = [flip(piece, core) for piece in own]
+    other = [up_y, up_d, down_y, down_d]
+    early_far = [flip(piece, core) for piece in other[::2]]
+    *own_far, late_0, late_1 = together(*own_far, *early_far)
+    early_far = [late_0, late_1]
+
+    def arranged(near, far):
+        pieces = near[:2] + far[:2] + near[2:] + far[2:]
+        return [piece.reshape(-1, part_hidden) for piece in pieces]
+
+    steps, block = 1, part_hidden
+    bias_strip = spec((1, 1, block), lambda t, n: (t, 0, n))
+    b_up = b_up.reshape(2, half, 1, part_hidden)
+    strips = [whole((width // 2, part_hidden))] * 8
+    strip_outs = [(((width, part_hidden), BF16), whole((width, part_hidden)))] * 4
+    strip_outs += [(((2, 1, part_hidden), F32), bias_strip)]
+    cost = 6 * total_rows * width * hidden, 10 * weights
+    *g_own, gb_own, sum_y, sum_h = call(
+        functools.partial(feed_forward, False),
+        (2, steps),
+        [whole(full), whole(full[::-1])] * 2 + strips + [bias_strip],
+        strip_outs + [((full, F32), whole(full))] * 2,
+        [],
+        *cost,
+        low,
+        low_t,
+        top,
+        top_t,
+        *arranged(own, own_far),
+        b_up[:, 0],
+    )
+    other[1], other[3], sum_y = together(other[1], other[3], sum_y)
+    late_far = [flip(piece, core) for piece in other[1::2]]
+    other_far = [early_far[0], late_far[0], early_far[1], late_far[1]]
+
     rest_bits = held[1:]
     shape = (2,) * len(rest_bits)
     tile = (part_rows, part_hidden)
+
     def pair(near, far, tile):
-        return near.reshape(shape + tile), flip(far.reshape(shape + tile), core)
-
-    down_terms = pair(gdown_near, gdown_far, tile)
-    up_terms = pair(gup_near, gup_far, tile)
-
-    have_down, have_up = list(rest_bits), list(rest_bits)
-    first_x, first_y = have_down.index(along_x[0]), have_up.index(along_y[0])
-    down_away = add(down_terms, 1, first_x)
-    up_away = add(up_terms, 1, first_y)
-    have_down.remove(along_x[0])
-    have_up.remove(along_y[0])
-    down_sent, up_sent = flip(down_away, along_x[0]), flip(up_away, along_y[0])
-    grad_context, down_away, up_away = together(grad_context, down_away, up_away)
-    g_out = g_out.reshape(devices, -1, width)[ranks]
-    g_out = g_out.reshape(devices, -1, n_head, part_cols).transpose(0, 2, 1, 3)
-    g_out = g_out.reshape(n_head, width, part_cols)
-
+        near = near.reshape(shape[1:] + tile)
+        return [near, flip(far.reshape(near.shape), core)]
+
+    gup_own, gdown_own = pair(*g_own[:2], tile), pair(*g_own[2:], tile)
+    *g_other, gb_other, layer_out, grad_middle, grad_attn, grad_context, sums_two = call(
+        functools.partial(feed_forward, True),
+        (2, steps),
+        [whole(full), whole(full[::-1])] * 2
+        + strips
+        + [bias_strip, whole(full), whole(full), smem, whole(full)]
+        + [whole((width, width)), whole(vectors.shape)],
+        strip_outs
+        + [
+            ((full, BF16), whole(full)),
+            ((full, F32), whole(full)),
+            ((full, BF16), whole(full)),
+            (((n_head,) + slab, BF16), whole((n_head,) + slab)),
+            (((4, width), F32), whole((4, width))),
+        ],
+        [pltpu.VMEM(full, F32), pltpu.VMEM(full, F32)],
+        *cost,
+        low,
+        low_t,
+        top,
+        top_t,
+        *arranged(other, other_far),
+        b_up[:, 1],
+        sum_y,
+        sum_h,
+        order_chunks,
+        middle,
+        w_out,
+        vectors,
+    )
+    g_bu = jnp.stack([gb_own, gb_other], axis=1).reshape(n_head, 1, part_hidden)
+    gup_other, gdown_other = pair(*g_other[:2], tile), pair(*g_other[2:], tile)
+
+    def low_total(terms):
+        return total(terms).astype(BF16)
+
+    away = [
+        low_total(side(gdown_own, 1, 0)),
+        low_total(side(gup_other, 1, 0)),
+        low_total(side(gdown_other, 1, 0)),
+        low_total(side(gup_other, 0, 0)),
+    ]
+    down_01, up_11 = flip(away[0], step_x), flip(away[1], step_y)
+    down_11, up_10 = flip(away[2], step_x), flip(away[3], step_y)
+    grad_context, *_ = together(grad_context, *away)
     tokens_grad, gqk_near, gqk_far, gvo_near, gvo_far, g_b, sums_one = call(
         functools.partial(attention_backward, item_count),
         (n_head,),
         [whole(full), whole(vectors.shape)]
         + first_specs
-        + [chunk((width, part_cols))]
         + [chunk(slab)] * 3
         + [chunk((pairs, padded, padded)), chunk(slab), whole(full)],
         [
             ((full, BF16), whole(full)),
             (((half,) + two_cols, BF16), near(two_cols)),
             (((half,) + two_cols, BF16), far(two_cols)),
-            (((half,) + two_cols, BF16), near(two_cols)),
-            (((half,) + two_cols, BF16), far(two_cols)),
+            (((half,) + one_col, BF16), near(one_col)),
+            (((half,) + one_col, BF16), far(one_col)),
             (((n_head, 1, 3 * part_cols), F32), chunk((1, 3 * part_cols))),
             (((2, width), F32), whole((2, width))),
         ],
@@ -655,7 +757,6 @@
         far_qk,
         near_vo,
         far_vo,
-        g_out,
         query,
         key,
         value,
@@ -664,74 +765,105 @@
         grad_middle,
     )
     two = (part_rows, 2 * part_cols)
-    down_sent, up_sent, gqk_near, gqk_far, gvo_near, gvo_far = together(
-        down_sent, up_sent, gqk_near, gqk_far, gvo_near, gvo_far
-    )
-    qk_terms, vo_terms = pair(gqk_near, gqk_far, two), pair(gvo_near, gvo_far, two)
+    down_01, up_11, down_11, up_10, gqk_near, gqk_far, gvo_near, gvo_far = together(
+        down_01, up_11, down_11, up_10, gqk_near, gqk_far, gvo_near, gvo_far
+    )
+
+    def pair_first(near, far):
+        return [near.reshape(shape + two), flip(far.reshape(shape + two), core)]
+
+    away_up = low_total(side(gup_own, 1, 0) + [up_11])
+    away_down = low_total(side(gdown_other, 0, 0) + [down_11])
+    up_01, down_10 = flip(away_up, step_x), flip(away_down, step_y)
+    qk_terms = pair_first(gqk_near, gqk_far)
+    grad_attn, *_ = together(grad_attn, away_up, away_down, gqk_far)
+    (g_out,) = call(
+        out_gradient,
+        (1,),
+        [smem, whole((n_head,) + slab), whole(full), whole((width, width))],
+        [(((width, width), BF16), whole((width, width)))],
+        [],
+        0,
+        0,
+        order_chunks,
+        context,
+        grad_attn,
+        turn,
+    )
+    g_out = g_out.reshape(devices, -1, width)[ranks]
+    g_out = g_out.reshape(devices, -1, n_head, part_cols).transpose(0, 2, 1, 3)
+    g_out = g_out.reshape(n_head, width, part_cols)
+    gvo_near = jnp.concatenate([gvo_near, g_out[:half]], axis=2)
+    gvo_far = jnp.concatenate([gvo_far, g_out[half:]], axis=2)
+    up_01, down_10, gvo_near, gvo_far, *qk_terms = together(
+        up_01, down_10, gvo_near, gvo_far, *qk_terms
+    )
+    vo_terms = pair_first(gvo_near, gvo_far)
     have_qk, have_vo = list(rest_bits), list(rest_bits)
-    down_terms = (add(down_terms, 0, first_x), down_sent)
-    up_terms = (add(up_terms, 0, first_y), up_sent)
+    up_terms = side(gup_own, 0, 0) + [up_10, up_01]
+    down_terms = side(gdown_own, 0, 0) + [down_01, down_10]
+    have_up = list(dp_bits[:-1][::-1])
 
     def descend(terms, steps, have):
         for step in steps:
-            near, away = shrink(terms, step, have)
-            terms = (near, flip(away, step))
+            terms = shrink(terms, step, have)
         return terms
 
-    def lockstep(*pairs):
-        flat = together(*(term for terms in pairs for term in terms))
-        return [tuple(flat[i : i + 2]) for i in range(0, len(flat), 2)]
+    def lockstep(*chains):
+        flat = together(*(chain[-1] for chain in chains))
+        return [chain[:-1] + [last] for chain, last in zip(chains, flat)]
 
     def descend_joined(one, other, axis, step, have):
         place = have.index(step)
         have.remove(step)
-        near, away = (
-            jnp.concatenate([add(one, which, place), add(other, which, place)], axis=axis)
-            for which in (0, 1)
-        )
-        return near, flip(away, step)
-
-    up_terms = descend(up_terms, along_y[1:] + along_x, have_up)
-    down_terms = descend(down_terms, along_x[1:] + along_y, have_down)
-    up_terms, down_terms, qk_terms, vo_terms = lockstep(up_terms, down_terms, qk_terms, vo_terms)
+        away = [total(side(terms, 1, place)).astype(BF16) for terms in (one, other)]
+        near = [total(side(terms, 0, place)) for terms in (one, other)]
+        away = flip(jnp.concatenate(away, axis=axis), step)
+        return [jnp.concatenate(near, axis=axis).astype(BF16), away]
+
     qk_terms = descend(qk_terms, along_y[:1], have_qk)
     vo_terms = descend(vo_terms, along_x, have_vo)
     back_z = along_z[::-1]
     rest_terms = descend_joined(up_terms, down_terms, -2, back_z[0], have_up)
-    rest_terms, qk_terms, vo_terms = lockstep(rest_terms, qk_terms, vo_terms)
+    sums_shape = (devices, small_size)
+    (sums,) = call(
+        functools.partial(collect_vectors, per),
+        (1,),
+        [smem, whole(sums_one.shape), whole(sums_two.shape), whole(g_b.shape), whole(g_bu.shape)]
+        + [whole((width, width))],
+        [((sums_shape, F32), whole(sums_shape))],
+        [],
+        0,
+        4 * width * width,
+        order_chunks,
+        sums_one,
+        sums_two,
+        g_b,
+        g_bu,
+        turn,
+    )
+    layer_out = turned_back(layer_out)
+    rest_terms, qk_terms, vo_terms, swapped, (layer_out,) = lockstep(
+        rest_terms, qk_terms, vo_terms, [sums], [layer_out]
+    )
     qk_terms = descend(qk_terms, along_y[1:] + along_x, have_qk)
     vo_terms = descend(vo_terms, along_y, have_vo)
     rest_terms = descend(rest_terms, back_z[1:], have_up)
-    rest_terms, qk_terms, vo_terms = lockstep(rest_terms, qk_terms, vo_terms)
+    layer_out = unpad(layer_out)
+    tokens_grad = unpad(turned_back(tokens_grad))
+
+    rest_terms, qk_terms, vo_terms, swapped = lockstep(
+        rest_terms, qk_terms, vo_terms, [exchange(swapped[0])]
+    )
     first_terms = descend_joined(qk_terms, vo_terms, -1, back_z[0], have_qk)
     first_terms = descend(first_terms, back_z[1:], have_qk)
-    rest = rest_terms[0].astype(F32) + rest_terms[1].astype(F32)
+    rest = total(rest_terms)
     g_up, g_down_t = rest[:part_rows], rest[part_rows:]
-    first = first_terms[0].astype(F32) + first_terms[1].astype(F32)
+    first = total(first_terms)
     g_qkv = first[:, : 3 * part_cols].reshape(part_rows, 3, part_cols)
     g_out = first[:, 3 * part_cols :].reshape(n_head, -1, part_cols).transpose(1, 0, 2)
     g_out = g_out.reshape(out_weight.shape)
-    layer_out = unpad(turned_back(layer_out))
-    tokens_grad = unpad(turned_back(tokens_grad))
-
-    sums = lax.dot_general(
-        jnp.concatenate([sums_one, sums_two]),
-        turn.astype(F32),
-        (((1,), (1,)), ((), ())),
-        precision=lax.Precision.HIGHEST,
-        preferred_element_type=F32,
-    )
-    g_b = g_b[chunk_of].reshape(n_head, 3, n_dp, per).transpose(2, 0, 1, 3)
-    g_bu = g_bu[chunk_of].reshape(n_head, n_dp, -1).transpose(1, 0, 2)
-    sums = jnp.concatenate(
-        [
-            sums.reshape(6, devices, per).transpose(1, 0, 2).reshape(devices, 6 * per),
-            g_b[:, :, ::2].reshape(devices, 2 * per),
-            g_bu.reshape(devices, -1),
-        ],
-        axis=1,
-    )
-    sums = jnp.sum(exchange(sums), axis=0)
+    sums = jnp.sum(swapped[0], axis=0)
 
     def part(index):
         return sums[index * per : (index + 1) * per]

time: 288 us -> 274 us (0.951); the launches traced: 287 us -> 270 us
  waiting for transfers between devices: 105 us -> 63.1 us
  Pallas kernels: 62.8 us -> 81 us
  starting transfers between devices: 35.5 us -> 49.3 us
  other arithmetic: 36.7 us -> 29.8 us
    ppermute x32 -> x44, waiting for transfers between devices: 93.3 us -> 52.8 us  [flip(): piece = lax.ppermute(piece, axis, [(i, i ^ bit) for i in range(count)])]
    pallas_call x3 -> x8, Pallas kernels: 62.8 us -> 81 us  [call(): pl.pallas_call(body, grid=grid, in_specs=in_specs, out_specs=[o[1] for o...]
    ppermute x32 -> x44, starting transfers between devices: 25.5 us -> 41.1 us  [flip(): piece = lax.ppermute(piece, axis, [(i, i ^ bit) for i in range(count)])]
    unnamed x78 -> x102, local copies, waits for them, and re-layouts: 4.09 us -> 11.7 us
    another operation x11 -> x9, other arithmetic: 7.71 us -> 1.73 us  [grow(): piece = jnp.stack([piece, other], axis=place_of(step, have))]
    convert_element_type x16 -> x11, other arithmetic: 20.2 us -> 14.7 us  [the longest x6 7.81 us: shrink(): away = total(side(terms, 1, place)).astype(BF16)]
    another operation x1 -> x5, other arithmetic: 3.3 us -> 6.24 us  [local(): w_up = jnp.stack([w_up, w_up_sent], axis=place_of(along_x[0], have_up))]
    dot_general x4 -> x3, matrix products: 6.61 us -> 6.27 us  [mm(): return jnp.dot(a, b, preferred_element_type=F32)]
  transfers between devices with their start and end apart: 34 -> 46, of which waited for: 20 -> 16; matrix products, arithmetic and copies ran while one was open for 22% -> 21% of each run, Pallas kernels for 12% -> 30%
where the time goes in v3:
time: 274 us; the launch traced here: 270 us
  Pallas kernels  81 us (30%)
  waiting for transfers between devices  63.1 us (23%)
  starting transfers between devices  49.3 us (18%)
  local copies, waits for them, and re-layouts  34.1 us (12%)
  other arithmetic  29.8 us (11%)
  matrix products  10.6 us (4%)
    pallas_call x8, Pallas kernels, call(): pl.pallas_call(body, grid=grid, in_specs=in_specs, out_specs=[o[1] for o...  81 us
    ppermute x44, waiting for transfers between devices, flip(): piece = lax.ppermute(piece, axis, [(i, i ^ bit) for i in range(count)])  52.8 us
    ppermute x44, starting transfers between devices, flip(): piece = lax.ppermute(piece, axis, [(i, i ^ bit) for i in range(count)])  41.1 us
    unnamed x102, local copies, waits for them, and re-layouts  11.7 us
    all_to_all x2, waiting for transfers between devices, exchange(): return lax.all_to_all(blocks, ALL, 0, 0, tiled=True)  10.4 us
    all_to_all x2, starting transfers between devices, exchange(): return lax.all_to_all(blocks, ALL, 0, 0, tiled=True)  8.26 us
    convert_element_type x6, other arithmetic, shrink(): away = total(side(terms, 1, place)).astype(BF16)  7.81 us
    convert_element_type x5, other arithmetic, low_total(): return total(terms).astype(BF16)  6.85 us
  transfers between devices with their start and end apart: 46, of which 16 were waited for; matrix products, arithmetic and copies ran while one was open for 21% of the time, Pallas kernels for 30%

profile of v3, /device:TPU:0, one launch (start us, length us, event | category | flops | bytes accessed | tf_op | source)
XLA Modules:
  0.0 269.6 jit_solution(10417203090496051414)
XLA Ops:
  0.6 1.1 copy.54
  3.0 4.1 %collective-permute-start = (bf16[96,768]{1,0:T(8,128)(2,1)S(1)}, bf16[96,768]{1,0:T(8,128)(2,1)S(1)}, u32[]{:S(2)}, u32[]{:S(2)}) collective-permute-start(bf16[96,768]{1,0:T(8,128)(2,1)S(1)} %pad_maximum_fusion.16), channel_id=1, source_target_pairs={{0,16},{4,20},{8,24},{12,28},{16,0},{20,4},{24,8},{28,12},{1,17},{... | collective-permute-start | bytes 442376 | tf_op jit(solution)/shard_map/ppermute | solution.py:438
  9.6 4.5 %collective-permute-done = bf16[96,768]{1,0:T(8,128)(2,1)S(1)} collective-permute-done((bf16[96,768]{1,0:T(8,128)(2,1)S(1)}, bf16[96,768]{1,0:T(8,128)(2,1)S(1)}, u32[]{:S(2)}, u32[]{:S(2)}) %collective-permute-start) | collective-permute-done | bytes 147488 | tf_op jit(solution)/shard_map/ppermute | solution.py:438
  15.0 1.5 convolution_convert_fusion.3.top
  16.4 1.4 convolution_convert_fusion.4.x
  17.9 4.5 %collective-permute-done.1 = bf16[2,96,768]{2,1,0:T(8,128)(2,1)S(1)} collective-permute-done((bf16[2,96,768]{2,1,0:T(8,128)(2,1)S(1)}, bf16[2,96,768]{2,1,0:T(8,128)(2,1)S(1)}, u32[]{:S(2)}, u32[]{:S(2)}) %collective-permute-start.1) | collective-permute-done | bytes 294944 | tf_op jit(solution)/shard_map/ppermute | solution.py:438
  22.6 1.4 collective-permute-start.3
  24.0 1.5 collective-permute-start.2
  27.5 5.0 %all-to-all-start = ((bf16[32,2,144]{2,1,0:T(2,128)(2,1)}), bf16[32,2,144]{2,1,0:T(2,128)(2,1)S(1)}, u32[]{:S(2)}, u32[]{:S(2)}) async-start(bf16[32,2,144]{2,1,0:T(2,128)(2,1)} %reshape.624), calls=%async_computation | async-start | bytes 65536 | tf_op jit(solution)/shard_map/all_to_all | solution.py:475
  32.6 2.9 %collective-permute-start.4 = (bf16[192,768]{1,0:T(8,128)(2,1)S(1)}, bf16[192,768]{1,0:T(8,128)(2,1)S(1)}, u32[]{:S(2)}, u32[]{:S(2)}) collective-permute-start(bf16[192,768]{1,0:T(8,128)(2,1)S(1)} %pad_maximum_fusion.13), channel_id=1, source_target_pairs={{0,16},{4,20},{8,24},{12,28},{16,0},{20,4},{24,8},{28,12},{1,17},{... | collective-permute-start | bytes 884744 | tf_op jit(solution)/shard_map/ppermute | solution.py:438
  35.9 4.0 %all-to-all-done = bf16[32,2,144]{2,1,0:T(2,128)(2,1)S(1)} async-done(((bf16[32,2,144]{2,1,0:T(2,128)(2,1)}), bf16[32,2,144]{2,1,0:T(2,128)(2,1)S(1)}, u32[]{:S(2)}, u32[]{:S(2)}) %all-to-all-start) | async-done | bytes 18464 | tf_op jit(solution)/shard_map/all_to_all | solution.py:475
  40.7 2.5 shard_map.254
  43.4 6.3 %collective-permute-done.4 = bf16[192,768]{1,0:T(8,128)(2,1)S(1)} collective-permute-done((bf16[192,768]{1,0:T(8,128)(2,1)S(1)}, bf16[192,768]{1,0:T(8,128)(2,1)S(1)}, u32[]{:S(2)}, u32[]{:S(2)}) %collective-permute-start.4) | collective-permute-done | bytes 294944 | tf_op jit(solution)/shard_map/ppermute | solution.py:438
  49.8 1.7 collective-permute-start.6
  51.4 1.5 collective-permute-start.5
  52.9 11.8 %collective-permute-done.6 = bf16[2,2,2,96,384]{4,3,2,1,0:T(8,128)(2,1)S(1)} collective-permute-done((bf16[2,2,2,96,384]{4,3,2,1,0:T(8,128)(2,1)S(1)}, bf16[2,2,2,96,384]{4,3,2,1,0:T(8,128)(2,1)S(1)}, u32[]{:S(2)}, u32[]{:S(2)}) %collective-permute-start.6) | collective-permute-done | bytes 589856 | tf_op jit(solution)/shard_map/ppermute | solution.py:438
  66.0 1.1 pad_maximum_fusion.5
  69.0 1.4 collective-permute-start.10
  71.7 1.4 collective-permute-start.9
  74.9 2.2 reshape.531
  77.1 3.1 %gather_fusion = bf16[32,24,768]{2,1,0:T(8,128)(2,1)} fusion(bf16[32,24,768]{2,1,0:T(8,128)(2,1)} %reshape.531, s32[1024]{0:T(1024)S(1)} %pad_clamp_fusion.1), kind=kCustom, calls=%fused_computation | custom fusion | bytes 2359424 | tf_op jit(solution)/shard_map/gather | solution.py:615
  80.2 3.4 %convolution_convert_fusion.w_out.rest_13_ = bf16[768,768]{1,0:T(8,128)(2,1)} fusion(bf16[768,768]{1,0:T(8,128)(2,1)} %bitcast.281, bf16[768,768]{1,0:T(8,128)(2,1)S(1)} %copy-done.1), kind=kOutput, calls=%fused_computation.7 | convolution fusion | flops 906559488 | bytes 3538944 | tf_op jit(solution)/shard_map/dot_general | solution.py:19
  83.6 11.6 %shard_map.255 = (bf16[4,384,192]{2,1,0:T(8,128)(2,1)}, bf16[4,384,192]{2,1,0:T(8,128)(2,1)}, bf16[4,384,192]{2,1,0:T(8,128)(2,1)}, f32[4,6,192,192]{3,2,1,0:T(8,128)}, bf16[4,384,192]{2,1,0:T(8,128)(2,1)}) custom-call(s32[2]{0:T(128)} %dynamic_slice.3.lengths, s32[4]{0:T(128)} %fusion.33.order.rest_11_, bf16[384,768]{1,0:T(8,128)(2,1)} %convolution_convert_fusion.4.x, ...), custom_call_target="tpu_custom_call" | custom-call | flops 226492416 | bytes 884736 | tf_op jit(solution)/shard_map/pallas_call | solution.py:389
  95.2 4.3 %shard_map.256 = (f32[384,768]{1,0:T(8,128)}, bf16[384,768]{1,0:T(8,128)(2,1)}, bf16[768,384]{1,0:T(8,128)(2,1)}, bf16[768,384]{1,0:T(8,128)(2,1)}) custom-call(s32[4]{0:T(128)} %fusion.33.order.rest_11_, bf16[384,768]{1,0:T(8,128)(2,1)} %convolution_convert_fusion.4.x, bf16[4,384,192]{2,1,0:T(8,128)(2,1)} %get-tuple-element.124.ctx, ...), custom_call_target="tpu_custom_call" | custom-call | flops 56623104 | bytes 589824 | tf_op jit(solution)/shard_map/pallas_call | solution.py:389
  101.7 1.4 collective-permute-start.23
  106.6 13.1 %shard_map.257 = (bf16[768,768]{1,0:T(8,128)(2,1)}, bf16[768,768]{1,0:T(8,128)(2,1)}, bf16[768,768]{1,0:T(8,128)(2,1)}, bf16[768,768]{1,0:T(8,128)(2,1)}, f32[2,...) custom-call(bf16[384,768]{1,0:T(8,128)(2,1)} %get-tuple-element.127.hidden, ...), custom_call_target="tpu_custom_call" | custom-call | flops 679477248 | bytes 737280 | tf_op jit(solution)/shard_map/pallas_call | solution.py:389
  120.4 1.4 collective-permute-done.25
  123.5 16.4 %shard_map.258 = (bf16[768,768]{1,0:T(8,128)(2,1)}, bf16[768,768]{1,0:T(8,128)(2,1)}, bf16[768,768]{1,0:T(8,128)(2,1)}, bf16[768,768]{1,0:T(8,128)(2,1)}, f32[2,...) custom-call(bf16[384,768]{1,0:T(8,128)(2,1)} %get-tuple-element.127., ...), custom_call_target="tpu_custom_call" | custom-call | flops 679477248 | bytes 737280 | tf_op jit(solution)/shard_map/pallas_call | solution.py:389
  141.3 1.2 copy-done.16
  142.7 1.4 collective-permute-start.22
  145.8 1.4 fusion.5
  148.0 1.2 collective-permute-start.31
  150.0 22.5 %shard_map.259 = (bf16[384,768]{1,0:T(8,128)(2,1)}, bf16[2,768,384]{2,1,0:T(8,128)(2,1)}, bf16[2,768,384]{2,1,0:T(8,128)(2,1)}, bf16[2,768,192]{2,1,0:T(8,128)(2...) custom-call(bf16[384,768]{1,0:T(8,128)(2,1)} %convolution_convert_fusion.4.x, ...), custom_call_target="tpu_custom_call" | custom-call | flops 452984832 | bytes 884736 | tf_op jit(solution)/shard_map/pallas_call | solution.py:389
  172.5 2.4 collective-permute-done.31
  174.9 2.1 fusion.2
  177.9 2.3 fusion.4
  180.1 1.3 collective-permute-start.32
  181.5 4.9 %shard_map.260 = bf16[768,768]{1,0:T(8,128)(2,1)} custom-call(s32[4]{0:T(128)} %fusion.33.order.rest_11_, bf16[4,384,192]{2,1,0:T(8,128)(2,1)} %get-tuple-element.124.ctx, bf16[384,768]{1,0:T(8,128)(2,1)} %get-tuple-element.172.grad_attn, bf16[768,768]{1,0:T(8,128)(2,1)} %copy-done), custom_call_target="tpu_custom_call" | custom-call | tf_op jit(solution)/shard_map/pallas_call | solution.py:389
  186.5 2.0 gather_fusion.1
  188.5 1.6 reshape.555
  193.1 2.8 %collective-permute-done.32 = bf16[2,2,96,768]{3,2,1,0:T(8,128)(2,1)} collective-permute-done((bf16[2,2,96,768]{3,2,1,0:T(8,128)(2,1)}, bf16[2,2,96,768]{3,2,1,0:T(8,128)(2,1)}, u32[]{:S(2)}, u32[]{:S(2)}) %collective-permute-start.32) | collective-permute-done | bytes 589856 | tf_op jit(solution)/shard_map/ppermute | solution.py:438
  196.0 2.0 fusion.9
  198.0 1.2 collective-permute-start.36
  199.2 1.8 fusion.15
  201.0 1.5 fusion.14
  205.2 1.5 collective-permute-start.38
  207.3 2.6 convolution_convert_fusion.2
  209.9 5.7 %shard_map.261 = f32[32,288]{1,0:T(8,128)} custom-call(s32[4]{0:T(128)} %fusion.33.order.rest_11_, f32[2,768]{1,0:T(2,128)} %get-tuple-element.182.sums_one, f32[4,768]{1,0:T(4,128)} %get-tuple-element.183.sums_two, f32[4,1,576]{2,1,0:T(1,128)} %get-tuple-element.184.g_b, f32[4,1,768]{2,1,0:T(1,128)} %reshape.560.g_bu, bf16[768,768]{1,0:T(8,128)(2,1)} %copy-done), custom_call_target="tpu_custom_call" | custom-call | bytes 294912 | tf_op jit(solution)/shard_map/pallas_call | solution.py:389
  215.6 3.6 %collective-permute-done.35 = bf16[2,192,768]{2,1,0:T(8,128)(2,1)} collective-permute-done((bf16[2,192,768]{2,1,0:T(8,128)(2,1)}, bf16[2,192,768]{2,1,0:T(8,128)(2,1)}, u32[]{:S(2)}, u32[]{:S(2)}) %collective-permute-start.35) | collective-permute-done | bytes 589856 | tf_op jit(solution)/shard_map/ppermute | solution.py:438
  219.2 1.3 collective-permute-done.38
  220.5 1.9 fusion.12
  223.2 2.0 fusion.13
  225.2 1.4 collective-permute-start.40
  226.6 1.7 fusion.18
  228.4 3.2 %collective-permute-start.39 = (bf16[192,768]{1,0:T(8,128)(2,1)}, bf16[192,768]{1,0:T(8,128)(2,1)}, u32[]{:S(2)}, u32[]{:S(2)}) collective-permute-start(bf16[192,768]{1,0:T(8,128)(2,1)} %fusion.18), channel_id=1, source_target_pairs={{0,16},{4,20},{8,24},{12,28},{16,0},{20,4},{24,8},{28,12},{1,17},{... | collective-permute-start | bytes 884744 | tf_op jit(solution)/shard_map/ppermute | solution.py:438
  232.2 3.2 %all-to-all-start.1 = ((f32[32,1,288]{2,1,0:T(1,128)}), f32[32,1,288]{2,1,0:T(1,128)}, u32[]{:S(2)}, u32[]{:S(2)}) async-start(f32[32,1,288]{2,1,0:T(1,128)} %copy.60), calls=%async_computation.1 | async-start | bytes 98304 | tf_op jit(solution)/shard_map/all_to_all | solution.py:475
  235.5 1.7 convolution_convert_fusion.1
  239.3 6.3 %all-to-all-done.1 = f32[32,1,288]{2,1,0:T(1,128)} async-done(((f32[32,1,288]{2,1,0:T(1,128)}), f32[32,1,288]{2,1,0:T(1,128)}, u32[]{:S(2)}, u32[]{:S(2)}) %all-to-all-start.1) | async-done | bytes 36896 | tf_op jit(solution)/shard_map/all_to_all | solution.py:475
  246.4 1.5 fusion.23
  247.9 1.4 fusion.22
  250.0 1.1 bitcast_add_fusion
  253.4 5.0 %collective-permute-done.42 = bf16[2,96,768]{2,1,0:T(8,128)(2,1)S(1)} collective-permute-done((bf16[2,96,768]{2,1,0:T(8,128)(2,1)S(1)}, bf16[2,96,768]{2,1,0:T(8,128)(2,1)S(1)}, u32[]{:S(2)}, u32[]{:S(2)}) %collective-permute-start.42) | collective-permute-done | bytes 294944 | tf_op jit(solution)/shard_map/ppermute | solution.py:438
  258.4 1.8 collective-permute-start.43
  260.8 6.6 %collective-permute-done.43 = bf16[96,768]{1,0:T(8,128)(2,1)S(1)} collective-permute-done((bf16[96,768]{1,0:T(8,128)(2,1)S(1)}, bf16[96,768]{1,0:T(8,128)(2,1)S(1)}, u32[]{:S(2)}, u32[]{:S(2)}) %collective-permute-start.43) | collective-permute-done | bytes 147488 | tf_op jit(solution)/shard_map/ppermute | solution.py:438
  (241 shorter events, 44.1 us)
Async XLA Ops:
  1.7 6.1 %copy-start.38 = (bf16[2,24]{1,0:T(2,128)(2,1)S(1)}, bf16[2,24]{1,0:T(2,128)(2,1)}, u32[]{:S(2)}) copy-start(bf16[2,24]{1,0:T(2,128)(2,1)} %param.20) | copy-start | bytes 292
  1.7 6.1 %copy-start.40 = (bf16[96]{0:T(256)(128)(2,1)S(1)}, bf16[96]{0:T(256)(128)(2,1)}, u32[]{:S(2)}) copy-start(bf16[96]{0:T(256)(128)(2,1)} %param.26) | copy-start | bytes 580
  1.7 6.1 %copy-start.41 = (bf16[24]{0:T(256)(128)(2,1)S(1)}, bf16[24]{0:T(256)(128)(2,1)}, u32[]{:S(2)}) copy-start(bf16[24]{0:T(256)(128)(2,1)} %param.28) | copy-start | bytes 148
  1.7 6.1 %copy-start.42 = (bf16[24]{0:T(256)(128)(2,1)S(1)}, bf16[24]{0:T(256)(128)(2,1)}, u32[]{:S(2)}) copy-start(bf16[24]{0:T(256)(128)(2,1)} %param.24) | copy-start | bytes 148
  1.8 6.1 %copy-start.43 = (bf16[24]{0:T(256)(128)(2,1)S(1)}, bf16[24]{0:T(256)(128)(2,1)}, u32[]{:S(2)}) copy-start(bf16[24]{0:T(256)(128)(2,1)} %param.23) | copy-start | bytes 148
  1.8 6.1 %copy-start.44 = (bf16[24]{0:T(256)(128)(2,1)S(1)}, bf16[24]{0:T(256)(128)(2,1)}, u32[]{:S(2)}) copy-start(bf16[24]{0:T(256)(128)(2,1)} %param.22) | copy-start | bytes 148
  1.8 6.1 %copy-start.45 = (bf16[24]{0:T(256)(128)(2,1)S(1)}, bf16[24]{0:T(256)(128)(2,1)}, u32[]{:S(2)}) copy-start(bf16[24]{0:T(256)(128)(2,1)} %param.18) | copy-start | bytes 148
  1.8 6.1 %copy-start.46 = (bf16[24]{0:T(256)(128)(2,1)S(1)}, bf16[24]{0:T(256)(128)(2,1)}, u32[]{:S(2)}) copy-start(bf16[24]{0:T(256)(128)(2,1)} %param.17) | copy-start | bytes 148
  1.8 6.2 %copy-start.29 = (bf16[370,768]{1,0:T(8,128)(2,1)S(1)}, bf16[370,768]{1,0:T(8,128)(2,1)}, u32[]{:S(2)}) copy-start(bf16[370,768]{1,0:T(8,128)(2,1)} %param.29) | copy-start | bytes 1704964
  3.0 11.1 %collective-permute-start = (bf16[96,768]{1,0:T(8,128)(2,1)S(1)}, bf16[96,768]{1,0:T(8,128)(2,1)S(1)}, u32[]{:S(2)}, u32[]{:S(2)}) collective-permute-start(bf16[96,768]{1,0:T(8,128)(2,1)S(1)} %pad_maximum_fusion.16), channel_id=1, source_target_pairs={{0,16},{4,20},{8,24},{12,28},{16,0},{20,4},{24,8},{28,12},{1,17},{... | collective-permute-start | bytes 442376 | tf_op jit(solution)/shard_map/ppermute | solution.py:438
  7.8 8.6 %copy-start = (bf16[768,768]{1,0:T(8,128)(2,1)}, bf16[768,768]{1,0:T(8,128)(2,1)S(1)}, u32[]{:S(2)}) copy-start(bf16[768,768]{1,0:T(8,128)(2,1)S(1)} %fusion.turn) | copy-start | bytes 3538948
  14.2 8.2 %collective-permute-start.1 = (bf16[2,96,768]{2,1,0:T(8,128)(2,1)S(1)}, bf16[2,96,768]{2,1,0:T(8,128)(2,1)S(1)}, u32[]{:S(2)}, u32[]{:S(2)}) collective-permute-start(bf16[2,96,768]{2,1,0:T(8,128)(2,1)S(1)} %pad_maximum_fusion.12), channel_id=1, source_target_pairs={{0,8},{4,12},{8,0},{12,4},{16,24},{20,28},{24,16},{28,20},{1,9},{5... | collective-permute-start | bytes 884744 | tf_op jit(solution)/shard_map/ppermute | solution.py:438
  22.6 20.6 %collective-permute-start.3 = (bf16[2,2,96,384]{3,2,1,0:T(8,128)(2,1)S(1)}, bf16[2,2,96,384]{3,2,1,0:T(8,128)(2,1)S(1)}, u32[]{:S(2)}, u32[]{:S(2)}) collective-permute-start(bf16[2,2,96,384]{3,2,1,0:T(8,128)(2,1)S(1)} %get-tuple-element.280), channel_id=1, source_target_pairs={{0,2},{1,3},{2,0},{3,1},{4,6},{5,7},{6,4},{7,5},{8,10},{9,11},{10,... | collective-permute-start | bytes 884744 | tf_op jit(solution)/shard_map/ppermute | solution.py:438
  24.0 19.3 %collective-permute-start.2 = (bf16[2,2,96,384]{3,2,1,0:T(8,128)(2,1)S(1)}, bf16[2,2,96,384]{3,2,1,0:T(8,128)(2,1)S(1)}, u32[]{:S(2)}, u32[]{:S(2)}) collective-permute-start(bf16[2,2,96,384]{3,2,1,0:T(8,128)(2,1)S(1)} %get-tuple-element.281), channel_id=1, source_target_pairs={{0,4},{4,0},{8,12},{12,8},{16,20},{20,16},{24,28},{28,24},{1,5},{5... | collective-permute-start | bytes 884744 | tf_op jit(solution)/shard_map/ppermute | solution.py:438
  27.5 12.4 %all-to-all-start = ((bf16[32,2,144]{2,1,0:T(2,128)(2,1)}), bf16[32,2,144]{2,1,0:T(2,128)(2,1)S(1)}, u32[]{:S(2)}, u32[]{:S(2)}) async-start(bf16[32,2,144]{2,1,0:T(2,128)(2,1)} %reshape.624), calls=%async_computation | async-start | bytes 65536 | tf_op jit(solution)/shard_map/all_to_all | solution.py:475
  32.6 17.1 %collective-permute-start.4 = (bf16[192,768]{1,0:T(8,128)(2,1)S(1)}, bf16[192,768]{1,0:T(8,128)(2,1)S(1)}, u32[]{:S(2)}, u32[]{:S(2)}) collective-permute-start(bf16[192,768]{1,0:T(8,128)(2,1)S(1)} %pad_maximum_fusion.13), channel_id=1, source_target_pairs={{0,16},{4,20},{8,24},{12,28},{16,0},{20,4},{24,8},{28,12},{1,17},{... | collective-permute-start | bytes 884744 | tf_op jit(solution)/shard_map/ppermute | solution.py:438
  49.8 14.9 %collective-permute-start.6 = (bf16[2,2,2,96,384]{4,3,2,1,0:T(8,128)(2,1)S(1)}, bf16[2,2,2,96,384]{4,3,2,1,0:T(8,128)(2,1)S(1)}, u32[]{:S(2)}, u32[]{:S(2)}) collective-permute-start(bf16[2,2,2,96,384]{4,3,2,1,0:T(8,128)(2,1)S(1)} %pad_maximum_fusion.8), channel_id=1, source_target_pairs={{0,4},{4,0},{8,12},{12,8},{16,20},{20,16},{24,28},{28,24},{1,5},{5... | collective-permute-start | bytes 1769480 | tf_op jit(solution)/shard_map/ppermute | solution.py:438
  51.4 14.5 %collective-permute-start.7 = (bf16[2,192,768]{2,1,0:T(8,128)(2,1)S(1)}, bf16[2,192,768]{2,1,0:T(8,128)(2,1)S(1)}, u32[]{:S(2)}, u32[]{:S(2)}) collective-permute-start(bf16[2,192,768]{2,1,0:T(8,128)(2,1)S(1)} %pad_maximum_fusion.9), channel_id=1, source_target_pairs={{0,8},{4,12},{8,0},{12,4},{16,24},{20,28},{24,16},{28,20},{1,9},{5... | collective-permute-start | bytes 1769480 | tf_op jit(solution)/shard_map/ppermute | solution.py:438
  51.4 15.6 %collective-permute-start.5 = (bf16[2,2,2,96,384]{4,3,2,1,0:T(8,128)(2,1)S(1)}, bf16[2,2,2,96,384]{4,3,2,1,0:T(8,128)(2,1)S(1)}, u32[]{:S(2)}, u32[]{:S(2)}) collective-permute-start(bf16[2,2,2,96,384]{4,3,2,1,0:T(8,128)(2,1)S(1)} %pad_maximum_fusion.7), channel_id=1, source_target_pairs={{0,2},{1,3},{2,0},{3,1},{4,6},{5,7},{6,4},{7,5},{8,10},{9,11},{10,... | collective-permute-start | bytes 1769480 | tf_op jit(solution)/shard_map/ppermute | solution.py:438
  64.9 8.2 %copy-start.4 = (bf16[2,2,2,2,96,384]{5,4,3,2,1,0:T(8,128)(2,1)}, bf16[2,2,2,2,96,384]{5,4,3,2,1,0:T(8,128)(2,1)S(1)}, u32[]{:S(2)}) copy-start(bf16[2,2,2,2,96,384]{5,4,3,2,1,0:T(8,128)(2,1)S(1)} %copy.57) | copy-start | bytes 3538948
  67.2 6.6 %copy-start.5 = (bf16[2,768,384]{2,1,0:T(8,128)(2,1)}, bf16[2,768,384]{2,1,0:T(8,128)(2,1)S(1)}, u32[]{:S(2)}) copy-start(bf16[2,768,384]{2,1,0:T(8,128)(2,1)S(1)} %pad_maximum_fusion.1.qk_near) | copy-start | bytes 3538948
  67.2 4.5 %collective-permute-start.13 = (bf16[2,768,384]{2,1,0:T(8,128)(2,1)S(1)}, bf16[2,768,384]{2,1,0:T(8,128)(2,1)S(1)}, u32[]{:S(2)}, u32[]{:S(2)}) collective-permute-start(bf16[2,768,384]{2,1,0:T(8,128)(2,1)S(1)} %bitcast.253), channel_id=1, source_target_pairs={{0,1},{1,0},{2,3},{3,2},{4,5},{5,4},{6,7},{7,6},{8,9},{9,8},{10,11... | collective-permute-start | bytes 3538952 | tf_op jit(solution)/shard_map/ppermute | solution.py:438
  67.3 12.9 %collective-permute-start.12 = (bf16[2,768,384]{2,1,0:T(8,128)(2,1)S(1)}, bf16[2,768,384]{2,1,0:T(8,128)(2,1)}, u32[]{:S(2)}, u32[]{:S(2)}) collective-permute-start(bf16[2,768,384]{2,1,0:T(8,128)(2,1)S(1)} %pad_maximum_fusion.1.qk_near), channel_id=1, source_target_pairs={{0,1},{1,0},{2,3},{3,2},{4,5},{5,4},{6,7},{7,6},{8,9},{9,8},{10,11... | collective-permute-start | bytes 3538952 | tf_op jit(solution)/shard_map/ppermute | solution.py:438
  69.0 30.4 %collective-permute-start.10 = (bf16[2,2,96,768]{3,2,1,0:T(8,128)(2,1)}, bf16[2,2,96,768]{3,2,1,0:T(8,128)(2,1)}, u32[]{:S(2)}, u32[]{:S(2)}) collective-permute-start(bf16[2,2,96,768]{3,2,1,0:T(8,128)(2,1)} %get-tuple-element.117), channel_id=1, source_target_pairs={{0,2},{1,3},{2,0},{3,1},{4,6},{5,7},{6,4},{7,5},{8,10},{9,11},{10,... | collective-permute-start | bytes 1769480 | tf_op jit(solution)/shard_map/ppermute | solution.py:438
  70.5 29.6 %collective-permute-start.8 = (bf16[2,2,96,768]{3,2,1,0:T(8,128)(2,1)}, bf16[2,2,96,768]{3,2,1,0:T(8,128)(2,1)}, u32[]{:S(2)}, u32[]{:S(2)}) collective-permute-start(bf16[2,2,96,768]{3,2,1,0:T(8,128)(2,1)} %get-tuple-element.117), channel_id=1, source_target_pairs={{0,4},{4,0},{8,12},{12,8},{16,20},{20,16},{24,28},{28,24},{1,5},{5... | collective-permute-start | bytes 1769480 | tf_op jit(solution)/shard_map/ppermute | solution.py:438
  71.2 28.9 %collective-permute-start.11 = (bf16[2,2,96,768]{3,2,1,0:T(8,128)(2,1)}, bf16[2,2,96,768]{3,2,1,0:T(8,128)(2,1)}, u32[]{:S(2)}, u32[]{:S(2)}) collective-permute-start(bf16[2,2,96,768]{3,2,1,0:T(8,128)(2,1)} %get-tuple-element.118), channel_id=1, source_target_pairs={{0,2},{1,3},{2,0},{3,1},{4,6},{5,7},{6,4},{7,5},{8,10},{9,11},{10,... | collective-permute-start | bytes 1769480 | tf_op jit(solution)/shard_map/ppermute | solution.py:438
  71.7 28.3 %collective-permute-start.9 = (bf16[2,2,96,768]{3,2,1,0:T(8,128)(2,1)}, bf16[2,2,96,768]{3,2,1,0:T(8,128)(2,1)}, u32[]{:S(2)}, u32[]{:S(2)}) collective-permute-start(bf16[2,2,96,768]{3,2,1,0:T(8,128)(2,1)} %get-tuple-element.118), channel_id=1, source_target_pairs={{0,4},{4,0},{8,12},{12,8},{16,20},{20,16},{24,28},{28,24},{1,5},{5... | collective-permute-start | bytes 1769480 | tf_op jit(solution)/shard_map/ppermute | solution.py:438
  80.2 20.5 %collective-permute-start.14 = (bf16[2,2,96,768]{3,2,1,0:T(8,128)(2,1)S(1)}, bf16[2,2,96,768]{3,2,1,0:T(8,128)(2,1)S(1)}, u32[]{:S(2)}, u32[]{:S(2)}) collective-permute-start(bf16[2,2,96,768]{3,2,1,0:T(8,128)(2,1)S(1)} %copy-done.8), channel_id=1, source_target_pairs={{0,1},{1,0},{2,3},{3,2},{4,5},{5,4},{6,7},{7,6},{8,9},{9,8},{10,11... | collective-permute-start | bytes 1769480 | tf_op jit(solution)/shard_map/ppermute | solution.py:438
  95.2 8.6 %copy-start.35 = (f32[4,1,768]{2,1,0:T(1,128)S(1)}, f32[4,1,768]{2,1,0:T(1,128)}, u32[]{:S(2)}) copy-start(f32[4,1,768]{2,1,0:T(1,128)} %get-tuple-element.138) | copy-start | bytes 36868
  99.5 2.2 collective-permute-start.16
  100.1 3.1 %collective-permute-start.15 = (bf16[2,2,96,768]{3,2,1,0:T(8,128)(2,1)}, bf16[2,2,96,768]{3,2,1,0:T(8,128)(2,1)S(1)}, u32[]{:S(2)}, u32[]{:S(2)}) collective-permute-start(bf16[2,2,96,768]{3,2,1,0:T(8,128)(2,1)} %collective-permute-done.8), channel_id=1, source_target_pairs={{0,1},{1,0},{2,3},{3,2},{4,5},{5,4},{6,7},{7,6},{8,9},{9,8},{10,11... | collective-permute-start | bytes 1769480 | tf_op jit(solution)/shard_map/ppermute | solution.py:438
  100.2 5.6 %collective-permute-start.17 = (bf16[2,2,96,768]{3,2,1,0:T(8,128)(2,1)}, bf16[2,2,96,768]{3,2,1,0:T(8,128)(2,1)S(1)}, u32[]{:S(2)}, u32[]{:S(2)}) collective-permute-start(bf16[2,2,96,768]{3,2,1,0:T(8,128)(2,1)} %collective-permute-done.9), channel_id=1, source_target_pairs={{0,1},{1,0},{2,3},{3,2},{4,5},{5,4},{6,7},{7,6},{8,9},{9,8},{10,11... | collective-permute-start | bytes 1769480 | tf_op jit(solution)/shard_map/ppermute | solution.py:438
  100.6 5.1 %collective-permute-start.18 = (bf16[2,2,96,768]{3,2,1,0:T(8,128)(2,1)}, bf16[2,2,96,768]{3,2,1,0:T(8,128)(2,1)}, u32[]{:S(2)}, u32[]{:S(2)}) collective-permute-start(bf16[2,2,96,768]{3,2,1,0:T(8,128)(2,1)} %collective-permute-done.10), channel_id=1, source_target_pairs={{0,1},{1,0},{2,3},{3,2},{4,5},{5,4},{6,7},{7,6},{8,9},{9,8},{10,11... | collective-permute-start | bytes 1769480 | tf_op jit(solution)/shard_map/ppermute | solution.py:438
  100.7 5.1 %copy-start.20 = (bf16[2,2,96,768]{3,2,1,0:T(8,128)(2,1)}, bf16[2,2,96,768]{3,2,1,0:T(8,128)(2,1)S(1)}, u32[]{:S(2)}) copy-start(bf16[2,2,96,768]{3,2,1,0:T(8,128)(2,1)S(1)} %collective-permute-done.14) | copy-start | bytes 1769476
  100.7 5.1 %collective-permute-start.19 = (bf16[2,2,96,768]{3,2,1,0:T(8,128)(2,1)}, bf16[2,2,96,768]{3,2,1,0:T(8,128)(2,1)S(1)}, u32[]{:S(2)}, u32[]{:S(2)}) collective-permute-start(bf16[2,2,96,768]{3,2,1,0:T(8,128)(2,1)} %collective-permute-done.11), channel_id=1, source_target_pairs={{0,1},{1,0},{2,3},{3,2},{4,5},{5,4},{6,7},{7,6},{8,9},{9,8},{10,11... | collective-permute-start | bytes 1769480 | tf_op jit(solution)/shard_map/ppermute | solution.py:438
  101.7 18.0 %collective-permute-start.23 = (bf16[2,2,96,768]{3,2,1,0:T(8,128)(2,1)}, bf16[2,2,96,768]{3,2,1,0:T(8,128)(2,1)S(1)}, u32[]{:S(2)}, u32[]{:S(2)}) collective-permute-start(bf16[2,2,96,768]{3,2,1,0:T(8,128)(2,1)} %collective-permute-done.8), channel_id=1, source_target_pairs={{0,2},{1,3},{2,0},{3,1},{4,6},{5,7},{6,4},{7,5},{8,10},{9,11},{10,... | collective-permute-start | bytes 1769480 | tf_op jit(solution)/shard_map/ppermute | solution.py:438
  103.1 16.6 %collective-permute-start.24 = (bf16[2,2,96,768]{3,2,1,0:T(8,128)(2,1)}, bf16[2,2,96,768]{3,2,1,0:T(8,128)(2,1)}, u32[]{:S(2)}, u32[]{:S(2)}) collective-permute-start(bf16[2,2,96,768]{3,2,1,0:T(8,128)(2,1)} %collective-permute-done.11), channel_id=1, source_target_pairs={{0,4},{4,0},{8,12},{12,8},{16,20},{20,16},{24,28},{28,24},{1,5},{5... | collective-permute-start | bytes 1769480 | tf_op jit(solution)/shard_map/ppermute | solution.py:438
  105.8 13.9 %copy-start.25 = (bf16[2,2,96,768]{3,2,1,0:T(8,128)(2,1)}, bf16[2,2,96,768]{3,2,1,0:T(8,128)(2,1)S(1)}, u32[]{:S(2)}) copy-start(bf16[2,2,96,768]{3,2,1,0:T(8,128)(2,1)S(1)} %collective-permute-done.19) | copy-start | bytes 1769476
  119.7 2.1 collective-permute-start.25
  119.8 2.8 %collective-permute-start.26 = (bf16[2,2,96,768]{3,2,1,0:T(8,128)(2,1)}, bf16[2,2,96,768]{3,2,1,0:T(8,128)(2,1)S(1)}, u32[]{:S(2)}, u32[]{:S(2)}) collective-permute-start(bf16[2,2,96,768]{3,2,1,0:T(8,128)(2,1)} %collective-permute-done.24), channel_id=1, source_target_pairs={{0,1},{1,0},{2,3},{3,2},{4,5},{5,4},{6,7},{7,6},{8,9},{9,8},{10,11... | collective-permute-start | bytes 1769480 | tf_op jit(solution)/shard_map/ppermute | solution.py:438
  120.3 22.2 %collective-permute-start.21 = (bf16[2,2,2,96,768]{4,3,2,1,0:T(8,128)(2,1)}, bf16[2,2,2,96,768]{4,3,2,1,0:T(8,128)(2,1)S(1)}, u32[]{:S(2)}, u32[]{:S(2)}) collective-permute-start(bf16[2,2,2,96,768]{4,3,2,1,0:T(8,128)(2,1)} %bitcast.321), channel_id=1, source_target_pairs={{0,1},{1,0},{2,3},{3,2},{4,5},{5,4},{6,7},{7,6},{8,9},{9,8},{10,11... | collective-permute-start | bytes 3538952 | tf_op jit(solution)/shard_map/ppermute | solution.py:438
  123.5 17.0 %copy-start.9 = (bf16[768,768]{1,0:T(8,128)(2,1)S(1)}, bf16[768,768]{1,0:T(8,128)(2,1)}, u32[]{:S(2)}) copy-start(bf16[768,768]{1,0:T(8,128)(2,1)} %get-tuple-element.141) | copy-start | bytes 3538948
  139.9 4.2 %collective-permute-start.29 = (bf16[2,2,2,96,768]{4,3,2,1,0:T(8,128)(2,1)}, bf16[2,2,2,96,768]{4,3,2,1,0:T(8,128)(2,1)S(1)}, u32[]{:S(2)}, u32[]{:S(2)}) collective-permute-start(bf16[2,2,2,96,768]{4,3,2,1,0:T(8,128)(2,1)} %bitcast.323), channel_id=1, source_target_pairs={{0,1},{1,0},{2,3},{3,2},{4,5},{5,4},{6,7},{7,6},{8,9},{9,8},{10,11... | collective-permute-start | bytes 3538952 | tf_op jit(solution)/shard_map/ppermute | solution.py:438
  140.1 5.6 %collective-permute-start.27 = (bf16[2,2,2,96,768]{4,3,2,1,0:T(8,128)(2,1)}, bf16[2,2,2,96,768]{4,3,2,1,0:T(8,128)(2,1)S(1)}, u32[]{:S(2)}, u32[]{:S(2)}) collective-permute-start(bf16[2,2,2,96,768]{4,3,2,1,0:T(8,128)(2,1)} %bitcast.322), channel_id=1, source_target_pairs={{0,1},{1,0},{2,3},{3,2},{4,5},{5,4},{6,7},{7,6},{8,9},{9,8},{10,11... | collective-permute-start | bytes 3538952 | tf_op jit(solution)/shard_map/ppermute | solution.py:438
  140.6 37.3 %collective-permute-start.20 = (bf16[2,2,2,96,768]{4,3,2,1,0:T(8,128)(2,1)}, bf16[2,2,2,96,768]{4,3,2,1,0:T(8,128)(2,1)}, u32[]{:S(2)}, u32[]{:S(2)}) collective-permute-start(bf16[2,2,2,96,768]{4,3,2,1,0:T(8,128)(2,1)} %bitcast.319), channel_id=1, source_target_pairs={{0,1},{1,0},{2,3},{3,2},{4,5},{5,4},{6,7},{7,6},{8,9},{9,8},{10,11... | collective-permute-start | bytes 3538952 | tf_op jit(solution)/shard_map/ppermute | solution.py:438
  142.7 29.8 %collective-permute-start.22 = (bf16[2,2,96,768]{3,2,1,0:T(8,128)(2,1)S(1)}, bf16[2,2,96,768]{3,2,1,0:T(8,128)(2,1)}, u32[]{:S(2)}, u32[]{:S(2)}) collective-permute-start(bf16[2,2,96,768]{3,2,1,0:T(8,128)(2,1)S(1)} %fusion.8), channel_id=1, source_target_pairs={{0,4},{4,0},{8,12},{12,8},{16,20},{20,16},{24,28},{28,24},{1,5},{5... | collective-permute-start | bytes 1769480 | tf_op jit(solution)/shard_map/ppermute | solution.py:438
  145.1 27.4 %collective-permute-start.30 = (bf16[2,2,96,768]{3,2,1,0:T(8,128)(2,1)}, bf16[2,2,96,768]{3,2,1,0:T(8,128)(2,1)}, u32[]{:S(2)}, u32[]{:S(2)}) collective-permute-start(bf16[2,2,96,768]{3,2,1,0:T(8,128)(2,1)} %fusion.6), channel_id=1, source_target_pairs={{0,4},{4,0},{8,12},{12,8},{16,20},{20,16},{24,28},{28,24},{1,5},{5... | collective-permute-start | bytes 1769480 | tf_op jit(solution)/shard_map/ppermute | solution.py:438
  147.2 25.4 %collective-permute-start.28 = (bf16[2,2,96,768]{3,2,1,0:T(8,128)(2,1)}, bf16[2,2,96,768]{3,2,1,0:T(8,128)(2,1)}, u32[]{:S(2)}, u32[]{:S(2)}) collective-permute-start(bf16[2,2,96,768]{3,2,1,0:T(8,128)(2,1)} %get-tuple-element.271), channel_id=1, source_target_pairs={{0,2},{1,3},{2,0},{3,1},{4,6},{5,7},{6,4},{7,5},{8,10},{9,11},{10,... | collective-permute-start | bytes 1769480 | tf_op jit(solution)/shard_map/ppermute | solution.py:438
  148.0 26.9 %collective-permute-start.31 = (bf16[2,2,96,768]{3,2,1,0:T(8,128)(2,1)}, bf16[2,2,96,768]{3,2,1,0:T(8,128)(2,1)}, u32[]{:S(2)}, u32[]{:S(2)}) collective-permute-start(bf16[2,2,96,768]{3,2,1,0:T(8,128)(2,1)} %get-tuple-element.270), channel_id=1, source_target_pairs={{0,2},{1,3},{2,0},{3,1},{4,6},{5,7},{6,4},{7,5},{8,10},{9,11},{10,... | collective-permute-start | bytes 1769480 | tf_op jit(solution)/shard_map/ppermute | solution.py:438
  174.9 21.0 %collective-permute-start.34 = (bf16[2,2,2,2,96,384]{5,4,3,2,1,0:T(8,128)(2,1)}, bf16[2,2,2,2,96,384]{5,4,3,2,1,0:T(8,128)(2,1)}, u32[]{:S(2)}, u32[]{:S(2)}) collective-permute-start(bf16[2,2,2,2,96,384]{5,4,3,2,1,0:T(8,128)(2,1)} %bitcast.320), channel_id=1, source_target_pairs={{0,1},{1,0},{2,3},{3,2},{4,5},{5,4},{6,7},{7,6},{8,9},{9,8},{10,11... | collective-permute-start | bytes 3538952 | tf_op jit(solution)/shard_map/ppermute | solution.py:438
  177.0 16.1 %collective-permute-start.33 = (bf16[2,2,96,768]{3,2,1,0:T(8,128)(2,1)}, bf16[2,2,96,768]{3,2,1,0:T(8,128)(2,1)}, u32[]{:S(2)}, u32[]{:S(2)}) collective-permute-start(bf16[2,2,96,768]{3,2,1,0:T(8,128)(2,1)} %fusion.2), channel_id=1, source_target_pairs={{0,2},{1,3},{2,0},{3,1},{4,6},{5,7},{6,4},{7,5},{8,10},{9,11},{10,... | collective-permute-start | bytes 1769480 | tf_op jit(solution)/shard_map/ppermute | solution.py:438
  180.1 15.8 %collective-permute-start.32 = (bf16[2,2,96,768]{3,2,1,0:T(8,128)(2,1)}, bf16[2,2,96,768]{3,2,1,0:T(8,128)(2,1)}, u32[]{:S(2)}, u32[]{:S(2)}) collective-permute-start(bf16[2,2,96,768]{3,2,1,0:T(8,128)(2,1)} %fusion.4), channel_id=1, source_target_pairs={{0,4},{4,0},{8,12},{12,8},{16,20},{20,16},{24,28},{28,24},{1,5},{5... | collective-permute-start | bytes 1769480 | tf_op jit(solution)/shard_map/ppermute | solution.py:438
  195.9 8.1 %collective-permute-start.37 = (bf16[2,2,2,2,96,384]{5,4,3,2,1,0:T(8,128)(2,1)S(1)}, bf16[2,2,2,2,96,384]{5,4,3,2,1,0:T(8,128)(2,1)S(1)}, u32[]{:S(2)}, u32[]{:S(2)}) collective-permute-start(bf16[2,2,2,2,96,384]{5,4,3,2,1,0:T(8,128)(2,1)S(1)} %bitcast.288), channel_id=1, source_target_pairs={{0,1},{1,0},{2,3},{3,2},{4,5},{5,4},{6,7},{7,6},{8,9},{9,8},{10,11... | collective-permute-start | bytes 3538952 | tf_op jit(solution)/shard_map/ppermute | solution.py:438
  198.0 17.6 %collective-permute-start.36 = (bf16[2,2,2,96,384]{4,3,2,1,0:T(8,128)(2,1)}, bf16[2,2,2,96,384]{4,3,2,1,0:T(8,128)(2,1)}, u32[]{:S(2)}, u32[]{:S(2)}) collective-permute-start(bf16[2,2,2,96,384]{4,3,2,1,0:T(8,128)(2,1)} %fusion.9), channel_id=1, source_target_pairs={{0,2},{1,3},{2,0},{3,1},{4,6},{5,7},{6,4},{7,5},{8,10},{9,11},{10,... | collective-permute-start | bytes 1769480 | tf_op jit(solution)/shard_map/ppermute | solution.py:438
  203.4 15.8 %collective-permute-start.35 = (bf16[2,192,768]{2,1,0:T(8,128)(2,1)}, bf16[2,192,768]{2,1,0:T(8,128)(2,1)}, u32[]{:S(2)}, u32[]{:S(2)}) collective-permute-start(bf16[2,192,768]{2,1,0:T(8,128)(2,1)} %pad_maximum_fusion.10), channel_id=1, source_target_pairs={{0,8},{4,12},{8,0},{12,4},{16,24},{20,28},{24,16},{28,20},{1,9},{5... | collective-permute-start | bytes 1769480 | tf_op jit(solution)/shard_map/ppermute | solution.py:438
  205.2 15.3 %collective-permute-start.38 = (bf16[2,2,2,96,384]{4,3,2,1,0:T(8,128)(2,1)S(1)}, bf16[2,2,2,96,384]{4,3,2,1,0:T(8,128)(2,1)}, u32[]{:S(2)}, u32[]{:S(2)}) collective-permute-start(bf16[2,2,2,96,384]{4,3,2,1,0:T(8,128)(2,1)S(1)} %fusion.10), channel_id=1, source_target_pairs={{0,4},{4,0},{8,12},{12,8},{16,20},{20,16},{24,28},{28,24},{1,5},{5... | collective-permute-start | bytes 1769480 | tf_op jit(solution)/shard_map/ppermute | solution.py:438
  222.4 9.2 %copy-start.31 = (f32[32,288]{1,0:T(8,128)S(1)}, f32[32,288]{1,0:T(8,128)}, u32[]{:S(2)}) copy-start(f32[32,288]{1,0:T(8,128)} %shard_map.261) | copy-start | bytes 110596
  222.4 13.1 %copy-start.3 = (bf16[768,768]{1,0:T(8,128)(2,1)S(1)}, bf16[768,768]{1,0:T(8,128)(2,1)}, u32[]{:S(2)}) copy-start(bf16[768,768]{1,0:T(8,128)(2,1)} %copy-done) | copy-start | bytes 3538948
  222.4 24.0 %collective-permute-start.41 = (bf16[2,2,96,384]{3,2,1,0:T(8,128)(2,1)}, bf16[2,2,96,384]{3,2,1,0:T(8,128)(2,1)}, u32[]{:S(2)}, u32[]{:S(2)}) collective-permute-start(bf16[2,2,96,384]{3,2,1,0:T(8,128)(2,1)} %fusion.12), channel_id=1, source_target_pairs={{0,2},{1,3},{2,0},{3,1},{4,6},{5,7},{6,4},{7,5},{8,10},{9,11},{10,... | collective-permute-start | bytes 884744 | tf_op jit(solution)/shard_map/ppermute | solution.py:438
  225.2 21.2 %collective-permute-start.40 = (bf16[2,2,96,384]{3,2,1,0:T(8,128)(2,1)}, bf16[2,2,96,384]{3,2,1,0:T(8,128)(2,1)}, u32[]{:S(2)}, u32[]{:S(2)}) collective-permute-start(bf16[2,2,96,384]{3,2,1,0:T(8,128)(2,1)} %fusion.13), channel_id=1, source_target_pairs={{0,4},{4,0},{8,12},{12,8},{16,20},{20,16},{24,28},{28,24},{1,5},{5... | collective-permute-start | bytes 884744 | tf_op jit(solution)/shard_map/ppermute | solution.py:438
  228.4 18.1 %collective-permute-start.39 = (bf16[192,768]{1,0:T(8,128)(2,1)}, bf16[192,768]{1,0:T(8,128)(2,1)}, u32[]{:S(2)}, u32[]{:S(2)}) collective-permute-start(bf16[192,768]{1,0:T(8,128)(2,1)} %fusion.18), channel_id=1, source_target_pairs={{0,16},{4,20},{8,24},{12,28},{16,0},{20,4},{24,8},{28,12},{1,17},{... | collective-permute-start | bytes 884744 | tf_op jit(solution)/shard_map/ppermute | solution.py:438
  232.2 13.4 %all-to-all-start.1 = ((f32[32,1,288]{2,1,0:T(1,128)}), f32[32,1,288]{2,1,0:T(1,128)}, u32[]{:S(2)}, u32[]{:S(2)}) async-start(f32[32,1,288]{2,1,0:T(1,128)} %copy.60), calls=%async_computation.1 | async-start | bytes 98304 | tf_op jit(solution)/shard_map/all_to_all | solution.py:475
  249.4 9.0 %collective-permute-start.42 = (bf16[2,96,768]{2,1,0:T(8,128)(2,1)S(1)}, bf16[2,96,768]{2,1,0:T(8,128)(2,1)S(1)}, u32[]{:S(2)}, u32[]{:S(2)}) collective-permute-start(bf16[2,96,768]{2,1,0:T(8,128)(2,1)S(1)} %pad_maximum_fusion.14), channel_id=1, source_target_pairs={{0,8},{4,12},{8,0},{12,4},{16,24},{20,28},{24,16},{28,20},{1,9},{5... | collective-permute-start | bytes 884744 | tf_op jit(solution)/shard_map/ppermute | solution.py:438
  258.4 9.0 %collective-permute-start.43 = (bf16[96,768]{1,0:T(8,128)(2,1)S(1)}, bf16[96,768]{1,0:T(8,128)(2,1)S(1)}, u32[]{:S(2)}, u32[]{:S(2)}) collective-permute-start(bf16[96,768]{1,0:T(8,128)(2,1)S(1)} %fusion.24), channel_id=1, source_target_pairs={{0,16},{4,20},{8,24},{12,28},{16,0},{20,4},{24,8},{28,12},{1,17},{... | collective-permute-start | bytes 442376 | tf_op jit(solution)/shard_map/ppermute | solution.py:438
  (30 other events, 68.2 us)
